TPU v7x, 256 devices: a whole 4x4x8 slice. The times are simulated.
256 devices in a mesh: grp: 8 (over z), shard: 32 (over y, x, core).
Axes of the slice: x: 4, y: 4, z: 8, core: 2. Of those that a mesh axis runs over, the one named last changes fastest.
Arguments:
- table: float32 [4096, 8, 128], P('shard')
- table_first: float32 [4096, 8, 128], P('shard'), may hold values from -3 to 3
- table_second: float32 [4096, 8, 128], P('shard')
- slot_table: int32 [4096], P('shard'), may hold values from 0 to 25
- touched: int32 [8, 4096], P('grp', 'shard'), may hold values from 0 to 4095, as said below
- emb_grads: bfloat16 [8, 4096, 8, 128], P('grp', 'shard'), may hold values from -6 to 6
- block_slot: int32 [4096], replicated, may hold values from 0 to 4095, as said below
- dense_x: bfloat16 [13, 1048576], P(None, ('grp', 'shard')), may hold values from -6 to 6
- dense_cot: bfloat16 [1048576, 128], P(('grp', 'shard')), may hold values from -0.0625 to 0.0625
- w_one: float32 [13, 512], replicated, may hold values from -1.75 to 1.75
- w_two: float32 [512, 256], replicated, may hold values from -0.25 to 0.25
- w_three: float32 [256, 128], replicated, may hold values from -0.375 to 0.375
- first_one: float32 [13, 512], replicated, may hold values from -3 to 3
- first_two: float32 [512, 256], replicated, may hold values from -3 to 3
- first_three: float32 [256, 128], replicated, may hold values from -3 to 3
- second_one: float32 [13, 512], replicated, may hold values from 0.001 to 0.3
- second_two: float32 [512, 256], replicated, may hold values from 0.001 to 0.3
- second_three: float32 [256, 128], replicated, may hold values from 0.001 to 0.3
Outputs:
- new_table: float32 [4096, 8, 128], P('shard')
- new_table_first: float32 [4096, 8, 128], P('shard')
- new_table_second: float32 [4096, 8, 128], P('shard')
- new_w_one: float32 [13, 512], replicated
- new_w_two: float32 [512, 256], replicated
- new_w_three: float32 [256, 128], replicated
- new_first_one: float32 [13, 512], replicated
- new_first_two: float32 [512, 256], replicated
- new_first_three: float32 [256, 128], replicated
- new_second_one: float32 [13, 512], replicated
- new_second_two: float32 [512, 256], replicated
- new_second_three: float32 [256, 128], replicated
Inputs may be any that keep to these rules, and one draw needn't show every extreme that they name: `touched`: each device's 128 ids are distinct; at most 8 of them have block_slot // 128 equal to any one shard, and in every draw some shard gets exactly 8 from every device. `block_slot`: A permutation of the 4096 slots.
All inputs are finite; a program needn't handle non-finite values.
Results may differ from a plain program's by a relative error of at most 0.0037.
Values may be sent and summed in bfloat16 or wider, within the bound.
No kernel may reach another device: no remote copies, remote signals or barrier semaphores. Data moves between devices by JAX's collectives and lax.ppermute only.
A program may use at most 128 MiB of HBM per device.

v0:
```python
import jax
import jax.numpy as jnp
from jax import lax
from jax.sharding import Mesh
from jax.sharding import PartitionSpec as P

TABLES = 26
CAP = 8
SHARD = ("shard_0", "shard_1", "shard_2")
GRP_SHARD = ("grp", "shard_0", "shard_1", "shard_2")


beta_one = 0.9
beta_two = 0.999
corr_first = 1.0 - 0.9**10
corr_second = 1.0 - 0.999**10
adam_eps = 1e-06
decay_rate = 0.01
learn_rate = 0.1
ratio_eps = 1e-06


def rows_for(lines, count):
    spare = -lines.shape[0] % count
    if not spare:
        return lines
    return jnp.concatenate([lines, jnp.zeros((spare, *lines.shape[1:]), lines.dtype)])


def from_everyone(value, axis):
    copies = jnp.broadcast_to(value, (lax.axis_size(axis), *value.shape))
    return lax.all_to_all(copies, axis, split_axis=0, concat_axis=0, tiled=True)


def in_order(pieces, dim):
    pieces = jnp.moveaxis(pieces, 0, dim)
    shape = pieces.shape
    return pieces.reshape(*shape[:dim], shape[dim] * shape[dim + 1], *shape[dim + 2 :])


def gathered_by_axis(value, axes, dim):
    far, near = axes
    pieces = from_everyone(from_everyone(value, far), near)
    return in_order(pieces.swapaxes(0, 1).reshape(-1, *value.shape), dim)


def cut_along(value, dim, count):
    before, after = (value.shape[:dim], value.shape[dim + 1 :])
    return jnp.moveaxis(value.reshape(*before, count, -1, *after), dim, 0)


def summed_on_arrival(value, axis, dim):
    count = lax.axis_size(axis)
    pieces = lax.all_to_all(cut_along(value, dim, count), axis, 0, 0, tiled=True)
    return jnp.sum(pieces, axis=0)


def summed_rows(value, axes, dim):
    far, near = axes
    pieces = cut_along(value, dim, lax.axis_size(far))
    nearer = summed_on_arrival(pieces, near, dim + 1)
    arrived = lax.all_to_all(nearer, far, split_axis=0, concat_axis=0, tiled=True)
    return arrived.sum(axis=0)


def total_of(value, axes):
    padded = rows_for(value, lax.axis_size(axes[0]) * lax.axis_size(axes[1]))
    whole = gathered_by_axis(summed_rows(padded, axes, 0), axes, 0)
    return lax.slice_in_dim(whole, 0, len(value)).reshape(value.shape)


def packed_total(arrays, axis):
    line, at, finished = (jnp.concatenate([a.reshape(-1) for a in arrays]), 0, [])
    running = total_of(line, axis)
    for a in arrays:
        finished.append(running[at : at + a.size].reshape(a.shape))
        at += a.size
    return tuple(finished)


def silu_slope(pre_value):
    logistic = jax.nn.sigmoid(pre_value)
    return logistic * (1.0 + pre_value * (1.0 - logistic))


def tower_grads(dense_x, dense_cot, w_one, w_two, w_three):
    w_one_bf = w_one.astype(jnp.bfloat16)
    w_two_bf = w_two.astype(jnp.bfloat16)
    w_three_bf = w_three.astype(jnp.bfloat16)
    pre_one = lax.dot_general(
        dense_x, w_one_bf, (((0,), (0,)), ((), ())), preferred_element_type=jnp.float32
    )
    hidden_one = jax.nn.silu(pre_one).astype(jnp.bfloat16)
    pre_two = jnp.dot(hidden_one, w_two_bf, preferred_element_type=jnp.float32)
    hidden_two = jax.nn.silu(pre_two).astype(jnp.bfloat16)
    grad_three = lax.dot_general(
        hidden_two, dense_cot, (((0,), (0,)), ((), ())), preferred_element_type=jnp.float32
    )
    back_two = (
        lax.dot_general(
            dense_cot, w_three_bf, (((1,), (1,)), ((), ())), preferred_element_type=jnp.float32
        )
        * silu_slope(pre_two)
    ).astype(jnp.bfloat16)
    grad_two = lax.dot_general(
        hidden_one, back_two, (((0,), (0,)), ((), ())), preferred_element_type=jnp.float32
    )
    back_one = (
        lax.dot_general(
            back_two, w_two_bf, (((1,), (1,)), ((), ())), preferred_element_type=jnp.float32
        )
        * silu_slope(pre_one)
    ).astype(jnp.bfloat16)
    grad_one = jnp.dot(dense_x, back_one, preferred_element_type=jnp.float32)
    return (grad_one, grad_two, grad_three)


def lamb_dense(weight, first_in, second_in, gradient):
    first_out = beta_one * first_in + (1.0 - beta_one) * gradient
    second_out = beta_two * second_in + (1.0 - beta_two) * gradient * gradient
    update = (
        first_out / corr_first / (jnp.sqrt(second_out / corr_second) + adam_eps)
        + decay_rate * weight
    )
    trust_ratio = jnp.sqrt(jnp.sum(weight * weight)) / (
        jnp.sqrt(jnp.sum(update * update)) + ratio_eps
    )
    return (weight - learn_rate * trust_ratio * update, first_out, second_out)


def body(
    table,
    table_first,
    table_second,
    slot_table,
    touched,
    emb_grads,
    block_slot,
    dense_x,
    dense_cot,
    w_one,
    w_two,
    w_three,
    first_one,
    first_two,
    first_three,
    second_one,
    second_two,
    second_three,
):
    shards = lax.axis_size(SHARD)
    local_blocks = table.shape[0]
    block_rows = table.shape[1]
    emb_width = table.shape[2]
    row_width = block_rows * emb_width
    capacity = CAP
    dense_terms = tower_grads(dense_x, dense_cot, w_one, w_two, w_three)
    table_hot = (slot_table[:, None] == jnp.arange(TABLES, dtype=jnp.int32)[None, :]).astype(
        jnp.float32
    )
    row_weight = jnp.sum(table * table, axis=(1, 2))
    part_weight = jnp.dot(row_weight, table_hot)
    block_ids = touched[0]
    count_touched = block_ids.shape[0]
    grad_rows = emb_grads[0].reshape(count_touched, row_width)
    slot_index = jnp.take(block_slot, block_ids)
    owner_shard = slot_index // local_blocks
    local_row = slot_index % local_blocks
    owner_hot = (owner_shard[:, None] == jnp.arange(shards, dtype=jnp.int32)[None, :]).astype(
        jnp.int32
    )
    bucket_rank = jnp.cumsum(owner_hot, axis=0) - 1
    bucket_place = jnp.sum(owner_hot * bucket_rank, axis=1)
    send_index = owner_shard * capacity + bucket_place
    picker = jnp.arange(shards * capacity, dtype=jnp.int32)[:, None] == send_index[None, :]
    send_rows = jnp.dot(
        picker.astype(jnp.bfloat16), grad_rows, preferred_element_type=jnp.float32
    ).astype(jnp.bfloat16)
    send_local = jnp.where(
        jnp.any(picker, axis=1), jnp.sum(jnp.where(picker, local_row[None, :], 0), axis=1), -1
    )
    send_rows = send_rows.reshape(shards, capacity, row_width)
    send_local = send_local.reshape(shards, capacity)
    recv_rows, recv_local = (
        lax.all_to_all(send_rows, SHARD, split_axis=0, concat_axis=0, tiled=True),
        lax.all_to_all(send_local, SHARD, split_axis=0, concat_axis=0, tiled=True),
    )
    piece_rows = lax.all_gather(recv_rows, "grp", axis=0, tiled=True).reshape(-1, row_width)
    piece_locals = lax.all_gather(recv_local, "grp", axis=0, tiled=True).reshape(-1)
    matches = piece_locals[:, None] == jnp.arange(local_blocks, dtype=jnp.int32)[None, :]
    summed = lax.dot_general(
        matches.astype(jnp.bfloat16),
        piece_rows,
        (((0,), (0,)), ((), ())),
        preferred_element_type=jnp.float32,
    )
    counted = jnp.sum(matches.astype(jnp.float32), axis=0)
    emb_grad = summed.reshape(local_blocks, block_rows, emb_width)
    touched_mask = (counted > 0.5)[:, None, None]
    new_first = jnp.where(
        touched_mask, beta_one * table_first + (1.0 - beta_one) * emb_grad, table_first
    )
    new_second = jnp.where(
        touched_mask, beta_two * table_second + (1.0 - beta_two) * emb_grad * emb_grad, table_second
    )
    update = jnp.where(
        touched_mask,
        new_first / corr_first / (jnp.sqrt(new_second / corr_second) + adam_eps)
        + decay_rate * table,
        0.0,
    )
    row_update = jnp.sum(update * update, axis=(1, 2))
    part_update = jnp.dot(row_update, table_hot)
    merged = packed_total(
        (dense_terms[0], dense_terms[1], dense_terms[2], part_weight, part_update),
        (("grp", "shard_0"), ("shard_1", "shard_2")),
    )
    dense_grads = (merged[0], merged[1], merged[2])
    weight_total = merged[3] / lax.axis_size("grp")
    update_total = merged[4] / lax.axis_size("grp")
    table_ratio = jnp.sqrt(weight_total) / (jnp.sqrt(update_total) + ratio_eps)
    ratio_rows = jnp.dot(table_hot, table_ratio)
    new_table = table - learn_rate * ratio_rows[:, None, None] * update
    layer_one = lamb_dense(w_one, first_one, second_one, dense_grads[0])
    layer_two = lamb_dense(w_two, first_two, second_two, dense_grads[1])
    layer_three = lamb_dense(w_three, first_three, second_three, dense_grads[2])
    return (
        new_table,
        new_first,
        new_second,
        layer_one[0],
        layer_two[0],
        layer_three[0],
        layer_one[1],
        layer_two[1],
        layer_three[1],
        layer_one[2],
        layer_two[2],
        layer_three[2],
    )


def solution(mesh):
    finer = Mesh(
        mesh.devices.reshape(mesh.shape["grp"], 4, 4, 2), ("grp", "shard_0", "shard_1", "shard_2")
    )
    placed = (
        P(SHARD, None, None),
        P(SHARD, None, None),
        P(SHARD, None, None),
        P(SHARD),
        P("grp", SHARD),
        P("grp", SHARD, None, None),
        P(),
        P(None, GRP_SHARD),
        P(GRP_SHARD, None),
        P(),
        P(),
        P(),
        P(),
        P(),
        P(),
        P(),
        P(),
        P(),
    )
    return jax.shard_map(
        body,
        mesh=finer,
        in_specs=placed,
        out_specs=(
            P(SHARD, None, None),
            P(SHARD, None, None),
            P(SHARD, None, None),
            P(),
            P(),
            P(),
            P(),
            P(),
            P(),
            P(),
            P(),
            P(),
        ),
        check_vma=False,
    )
```

profile of v0, /device:TPU:1, one launch (start us, length us, event | category | flops | bytes accessed | tf_op | source)
XLA Modules:
  0.0 203.5 jit_solution(15515118279379365087)
XLA Ops:
  7.2 0.0 all-gather.3.cloned.1.call-start
  7.2 0.7 fusion.30
  8.0 1.6 gather_fusion
  9.6 0.7 and_select_fusion.1
  10.3 0.7 fusion.29
  11.0 0.1 fusion.21
  11.1 0.2 reduce_window_sum.11
  11.2 0.2 select_reduce_fusion.1
  11.4 1.2 fusion.2
  12.7 19.9 %all_to_all.42 = bf16[32,8,1024]{2,1,0:T(8,128)(2,1)} all-to-all(bf16[32,8,1024]{2,1,0:T(8,128)(2,1)S(1)} %fusion.2), channel_id=1, replica_groups=mesh['grp'=8,'shard_0'=4,'shard_1'=4,'shard_2'=2] {'shard_0','shard_1','..., dimensions={0} | all-to-all | bytes 1048576 | tf_op jit(solution)/shard_map/all_to_all | solution.py:185
  32.6 0.0 all-gather.3.cloned.1.call-update
  32.6 0.1 fusion.15
  32.7 0.1 select_reduce_fusion
  32.9 0.7 select_n.94
  33.6 3.9 %all-to-all-start = ((s32[32,1,8]{2,1,0:T(1,128)}), s32[32,1,8]{2,1,0:T(1,128)S(1)}, u32[]{:S(2)}, u32[]{:S(2)}) async-start(s32[32,1,8]{2,1,0:T(1,128)} %bitcast.11), calls=%async_computation | async-start | bytes 32768 | tf_op jit(solution)/shard_map/all_to_all | solution.py:186
  37.4 2.1 %multiply_reduce_fusion.3 = bf16[128]{0:T(256)(128)(2,1)S(1)} fusion(f32[128,8,128]{2,1,0:T(8,128)} %param.18), kind=kLoop, calls=%fused_computation.37 | loop fusion | flops 262016 | bytes 524544 | tf_op jit(solution)/shard_map/reduce_sum | solution.py:161
  39.5 6.6 %multiply_convert_fusion.1 = (bf16[4096,512]{1,0:T(8,128)(2,1)S(1)}, f32[4096,512]{1,0:T(8,128)}) fusion(bf16[13,4096]{1,0:T(8,128)(2,1)} %param.25, f32[13,512]{1,0:T(8,128)} %param.27), kind=kOutput, calls=%fused_computation.2 | convolution fusion | flops 65018368 | bytes 12716032 | tf_op jit(solution)/shard_map/dot_general | solution.py:90
  46.1 1.3 fusion.18
  47.4 1.7 fusion
  49.1 2.1 %convolution_bitcast_fusion.1 = f32[64,2,8,128]{3,2,1,0:T(8,128)} fusion(bf16[4096,512]{1,0:T(8,128)(2,1)S(1)} %get-tuple-element.102, bf16[4096,256]{1,0:T(8,128)(2,1)S(1)} %fusion), kind=kOutput, calls=%fused_computation.12 | convolution fusion | flops 1073741824 | bytes 6815744 | tf_op jit(solution)/shard_map/dot_general | solution.py:105
  51.2 1.3 convolution_bitcast_fusion
  52.5 7.6 %fusion.3 = f32[13,512]{1,0:T(8,128)S(1)} fusion(bf16[13,4096]{1,0:T(8,128)(2,1)S(1)} %copy-done.18, f32[4096,512]{1,0:T(8,128)} %get-tuple-element.103, bf16[4096,256]{1,0:T(8,128)(2,1)} %copy-done.20, f32[512,256]{1,0:T(8,128)S(1)} %copy-done.1), kind=kOutput, calls=%fused_computation.13 | convolution fusion | flops 1147273216 | bytes 11143168 | tf_op jit(solution)/shard_map/dot_general | solution.py:114
  60.2 0.2 convolution_bitcast_fusion.4
  60.4 0.4 copy.100
  60.8 1.0 copy.92
  61.9 2.0 %copy.95 = f32[128,8,128]{0,2,1:T(8,128)} copy(f32[128,8,128]{2,1,0:T(8,128)} %param.20) | data formatting | bytes 1048576 | tf_op args[2]
  63.9 1.3 copy.107
  65.2 24.8 %all-gather = s32[256,1,8]{2,1,0:T(1,128)S(1)} all-gather(s32[32,1,8]{2,1,0:T(1,128)S(1)} %all-to-all-done), channel_id=2, replica_groups=mesh['grp'=8,'shard_0'=4,'shard_1'=4,'shard_2'=2] {'grp'}, dimensions={0}, use_global_device_ids=true | all-gather | bytes 9216 | tf_op jit(solution)/shard_map/all_gather | solution.py:189
  90.1 0.5 broadcast.181
  90.6 1.0 reduce.4
  91.5 0.1 eq.68
  91.6 0.4 convert_reduce_fusion
  92.0 0.0 all-gather.3.cloned.1.call-done
  92.1 6.6 %copy.93 = bf16[2048,1024]{0,1:T(8,128)(2,1)} copy(bf16[2048,1024]{1,0:T(8,128)(2,1)} %bitcast.74) | data formatting | bytes 8388608 | tf_op jit(solution)/shard_map/reshape | solution.py:188
  98.6 5.1 %multiply_reduce_fusion.2 = (bf16[128]{0:T(256)(128)(2,1)S(1)}, f32[128,8,128]{0,2,1:T(8,128)}, f32[128,8,128]{0,2,1:T(8,128)}, f32[128,8,128]{0,2,1:T(8,128)}) fusion(f32[128,8,128]{0,2,1:T(8,128)S(1)} %copy.100, pred[128]{0:T(512)(128)(4,1)S(1)} %broadcast_compare_fusion, f32[128,8,128]{0,2,1:T(8,128)S(1)} %copy-done.9, f32[128,8,128]{0,2,1:T(8,128)} %copy.95, ...), kind=kOutput, calls=%fused_computation.33 | convolution fusion | flops 539492224 | bytes 7348608 | tf_op jit(solution)/shard_map/dot_general | solution.py:191
  103.7 0.2 convolution_bitcast_fusion.3
  103.9 2.8 %concatenate.3 = f32[170752]{0:T(1024)S(1)} concatenate(f32[6656]{0:T(1024)S(1)} %reshape.152, f32[131072]{0:T(1024)S(1)} %bitcast.78, f32[32768]{0:T(1024)S(1)} %convolution_bitcast_fusion, f32[26]{0:T(128)S(1)} %convolution_bitcast_fusion.4, f32[26]{0:T(128)S(1)} %convolution_bitcast_fusion.3, f32[204]{0:T(256)S(1)} %broadcast_in_dim.74), dimensions={0} | concatenate | bytes 1366016 | tf_op jit(solution)/shard_map/concatenate | solution.py:27
  106.7 0.7 reshape_reshape.6
  107.5 0.3 copy.98
  107.7 21.0 %all_to_all.43 = f32[8,32,667]{2,1,0:T(8,128)S(1)} all-to-all(f32[8,32,667]{2,1,0:T(8,128)S(1)} %copy.98), channel_id=1, replica_groups=mesh['grp'=8,'shard_0'=4,'shard_1'=4,'shard_2'=2] {'shard_1','shard_2'}, dimensions={0} | all-to-all | bytes 1366016 | tf_op jit(solution)/shard_map/all_to_all | solution.py:54
  128.8 0.7 reduce_sum.125
  129.4 1.0 all_to_all.31
  130.4 16.4 %all_to_all.44 = f32[32,1,667]{2,1,0:T(1,128)S(1)} all-to-all(f32[32,1,667]{2,1,0:T(1,128)S(1)} %all_to_all.31), channel_id=1, replica_groups=mesh['grp'=8,'shard_0'=4,'shard_1'=4,'shard_2'=2] {'grp','shard_0'}, dimensions={0} | all-to-all | bytes 170752 | tf_op jit(solution)/shard_map/all_to_all | solution.py:62
  146.8 0.1 reduce_sum.126
  146.9 0.1 broadcast_in_dim.75
  147.0 12.3 %all_to_all.45 = f32[32,1,667]{2,1,0:T(1,128)S(1)} all-to-all(f32[32,1,667]{2,1,0:T(1,128)S(1)} %broadcast_in_dim.75), channel_id=1, replica_groups=mesh['grp'=8,'shard_0'=4,'shard_1'=4,'shard_2'=2] {'grp','shard_0'}, dimensions={0} | all-to-all | bytes 170752 | tf_op jit(solution)/shard_map/all_to_all | solution.py:32
  159.3 0.9 broadcast_in_dim.76
  160.2 7.1 %all-to-all-start.5 = ((f32[8,32,667]{2,1,0:T(8,128)}), f32[8,32,667]{2,1,0:T(8,128)S(1)}, u32[]{:S(2)}, u32[]{:S(2)}) async-start(f32[8,32,667]{2,1,0:T(8,128)} %broadcast_in_dim.76), calls=%async_computation.5 | async-start | bytes 1572864 | tf_op jit(solution)/shard_map/all_to_all | solution.py:32
  167.3 1.0 copy.104
  168.3 1.0 copy.105
  169.3 10.2 %all-to-all-done.5 = f32[8,32,667]{2,1,0:T(8,128)S(1)} async-done(((f32[8,32,667]{2,1,0:T(8,128)}), f32[8,32,667]{2,1,0:T(8,128)S(1)}, u32[]{:S(2)}, u32[]{:S(2)}) %all-to-all-start.5) | async-done | bytes 683040 | tf_op jit(solution)/shard_map/all_to_all | solution.py:32
  179.5 0.5 copy.99
  180.0 0.5 reshape_reshape.7
  180.5 0.2 fusion.4
  180.7 0.8 slice.30
  181.5 1.4 slice.32
  182.9 1.3 multiply_subtract_fusion.1
  184.1 1.0 copy.103
  185.2 0.6 multiply_reduce_fusion.6
  187.2 2.3 %multiply_reduce_fusion = (f32[]{:T(128)}, f32[]{:T(128)}, f32[512,256]{1,0:T(8,128)S(1)}, f32[512,256]{1,0:T(8,128)S(1)}) fusion(f32[512,256]{1,0:T(8,128)S(1)} %copy-done.1, f32[667,256]{1,0:T(8,128)S(1)} %slice.30, f32[512,256]{1,0:T(8,128)} %param.31, f32[512,256]{1,0:T(8,128)} %param.34), kind=kLoop, calls=%fused_computation.28 | loop fusion | flops 2228222 | bytes 3145736 | tf_op jit(solution)/shard_map/reduce_sum | solution.py:126
  190.9 1.8 multiply_reduce_fusion.4
  194.1 0.6 multiply_subtract_fusion.3
  194.8 1.1 multiply_subtract_fusion
  195.9 0.7 multiply_subtract_fusion.2
  (52 shorter events, 0.2 us)
Async XLA Ops:
  7.2 40.2 %copy-start = (bf16[4096,128]{1,0:T(8,128)(2,1)S(1)}, bf16[4096,128]{1,0:T(8,128)(2,1)}, u32[]{:S(2)}) copy-start(bf16[4096,128]{1,0:T(8,128)(2,1)} %param.26) | copy-start | bytes 3145732
  7.2 84.8 %all-gather.3.cloned.1.call-start = ((), (), s32[]{:S(2)}) async-start(), calls=%async_computation.6 | async-start | bytes 4718592 | tf_op jit(solution)/shard_map/all_gather | solution.py:188
  33.6 31.7 %all-to-all-start = ((s32[32,1,8]{2,1,0:T(1,128)}), s32[32,1,8]{2,1,0:T(1,128)S(1)}, u32[]{:S(2)}, u32[]{:S(2)}) async-start(s32[32,1,8]{2,1,0:T(1,128)} %bitcast.11), calls=%async_computation | async-start | bytes 32768 | tf_op jit(solution)/shard_map/all_to_all | solution.py:186
  39.5 6.6 %copy-start.1 = (f32[512,256]{1,0:T(8,128)S(1)}, f32[512,256]{1,0:T(8,128)}, u32[]{:S(2)}) copy-start(f32[512,256]{1,0:T(8,128)} %param.28) | copy-start | bytes 1572868
  46.1 1.3 copy-start.10
  49.1 2.1 %copy-start.20 = (bf16[4096,256]{1,0:T(8,128)(2,1)}, bf16[4096,256]{1,0:T(8,128)(2,1)S(1)}, u32[]{:S(2)}) copy-start(bf16[4096,256]{1,0:T(8,128)(2,1)S(1)} %fusion) | copy-start | bytes 6291460
  51.2 1.3 copy-start.18
  52.5 7.7 %copy-start.19 = (s32[128]{0:T(128)S(1)}, s32[128]{0:T(128)}, u32[]{:S(2)}) copy-start(s32[128]{0:T(128)} %param.21) | copy-start | bytes 1540
  52.5 7.9 %copy-start.2 = (f32[128,8,128]{2,1,0:T(8,128)S(1)}, f32[128,8,128]{2,1,0:T(8,128)}, u32[]{:S(2)}) copy-start(f32[128,8,128]{2,1,0:T(8,128)} %param.18) | copy-start | bytes 1572868
  52.5 8.3 %copy-start.6 = (f32[128,8,128]{2,1,0:T(8,128)S(1)}, f32[128,8,128]{2,1,0:T(8,128)}, u32[]{:S(2)}) copy-start(f32[128,8,128]{2,1,0:T(8,128)} %param.19) | copy-start | bytes 1572868
  60.8 37.8 %copy-start.3 = (f32[128,8,128]{0,2,1:T(8,128)}, f32[128,8,128]{0,2,1:T(8,128)S(1)}, u32[]{:S(2)}) copy-start(f32[128,8,128]{0,2,1:T(8,128)S(1)} %copy.100) | copy-start | bytes 1572868
  92.0 6.6 %copy-start.9 = (f32[128,8,128]{0,2,1:T(8,128)S(1)}, f32[128,8,128]{0,2,1:T(8,128)}, u32[]{:S(2)}) copy-start(f32[128,8,128]{0,2,1:T(8,128)} %copy.92) | copy-start | bytes 1572868
  107.4 59.9 %copy-start.8 = (f32[128,8,128]{0,2,1:T(8,128)S(1)}, f32[128,8,128]{0,2,1:T(8,128)}, u32[]{:S(2)}) copy-start(f32[128,8,128]{0,2,1:T(8,128)} %get-tuple-element.98) | copy-start | bytes 1572868
  107.4 60.9 %copy-start.7 = (f32[128,8,128]{0,2,1:T(8,128)S(1)}, f32[128,8,128]{0,2,1:T(8,128)}, u32[]{:S(2)}) copy-start(f32[128,8,128]{0,2,1:T(8,128)} %get-tuple-element.99) | copy-start | bytes 1572868
  160.2 19.3 %all-to-all-start.5 = ((f32[8,32,667]{2,1,0:T(8,128)}), f32[8,32,667]{2,1,0:T(8,128)S(1)}, u32[]{:S(2)}, u32[]{:S(2)}) async-start(f32[8,32,667]{2,1,0:T(8,128)} %broadcast_in_dim.76), calls=%async_computation.5 | async-start | bytes 1572864 | tf_op jit(solution)/shard_map/all_to_all | solution.py:32
  179.5 5.6 %copy-start.13 = (f32[13,512]{1,0:T(8,128)S(1)}, f32[13,512]{1,0:T(8,128)}, u32[]{:S(2)}) copy-start(f32[13,512]{1,0:T(8,128)} %param.27) | copy-start | bytes 79876
  179.5 5.6 %copy-start.16 = (f32[13,512]{1,0:T(8,128)S(1)}, f32[13,512]{1,0:T(8,128)}, u32[]{:S(2)}) copy-start(f32[13,512]{1,0:T(8,128)} %param.30) | copy-start | bytes 79876
  179.5 5.6 %copy-start.17 = (f32[13,512]{1,0:T(8,128)S(1)}, f32[13,512]{1,0:T(8,128)}, u32[]{:S(2)}) copy-start(f32[13,512]{1,0:T(8,128)} %param.33) | copy-start | bytes 79876
  185.8 10.8 %copy-start.14 = (f32[13,512]{1,0:T(8,128)}, f32[13,512]{1,0:T(8,128)S(1)}, u32[]{:S(2)}) copy-start(f32[13,512]{1,0:T(8,128)S(1)} %get-tuple-element.94) | copy-start | bytes 79876
  185.8 10.8 %copy-start.15 = (f32[13,512]{1,0:T(8,128)}, f32[13,512]{1,0:T(8,128)S(1)}, u32[]{:S(2)}) copy-start(f32[13,512]{1,0:T(8,128)S(1)} %get-tuple-element.95) | copy-start | bytes 79876
  189.5 7.1 %copy-start.4 = (f32[512,256]{1,0:T(8,128)}, f32[512,256]{1,0:T(8,128)S(1)}, u32[]{:S(2)}) copy-start(f32[512,256]{1,0:T(8,128)S(1)} %get-tuple-element.92) | copy-start | bytes 1572868
  189.5 7.1 %copy-start.5 = (f32[512,256]{1,0:T(8,128)}, f32[512,256]{1,0:T(8,128)S(1)}, u32[]{:S(2)}) copy-start(f32[512,256]{1,0:T(8,128)S(1)} %get-tuple-element.93) | copy-start | bytes 1572868
  192.7 3.9 %copy-start.11 = (f32[256,128]{1,0:T(8,128)}, f32[256,128]{1,0:T(8,128)S(1)}, u32[]{:S(2)}) copy-start(f32[256,128]{1,0:T(8,128)S(1)} %get-tuple-element.90) | copy-start | bytes 393220
  192.7 3.9 %copy-start.12 = (f32[256,128]{1,0:T(8,128)}, f32[256,128]{1,0:T(8,128)S(1)}, u32[]{:S(2)}) copy-start(f32[256,128]{1,0:T(8,128)S(1)} %get-tuple-element.91) | copy-start | bytes 393220
Sparse Core Ops, SparseCore 0:
  32.7 54.4 all-gather.2
where the time goes:
time: 204 us; the launch traced here: 203 us
  blocking collectives  94.5 us (46%)
  matrix products  27.5 us (13%)
  local copies, waits for them, and re-layouts  26.3 us (13%)
  between operations  18.6 us (9%)
  other arithmetic  15.3 us (8%)
  starting transfers between devices  11 us (5%)
  waiting for transfers between devices  10.2 us (5%)
    all_gather x1, blocking collectives, body(): lax.all_gather(recv_local, 'grp', axis=0, tiled=True).reshape(-1)  24.8 us
    all_to_all x1, blocking collectives, summed_on_arrival(): lax.all_to_all(cut_along(value, dim, count), axis, 0, 0, tiled=True)  21 us
    all_to_all x1, blocking collectives, body(): lax.all_to_all(send_rows, SHARD, split_axis=0, concat_axis=0, tiled=True)  19.9 us
    all_to_all x1, blocking collectives, summed_rows(): lax.all_to_all(nearer, far, split_axis=0, concat_axis=0, tiled=True)  16.4 us
    all_to_all x1, blocking collectives, from_everyone(): return lax.all_to_all(copies, axis, split_axis=0, concat_axis=0, tiled=True)  12.3 us
    all_to_all x1, waiting for transfers between devices, from_everyone(): return lax.all_to_all(copies, axis, split_axis=0, concat_axis=0, tiled=True)  10.2 us
    unnamed x50, local copies, waits for them, and re-layouts  7.89 us
    dot_general x1, matrix products, tower_grads(): grad_one = jnp.dot(dense_x, back_one, preferred_element_type=jnp.float32)  7.65 us
  transfers between devices with their start and end apart: 3, of which 1 were waited for; matrix products, arithmetic and copies ran while one was open for 16% of the time, Pallas kernels for 0%

commit v1 on v0

v1 whole, which is shorter than its diff:
```python
import functools
import jax
import jax.numpy as jnp
from jax import lax
from jax.experimental import pallas as pl
from jax.experimental.pallas import tpu as pltpu
from jax.sharding import Mesh
from jax.sharding import PartitionSpec as P

TABLES = 26
CAP = 8
SHARD = ("shard_0", "shard_1", "shard_2")
GRP_SHARD = ("grp", "shard_0", "shard_1", "shard_2")
SUB = 8
LANE = 128

beta_one = 0.9
beta_two = 0.999
corr_first = 1.0 - 0.9**10
corr_second = 1.0 - 0.999**10
adam_eps = 1e-06
decay_rate = 0.01
learn_rate = 0.1
ratio_eps = 1e-06

f32 = jnp.float32
bf16 = jnp.bfloat16
VMEM = pl.BlockSpec(memory_space=pltpu.VMEM)
SMEM = pl.BlockSpec(memory_space=pltpu.SMEM)


def lanes():
    return lax.broadcasted_iota(jnp.int32, (SUB, LANE), 1)


def subs():
    return lax.broadcasted_iota(jnp.int32, (SUB, LANE), 0)


def bucket_kernel(shards, blocks, ids, block_slot, grads, out, count, local):
    width = CAP + 1
    out[...] = jnp.zeros_like(out)
    for s in range(shards):
        count[s] = 0
    for r in range(shards * CAP):
        local[r] = 0

    def place(i, carry):
        slot = block_slot[ids[0, i]]
        owner = slot // blocks
        rank = count[owner]
        count[owner] = rank + 1
        out[owner * width + rank] = grads[i]
        local[owner * CAP + rank] = slot - owner * blocks + 1
        return carry

    lax.fori_loop(0, grads.shape[0], place, 0, unroll=8)
    lane = lanes()
    for s in range(shards):
        tile = jnp.zeros((SUB, LANE), f32)
        for a in range(CAP):
            tile = jnp.where(lane == a, local[s * CAP + a].astype(f32), tile)
        out[s * width + CAP] = tile.astype(bf16)


def bucketed(touched, block_slot, grads, shards, blocks):
    return pl.pallas_call(
        functools.partial(bucket_kernel, shards, blocks),
        out_shape=jax.ShapeDtypeStruct((shards * (CAP + 1), SUB, LANE), bf16),
        in_specs=[SMEM, SMEM, VMEM],
        out_specs=VMEM,
        scratch_shapes=[
            pltpu.SMEM((shards,), jnp.int32),
            pltpu.SMEM((shards * CAP,), jnp.int32),
        ],
        name="bucket",
    )(touched, block_slot, grads)


def combine_kernel(shards, groups, blocks, recv, out, total, place_v, place_s, hit, sem):
    width = CAP + 1
    own = blocks // groups
    for s in range(shards):
        place_v[s : s + 1, :] = recv[s * width + CAP].astype(f32)[0:1, :].astype(jnp.int32)
    copy = pltpu.make_async_copy(place_v, place_s, sem)
    copy.start()
    total[...] = jnp.zeros_like(total)
    for q in range(blocks + 1):
        hit[q] = 0
    copy.wait()

    def add(s, carry):
        for a in range(CAP):
            slot = place_s[s, a]
            total[slot] = total[slot] + recv[s * width + a].astype(f32)
            hit[slot] = 1
        return carry

    lax.fori_loop(0, shards, add, 0)
    lane = lanes()
    for g in range(groups):
        out[g * (own + 1) : g * (own + 1) + own] = total[1 + g * own : 1 + (g + 1) * own].astype(
            bf16
        )
        tile = jnp.zeros((SUB, LANE), f32)
        for j in range(own):
            tile = jnp.where(lane == j, hit[1 + g * own + j].astype(f32), tile)
        out[g * (own + 1) + own] = tile.astype(bf16)


def combined(recv, shards, groups, blocks):
    own = blocks // groups
    return pl.pallas_call(
        functools.partial(combine_kernel, shards, groups, blocks),
        out_shape=jax.ShapeDtypeStruct((groups * (own + 1), SUB, LANE), bf16),
        in_specs=[VMEM],
        out_specs=VMEM,
        scratch_shapes=[
            pltpu.VMEM((blocks + 1, SUB, LANE), f32),
            pltpu.VMEM((shards, LANE), jnp.int32),
            pltpu.SMEM((shards, LANE), jnp.int32),
            pltpu.SMEM((blocks + 1,), jnp.int32),
            pltpu.SemaphoreType.DMA,
        ],
        name="combine",
    )(recv)


def act(pre):
    gate = 0.5 * jnp.tanh(0.5 * pre) + 0.5
    hidden = pre * gate
    return hidden.astype(bf16), gate + hidden * (1.0 - gate)


def dot(a, b, ca, cb):
    return lax.dot_general(a, b, (((ca,), (cb,)), ((), ())), preferred_element_type=f32)


def tower_kernel(shards, x, cot, w_one_t, w_two, w_two_t, w_three, out, g_one, g_two, g_three):
    step = pl.program_id(0)

    @pl.when(step == 0)
    def _():
        g_one[...] = jnp.zeros_like(g_one)
        g_two[...] = jnp.zeros_like(g_two)
        g_three[...] = jnp.zeros_like(g_three)

    xs = x[...]
    cots = cot[...]
    hidden_one, slope_one = act(dot(w_one_t[...], xs, 1, 0))
    hidden_two, slope_two = act(dot(w_two_t[...], hidden_one, 1, 0))
    g_three[...] += dot(hidden_two, cots, 1, 0)
    back_two = (dot(w_three[...], cots, 1, 1) * slope_two).astype(bf16)
    g_two[...] += dot(hidden_one, back_two, 1, 1)
    back_one = (dot(w_two[...], back_two, 1, 0) * slope_one).astype(bf16)
    g_one[0 : xs.shape[0], :] += dot(xs, back_one, 1, 1)

    @pl.when(step == pl.num_programs(0) - 1)
    def _():
        rows_two = g_two.shape[0] // shards
        rows_three = g_three.shape[0] // shards
        halves = g_two.shape[1] // LANE
        for s in range(shards):
            at = 0
            for h in range(halves):
                for r in range(0, rows_two, SUB):
                    out[s, at] = g_two[
                        s * rows_two + r : s * rows_two + r + SUB, h * LANE : (h + 1) * LANE
                    ].astype(bf16)
                    at += 1
            for r in range(0, rows_three, SUB):
                out[s, at] = g_three[s * rows_three + r : s * rows_three + r + SUB, :].astype(bf16)
                at += 1
            c, r = s // 2, s % 2
            if c < g_one.shape[1] // LANE:
                out[s, at] = g_one[r * SUB : (r + 1) * SUB, c * LANE : (c + 1) * LANE].astype(bf16)
            else:
                out[s, at] = jnp.zeros((SUB, LANE), bf16)


def tower(x, cot, w_one, w_two, w_three, shards, tiles, step=512):
    din, samples = x.shape
    h_one, h_two = w_two.shape
    width = w_three.shape[1]
    whole = lambda shape: pl.BlockSpec(shape, lambda i: tuple(0 for _ in shape))
    macs = samples * (2 * din * h_one + 3 * h_one * h_two + 2 * h_two * width)
    return pl.pallas_call(
        functools.partial(tower_kernel, shards),
        grid=(samples // step,),
        out_shape=jax.ShapeDtypeStruct((shards, tiles, SUB, LANE), bf16),
        in_specs=[
            pl.BlockSpec((din, step), lambda i: (0, i)),
            pl.BlockSpec((step, width), lambda i: (i, 0)),
            whole((h_one, din)),
            whole((h_one, h_two)),
            whole((h_two, h_one)),
            whole((h_two, width)),
        ],
        out_specs=whole((shards, tiles, SUB, LANE)),
        scratch_shapes=[
            pltpu.VMEM((2 * SUB, h_one), f32),
            pltpu.VMEM((h_one, h_two), f32),
            pltpu.VMEM((h_two, width), f32),
        ],
        cost_estimate=pl.CostEstimate(
            flops=2 * macs, bytes_accessed=4 * samples * width, transcendentals=samples * h_one
        ),
        name="tower",
    )(
        x,
        cot,
        w_one.T.astype(bf16),
        w_two.astype(bf16),
        w_two.T.astype(bf16),
        w_three.astype(bf16),
    )


def lamb_step(weight, first_in, second_in, gradient):
    first_out = beta_one * first_in + (1.0 - beta_one) * gradient
    second_out = beta_two * second_in + (1.0 - beta_two) * gradient * gradient
    update = (
        first_out / corr_first / (jnp.sqrt(second_out / corr_second) + adam_eps)
        + decay_rate * weight
    )
    return update, first_out, second_out


def flags_of(tile, own):
    return [jnp.broadcast_to(tile[0:1, j : j + 1], (SUB, LANE)) > 0.5 for j in range(own)]


def split_rows(rows):
    tile = jnp.zeros((SUB, LANE), f32)
    sub = subs()
    for i, row in enumerate(rows):
        high = row.astype(bf16).astype(f32)
        tile = jnp.where(sub == 2 * i, high, tile)
        tile = jnp.where(sub == 2 * i + 1, row - high, tile)
    return tile.astype(bf16)


def own_kernel(groups, shards, tiles, who, slot_table, recv, dense, table, first, second, out):
    own = out.shape[1] - 2 - tiles
    at = who[0] * own
    rows = recv[0:own].astype(f32)
    flag = recv[own].astype(f32)
    for g in range(1, groups):
        rows = rows + recv[g * (own + 1) : g * (own + 1) + own].astype(f32)
        flag = flag + recv[g * (own + 1) + own].astype(f32)
    sent = rows.astype(bf16)
    touched = flags_of(flag, own)
    lane = lax.broadcasted_iota(jnp.int32, (1, LANE), 1)
    weight_sq = jnp.zeros((1, LANE), f32)
    update_sq = jnp.zeros((1, LANE), f32)
    for j in range(own):
        weight = table[at + j]
        update, unused, unused_too = lamb_step(
            weight, first[at + j], second[at + j], sent[j].astype(f32)
        )
        update = jnp.where(touched[j], update, 0.0)
        mine = lane == slot_table[at + j]
        weight_sq += jnp.where(mine, jnp.sum(weight * weight, keepdims=True), 0.0)
        update_sq += jnp.where(mine, jnp.sum(update * update, keepdims=True), 0.0)
    sums = dense[0].astype(f32)
    for s in range(1, shards):
        sums = sums + dense[s].astype(f32)
    sums = sums.astype(bf16)
    flag = flag.astype(bf16)
    both = split_rows((weight_sq, update_sq))
    for g in range(groups):
        out[g, 0:own] = sent
        out[g, own] = flag
        out[g, own + 1] = both
        out[g, own + 2 :] = sums


def owned(who, slot_table, recv, dense, table, first, second, groups, shards, tiles):
    own = table.shape[0] // groups
    return pl.pallas_call(
        functools.partial(own_kernel, groups, shards, tiles),
        out_shape=jax.ShapeDtypeStruct((groups, own + 2 + tiles, SUB, LANE), bf16),
        in_specs=[SMEM, SMEM] + [VMEM] * 5,
        out_specs=VMEM,
        name="own",
    )(who, slot_table, recv, dense, table, first, second)


def pack_kernel(groups, own, recv, out):
    dense = recv[0, own + 2 :].astype(f32)
    both = recv[0, own + 1].astype(f32)
    for g in range(1, groups):
        dense = dense + recv[g, own + 2 :].astype(f32)
        both = both + recv[g, own + 1].astype(f32)
    dense = dense.astype(bf16)
    both = split_rows((both[0:1] + both[1:2], both[2:3] + both[3:4]))
    for s in range(out.shape[0]):
        out[s, 0:-1] = dense
        out[s, out.shape[1] - 1] = both


def packed(recv, groups, shards, own, tiles):
    return pl.pallas_call(
        functools.partial(pack_kernel, groups, own),
        out_shape=jax.ShapeDtypeStruct((shards, tiles + 1, SUB, LANE), bf16),
        in_specs=[VMEM],
        out_specs=VMEM,
        name="pack",
    )(recv)


def slots_kernel(groups, own, recv, table, first, second, new_first, new_second, update_out):
    for g in range(groups):
        touched = flags_of(recv[g, own].astype(f32), own)
        for j in range(own):
            q = g * own + j
            update, first_out, second_out = lamb_step(
                table[q], first[q], second[q], recv[g, j].astype(f32)
            )
            new_first[q] = jnp.where(touched[j], first_out, first[q])
            new_second[q] = jnp.where(touched[j], second_out, second[q])
            update_out[q] = jnp.where(touched[j], update, 0.0)


def slots(recv, table, first, second, groups, own):
    shape = jax.ShapeDtypeStruct(table.shape, f32)
    return pl.pallas_call(
        functools.partial(slots_kernel, groups, own),
        out_shape=(shape,) * 3,
        in_specs=[VMEM] * 4,
        out_specs=(VMEM,) * 3,
        cost_estimate=pl.CostEstimate(
            flops=2000 * table.size, bytes_accessed=24 * table.size, transcendentals=table.size
        ),
        name="slots",
    )(recv, table, first, second)


def lamb_whole(weight, first_in, second_in, gradient):
    update, first_out, second_out = lamb_step(weight, first_in, second_in, gradient)
    ratio = jnp.sqrt(jnp.sum(weight * weight, keepdims=True)) / (
        jnp.sqrt(jnp.sum(update * update, keepdims=True)) + ratio_eps
    )
    return (weight - learn_rate * ratio * update, first_out, second_out)


def last_kernel(
    shards,
    slot_table,
    recv,
    table,
    update,
    w_one,
    w_two,
    w_three,
    first_one,
    first_two,
    first_three,
    second_one,
    second_two,
    second_three,
    new_table,
    new_w_one,
    new_w_two,
    new_w_three,
    new_first_one,
    new_first_two,
    new_first_three,
    new_second_one,
    new_second_two,
    new_second_three,
    ratio_v,
    ratio_s,
    g_one,
    g_two,
    g_three,
    sem,
):
    tiles = recv.shape[1] - 1
    both = recv[0, tiles].astype(f32)
    for s in range(1, shards):
        both = both + recv[s, tiles].astype(f32)
    weight_sq = both[0:1] + both[1:2]
    update_sq = both[2:3] + both[3:4]
    ratio = learn_rate * (jnp.sqrt(weight_sq) / (jnp.sqrt(update_sq) + ratio_eps))
    ratio_v[...] = jnp.broadcast_to(ratio, (SUB, LANE))
    copy = pltpu.make_async_copy(ratio_v, ratio_s, sem)
    copy.start()
    rows_two = g_two.shape[0] // shards
    rows_three = g_three.shape[0] // shards
    halves = g_two.shape[1] // LANE
    for s in range(shards):
        at = 0
        for h in range(halves):
            for r in range(0, rows_two, SUB):
                g_two[s * rows_two + r : s * rows_two + r + SUB, h * LANE : (h + 1) * LANE] = recv[
                    s, at
                ].astype(f32)
                at += 1
        for r in range(0, rows_three, SUB):
            g_three[s * rows_three + r : s * rows_three + r + SUB, :] = recv[s, at].astype(f32)
            at += 1
        c, r = s // 2, s % 2
        if c < g_one.shape[1] // LANE:
            g_one[r * SUB : (r + 1) * SUB, c * LANE : (c + 1) * LANE] = recv[s, at].astype(f32)
    for w, f, v, g, nw, nf, nv in (
        (w_one, first_one, second_one, g_one, new_w_one, new_first_one, new_second_one),
        (w_two, first_two, second_two, g_two, new_w_two, new_first_two, new_second_two),
        (w_three, first_three, second_three, g_three, new_w_three, new_first_three, new_second_three),
    ):
        nw[...], nf[...], nv[...] = lamb_whole(w[...], f[...], v[...], g[0 : w.shape[0], :])
    copy.wait()

    def step(q, carry):
        new_table[q] = table[q] - ratio_s[0, slot_table[q]] * update[q]
        return carry

    lax.fori_loop(0, table.shape[0], step, 0, unroll=8)


def last(slot_table, recv, table, update, weights, shards):
    outs = (table,) + weights
    return pl.pallas_call(
        functools.partial(last_kernel, shards),
        out_shape=tuple(jax.ShapeDtypeStruct(a.shape, f32) for a in outs),
        in_specs=[SMEM] + [VMEM] * 12,
        out_specs=(VMEM,) * 10,
        scratch_shapes=[
            pltpu.VMEM((SUB, LANE), f32),
            pltpu.SMEM((SUB, LANE), f32),
            pltpu.VMEM((2 * SUB, weights[0].shape[1]), f32),
            pltpu.VMEM(weights[1].shape, f32),
            pltpu.VMEM(weights[2].shape, f32),
            pltpu.SemaphoreType.DMA,
        ],
        name="last",
    )(slot_table, recv, table, update, *weights)


def exchange(value, axis):
    return lax.all_to_all(value, axis, split_axis=0, concat_axis=0, tiled=True)


def body(
    table,
    table_first,
    table_second,
    slot_table,
    touched,
    emb_grads,
    block_slot,
    dense_x,
    dense_cot,
    w_one,
    w_two,
    w_three,
    first_one,
    first_two,
    first_three,
    second_one,
    second_two,
    second_three,
):
    shards = lax.axis_size(SHARD)
    groups = lax.axis_size("grp")
    blocks = table.shape[0]
    own = blocks // groups
    tiles = (w_two.size + w_three.size) // (shards * SUB * LANE) + 1
    who = jnp.reshape(lax.axis_index("grp"), (1,)).astype(jnp.int32)

    send = bucketed(touched, block_slot, emb_grads[0], shards, blocks)
    recv = exchange(send.reshape(shards, CAP + 1, SUB, LANE), SHARD)
    dense = tower(dense_x, dense_cot, w_one, w_two, w_three, shards, tiles)
    part = combined(recv.reshape(send.shape), shards, groups, blocks)
    dense = exchange(dense, SHARD)
    part = exchange(part.reshape(groups, own + 1, SUB, LANE), "grp")
    mine = owned(
        who,
        slot_table,
        part.reshape(-1, SUB, LANE),
        dense,
        table,
        table_first,
        table_second,
        groups,
        shards,
        tiles,
    )
    whole = exchange(mine, "grp")
    spread = exchange(packed(whole, groups, shards, own, tiles), SHARD)
    new_first, new_second, update = slots(whole, table, table_first, table_second, groups, own)
    weights = (
        w_one,
        w_two,
        w_three,
        first_one,
        first_two,
        first_three,
        second_one,
        second_two,
        second_three,
    )
    new_table, *rest = last(slot_table, spread, table, update, weights, shards)
    return (new_table, new_first, new_second, *rest)


def solution(mesh):
    finer = Mesh(
        mesh.devices.reshape(mesh.shape["grp"], 4, 4, 2), ("grp", "shard_0", "shard_1", "shard_2")
    )
    rows = P(SHARD, None, None)
    placed = (
        rows,
        rows,
        rows,
        P(SHARD),
        P("grp", SHARD),
        P("grp", SHARD, None, None),
        P(),
        P(None, GRP_SHARD),
        P(GRP_SHARD, None),
    ) + (P(),) * 9
    return jax.shard_map(
        body,
        mesh=finer,
        in_specs=placed,
        out_specs=(rows, rows, rows) + (P(),) * 9,
        check_vma=False,
    )
```

time: 204 us -> 112 us (0.55)
  blocking collectives: 94.5 us -> 18 us
  Pallas kernels: 0 us -> 32.9 us
  matrix products: 27.5 us -> 0 us
  local copies, waits for them, and re-layouts: 26.3 us -> 3.26 us
  starting transfers between devices: 11 us -> 29.9 us
  between operations: 18.6 us -> 0.74 us
  waiting for transfers between devices: 10.2 us -> 26.4 us
  other arithmetic: 15.3 us -> 0.64 us
    all_to_all x4 -> x1, blocking collectives: 69.7 us -> 18 us  [exchange(): return lax.all_to_all(value, axis, split_axis=0, concat_axis=0, tiled=True)]
    pallas_call x0 -> x7, Pallas kernels: none -> 32.9 us  [the longest x1 12.7 us: tower(): pl.pallas_call(functools.partial(tower_kernel, shards), grid=(samples //...]
    dot_general x11 -> x0, matrix products: 27.5 us -> none  [the longest x1 7.65 us: tower_grads(): grad_one = jnp.dot(dense_x, back_one, preferred_element_type=jnp.float32)]
    all_gather x1 -> x0, blocking collectives: 24.8 us -> none  [body(): lax.all_gather(recv_local, 'grp', axis=0, tiled=True).reshape(-1)]
    all_to_all x2 -> x4, starting transfers between devices: 11 us -> 29.9 us  [exchange(): return lax.all_to_all(value, axis, split_axis=0, concat_axis=0, tiled=True)]
    all_to_all x2 -> x4, waiting for transfers between devices: 10.2 us -> 26.4 us  [exchange(): return lax.all_to_all(value, axis, split_axis=0, concat_axis=0, tiled=True)]
    reduce_sum x9 -> x0, other arithmetic: 8.16 us -> none  [the longest x3 4.69 us: lamb_dense(): jnp.sum(update * update)]
    reshape x3 -> x0, local copies, waits for them, and re-layouts: 6.57 us -> none  [the longest x1 6.56 us: body(): lax.all_gather(recv_rows, 'grp', axis=0, tiled=True).reshape(-1, row_width)]
  transfers between devices with their start and end apart: 3 -> 4, of which waited for: 1 -> 3; matrix products, arithmetic and copies ran while one was open for 16% -> 2% of each run, Pallas kernels for 0% -> 18%
where the time goes in v1:
time: 112 us
  Pallas kernels  32.9 us (29%)
  starting transfers between devices  29.9 us (27%)
  waiting for transfers between devices  26.4 us (24%)
  blocking collectives  18 us (16%)
  local copies, waits for them, and re-layouts  3.26 us (3%)
    all_to_all x4, starting transfers between devices, exchange(): return lax.all_to_all(value, axis, split_axis=0, concat_axis=0, tiled=True)  29.9 us
    all_to_all x4, waiting for transfers between devices, exchange(): return lax.all_to_all(value, axis, split_axis=0, concat_axis=0, tiled=True)  26.4 us
    all_to_all x1, blocking collectives, exchange(): return lax.all_to_all(value, axis, split_axis=0, concat_axis=0, tiled=True)  18 us
    pallas_call x1, Pallas kernels, tower(): pl.pallas_call(functools.partial(tower_kernel, shards), grid=(samples //...  12.7 us
    pallas_call x1, Pallas kernels, last(): pl.pallas_call(functools.partial(last_kernel, shards), out_shape=tuple((j...  5.39 us
    pallas_call x1, Pallas kernels, combined(): pl.pallas_call(functools.partial(combine_kernel, shards, groups, blocks),...  3.94 us
    pallas_call x1, Pallas kernels, bucketed(): pl.pallas_call(functools.partial(bucket_kernel, shards, blocks), out_shap...  3.31 us
    pallas_call x1, Pallas kernels, slots(): pl.pallas_call(functools.partial(slots_kernel, groups, own), out_shape=(s...  3.13 us
  transfers between devices with their start and end apart: 4, of which 3 were waited for; matrix products, arithmetic and copies ran while one was open for 2% of the time, Pallas kernels for 18%

profile of v1, /device:TPU:1, one launch (start us, length us, event | category | flops | bytes accessed | tf_op | source)
XLA Modules:
  0.0 111.7 jit_solution(11858129630647544367)
XLA Ops:
  0.6 3.3 %bucket.1 = bf16[288,8,128]{2,1,0:T(8,128)(2,1)} custom-call(s32[1,128]{1,0:T(1,128)} %ids.1, s32[4096]{0:T(1024)} %block_slot.1, bf16[128,8,128]{2,1,0:T(8,128)(2,1)} %bitcast.13), custom_call_target="tpu_custom_call" | custom-call | tf_op jit(solution)/shard_map/bucket/pallas_call | solution.py:67
  4.0 0.0 copy-start.7
  4.0 0.0 copy-start.6
  4.0 0.0 copy-start.1
  4.0 8.7 %all-to-all-start = ((bf16[32,9,8,128]{3,2,1,0:T(8,128)(2,1)}), bf16[32,9,8,128]{3,2,1,0:T(8,128)(2,1)S(1)}, u32[]{:S(2)}, u32[]{:S(2)}) async-start(bf16[32,9,8,128]{3,2,1,0:T(8,128)(2,1)} %bitcast.9), calls=%async_computation | async-start | bytes 1179648 | tf_op jit(solution)/shard_map/all_to_all | solution.py:441
  12.7 0.0 copy-done.7
  12.7 0.0 copy-done.6
  12.7 0.6 convert_element_type.18.w_three
  13.4 0.8 copy.30
  14.1 0.0 copy-done.1
  14.1 0.1 copy.31
  14.3 0.0 copy-start.5
  14.3 0.8 copy.32.w_two
  15.1 0.0 copy-done.5
  15.1 12.7 %tower.1 = bf16[32,6,8,128]{3,2,1,0:T(8,128)(2,1)} custom-call(bf16[13,4096]{1,0:T(8,128)(2,1)} %x.1, bf16[4096,128]{1,0:T(8,128)(2,1)} %cot.1, bf16[512,13]{1,0:T(8,128)(2,1)} %bitcast.14, bf16[512,256]{1,0:T(8,128)(2,1)} %copy.32.w_two, bf16[256,512]{1,0:T(8,128)(2,1)} %bitcast.12, bf16[256,128]{1,0:T(8,128)(2,1)} %convert_element_type.18.w_three), custom_call_target="tpu_custom_call" | custom-call | flops 3867148288 | bytes 2097152 | tf_op jit(solution)/shard_map/tower/pallas_call | solution.py:187
  27.8 0.0 all-to-all-done
  27.8 0.0 copy-start
  27.9 7.4 %all-to-all-start.2 = ((bf16[32,6,8,128]{3,2,1,0:T(8,128)(2,1)}), bf16[32,6,8,128]{3,2,1,0:T(8,128)(2,1)S(1)}, u32[]{:S(2)}, u32[]{:S(2)}) async-start(bf16[32,6,8,128]{3,2,1,0:T(8,128)(2,1)} %tower.1), calls=%async_computation.2 | async-start | bytes 786432 | tf_op jit(solution)/shard_map/all_to_all | solution.py:441
  35.3 0.0 copy-done
  35.3 3.9 %combine.1 = bf16[136,8,128]{2,1,0:T(8,128)(2,1)} custom-call(bf16[288,8,128]{2,1,0:T(8,128)(2,1)} %bitcast.8), custom_call_target="tpu_custom_call" | custom-call | tf_op jit(solution)/shard_map/combine/pallas_call | solution.py:113
  39.2 6.2 %all-to-all-done.2.dense = bf16[32,6,8,128]{3,2,1,0:T(8,128)(2,1)S(1)} async-done(((bf16[32,6,8,128]{3,2,1,0:T(8,128)(2,1)}), bf16[32,6,8,128]{3,2,1,0:T(8,128)(2,1)S(1)}, u32[]{:S(2)}, u32[]{:S(2)}) %all-to-all-start.2) | async-done | bytes 393248 | tf_op jit(solution)/shard_map/all_to_all | solution.py:441
  45.4 0.0 copy-start.3
  45.4 8.2 %all-to-all-start.1 = ((bf16[8,17,8,128]{3,2,1,0:T(8,128)(2,1)}), bf16[8,17,8,128]{3,2,1,0:T(8,128)(2,1)S(1)}, u32[]{:S(2)}, u32[]{:S(2)}) async-start(bf16[8,17,8,128]{3,2,1,0:T(8,128)(2,1)} %bitcast.11), calls=%async_computation.1 | async-start | bytes 557056 | tf_op jit(solution)/shard_map/all_to_all | solution.py:441
  53.6 12.5 %all-to-all-done.1 = bf16[8,17,8,128]{3,2,1,0:T(8,128)(2,1)S(1)} async-done(((bf16[8,17,8,128]{3,2,1,0:T(8,128)(2,1)}), bf16[8,17,8,128]{3,2,1,0:T(8,128)(2,1)S(1)}, u32[]{:S(2)}, u32[]{:S(2)}) %all-to-all-start.1) | async-done | bytes 278560 | tf_op jit(solution)/shard_map/all_to_all | solution.py:441
  66.1 0.0 copy-start.4
  66.1 0.0 copy-done.3
  66.1 0.7 copy-done.4
  66.8 2.6 %own.1 = bf16[8,24,8,128]{3,2,1,0:T(8,128)(2,1)} custom-call(s32[1]{0:T(128)} %bitcast.who, s32[128]{0:T(128)} %slot_table.3, bf16[136,8,128]{2,1,0:T(8,128)(2,1)} %bitcast.10, bf16[32,6,8,128]{3,2,1,0:T(8,128)(2,1)} %copy-done.3, f32[128,8,128]{2,1,0:T(8,128)} %table.5, f32[128,8,128]{2,1,0:T(8,128)} %first.3, f32[128,8,128]{2,1,0:T(8,128)} %second.3), custom_call_target="tpu_custom_call" | custom-call | tf_op jit(solution)/shard_map/own/pallas_call | solution.py:280
  69.4 18.0 %all_to_all.25.recv = bf16[8,24,8,128]{3,2,1,0:T(8,128)(2,1)} all-to-all(bf16[8,24,8,128]{3,2,1,0:T(8,128)(2,1)} %own.1), channel_id=1, replica_groups=mesh['grp'=8,'shard_0'=4,'shard_1'=4,'shard_2'=2] {'grp'}, dimensions={0} | all-to-all | bytes 786432 | tf_op jit(solution)/shard_map/all_to_all | solution.py:441
  87.4 1.8 %pack.1 = bf16[32,7,8,128]{3,2,1,0:T(8,128)(2,1)} custom-call(bf16[8,24,8,128]{3,2,1,0:T(8,128)(2,1)} %all_to_all.25.recv), custom_call_target="tpu_custom_call" | custom-call | tf_op jit(solution)/shard_map/pack/pallas_call | solution.py:303
  89.2 5.6 %all-to-all-start.4 = ((bf16[32,7,8,128]{3,2,1,0:T(8,128)(2,1)}), bf16[32,7,8,128]{3,2,1,0:T(8,128)(2,1)S(1)}, u32[]{:S(2)}, u32[]{:S(2)}) async-start(bf16[32,7,8,128]{3,2,1,0:T(8,128)(2,1)} %pack.1), calls=%async_computation.4 | async-start | bytes 917504 | tf_op jit(solution)/shard_map/all_to_all | solution.py:441
  94.7 3.1 %slots.1 = (f32[128,8,128]{2,1,0:T(8,128)}, f32[128,8,128]{2,1,0:T(8,128)}, f32[128,8,128]{2,1,0:T(8,128)}) custom-call(bf16[8,24,8,128]{3,2,1,0:T(8,128)(2,1)} %all_to_all.25.recv, f32[128,8,128]{2,1,0:T(8,128)} %table.5, f32[128,8,128]{2,1,0:T(8,128)} %first.3, f32[128,8,128]{2,1,0:T(8,128)} %second.3), custom_call_target="tpu_custom_call" | custom-call | flops 262144000 | bytes 3145728 | tf_op jit(solution)/shard_map/slots/pallas_call | solution.py:327
  97.9 7.7 %all-to-all-done.4.recv = bf16[32,7,8,128]{3,2,1,0:T(8,128)(2,1)S(1)} async-done(((bf16[32,7,8,128]{3,2,1,0:T(8,128)(2,1)}), bf16[32,7,8,128]{3,2,1,0:T(8,128)(2,1)S(1)}, u32[]{:S(2)}, u32[]{:S(2)}) %all-to-all-start.4) | async-done | bytes 458784 | tf_op jit(solution)/shard_map/all_to_all | solution.py:441
  105.5 0.0 copy-start.2
  105.5 0.8 copy-done.2
  106.3 5.4 %last.1 = (f32[128,8,128]{2,1,0:T(8,128)}, f32[13,512]{1,0:T(8,128)}, f32[512,256]{1,0:T(8,128)}, f32[256,128]{1,0:T(8,128)}, f32[13,512]{1,0:T(8,128)}, /*index...) custom-call(s32[128]{0:T(128)} %slot_table.3, ...), custom_call_target="tpu_custom_call" | custom-call | tf_op jit(solution)/shard_map/last/pallas_call | solution.py:423
  (1 shorter events, 0.0 us)
Async XLA Ops:
  4.0 8.7 %copy-start.7 = (f32[13,512]{1,0:T(8,128)S(1)}, f32[13,512]{1,0:T(8,128)}, u32[]{:S(2)}) copy-start(f32[13,512]{1,0:T(8,128)} %w_one.1) | copy-start | bytes 79876
  4.0 8.8 %copy-start.6 = (f32[256,128]{1,0:T(8,128)S(1)}, f32[256,128]{1,0:T(8,128)}, u32[]{:S(2)}) copy-start(f32[256,128]{1,0:T(8,128)} %w_three.1) | copy-start | bytes 393220
  4.0 10.2 %copy-start.1 = (f32[512,256]{1,0:T(8,128)S(1)}, f32[512,256]{1,0:T(8,128)}, u32[]{:S(2)}) copy-start(f32[512,256]{1,0:T(8,128)} %w_two.1) | copy-start | bytes 1572868
  4.0 23.9 %all-to-all-start = ((bf16[32,9,8,128]{3,2,1,0:T(8,128)(2,1)}), bf16[32,9,8,128]{3,2,1,0:T(8,128)(2,1)S(1)}, u32[]{:S(2)}, u32[]{:S(2)}) async-start(bf16[32,9,8,128]{3,2,1,0:T(8,128)(2,1)} %bitcast.9), calls=%async_computation | async-start | bytes 1179648 | tf_op jit(solution)/shard_map/all_to_all | solution.py:441
  14.3 0.9 copy-start.5
  27.8 7.4 %copy-start = (bf16[32,9,8,128]{3,2,1,0:T(8,128)(2,1)}, bf16[32,9,8,128]{3,2,1,0:T(8,128)(2,1)S(1)}, u32[]{:S(2)}) copy-start(bf16[32,9,8,128]{3,2,1,0:T(8,128)(2,1)S(1)} %all-to-all-done) | copy-start | bytes 1769476
  27.9 17.6 %all-to-all-start.2 = ((bf16[32,6,8,128]{3,2,1,0:T(8,128)(2,1)}), bf16[32,6,8,128]{3,2,1,0:T(8,128)(2,1)S(1)}, u32[]{:S(2)}, u32[]{:S(2)}) async-start(bf16[32,6,8,128]{3,2,1,0:T(8,128)(2,1)} %tower.1), calls=%async_computation.2 | async-start | bytes 786432 | tf_op jit(solution)/shard_map/all_to_all | solution.py:441
  45.4 20.7 %copy-start.3 = (bf16[32,6,8,128]{3,2,1,0:T(8,128)(2,1)}, bf16[32,6,8,128]{3,2,1,0:T(8,128)(2,1)S(1)}, u32[]{:S(2)}) copy-start(bf16[32,6,8,128]{3,2,1,0:T(8,128)(2,1)S(1)} %all-to-all-done.2.dense) | copy-start | bytes 1179652
  45.4 20.7 %all-to-all-start.1 = ((bf16[8,17,8,128]{3,2,1,0:T(8,128)(2,1)}), bf16[8,17,8,128]{3,2,1,0:T(8,128)(2,1)S(1)}, u32[]{:S(2)}, u32[]{:S(2)}) async-start(bf16[8,17,8,128]{3,2,1,0:T(8,128)(2,1)} %bitcast.11), calls=%async_computation.1 | async-start | bytes 557056 | tf_op jit(solution)/shard_map/all_to_all | solution.py:441
  66.1 0.7 copy-start.4
  89.2 16.4 %all-to-all-start.4 = ((bf16[32,7,8,128]{3,2,1,0:T(8,128)(2,1)}), bf16[32,7,8,128]{3,2,1,0:T(8,128)(2,1)S(1)}, u32[]{:S(2)}, u32[]{:S(2)}) async-start(bf16[32,7,8,128]{3,2,1,0:T(8,128)(2,1)} %pack.1), calls=%async_computation.4 | async-start | bytes 917504 | tf_op jit(solution)/shard_map/all_to_all | solution.py:441
  105.5 0.8 copy-start.2

commit v2 on v1

v2 whole, which is shorter than its diff:
```python
import functools
import jax
import jax.numpy as jnp
from jax import lax
from jax.experimental import pallas as pl
from jax.experimental.pallas import tpu as pltpu
from jax.sharding import Mesh
from jax.sharding import PartitionSpec as P

TABLES = 26
CAP = 8
SHARD = ("shard_0", "shard_1", "shard_2")
GRP_SHARD = ("grp", "shard_0", "shard_1", "shard_2")
SUB = 8
LANE = 128

beta_one = 0.9
beta_two = 0.999
corr_first = 1.0 - 0.9**10
corr_second = 1.0 - 0.999**10
adam_eps = 1e-06
decay_rate = 0.01
learn_rate = 0.1
ratio_eps = 1e-06

f32 = jnp.float32
bf16 = jnp.bfloat16
VMEM = pl.BlockSpec(memory_space=pltpu.VMEM)
SMEM = pl.BlockSpec(memory_space=pltpu.SMEM)


LIMIT = pltpu.CompilerParams(vmem_limit_bytes=20 * 2**20)


def iota(shape, dim):
    return lax.broadcasted_iota(jnp.int32, shape, dim)


def subs():
    return iota((SUB, LANE), 0)


def dot(a, b, ca, cb):
    return lax.dot_general(a, b, (((ca,), (cb,)), ((), ())), preferred_element_type=f32)


def log_two(n):
    return n.bit_length() - 1


def route_kernel(shards, blocks, groups, ids, block_slot, grads, out, wide):
    count = ids.shape[1]
    wide[...] = grads[...].astype(f32)
    for g in range(groups):
        rows = wide[pl.ds(g, count, stride=groups), :]
        out[g, 0 : count // SUB] = rows.reshape(count // SUB, SUB, LANE).astype(bf16)
    table_rows = block_slot.shape[0]
    high = ids[...] >> log_two(LANE)
    low = ids[...] & (LANE - 1)
    high_hot = iota((table_rows, count), 0) == high
    low_hot = iota((LANE, count), 0) == low
    slot = block_slot[...]
    one = high_hot.astype(f32).astype(bf16)
    owner_of = (slot >> log_two(blocks)).astype(f32).astype(bf16)
    local_of = (slot & (blocks - 1)).astype(f32).astype(bf16)
    owner = jnp.sum(jnp.where(low_hot, dot(owner_of, one, 0, 0), 0.0), axis=0, keepdims=True)
    local = jnp.sum(jnp.where(low_hot, dot(local_of, one, 0, 0), 0.0), axis=0, keepdims=True)
    owner_hot = iota((shards, count), 0).astype(f32) == owner
    before = (iota((count, count), 0) < iota((count, count), 1)).astype(f32).astype(bf16)
    rank = dot(owner_hot.astype(f32).astype(bf16), before, 1, 0)
    rank = jnp.sum(jnp.where(owner_hot, rank, 0.0), axis=0, keepdims=True)
    sub = iota((SUB, count), 0)
    tile = jnp.where(sub == 0, owner * CAP + rank, jnp.where(sub == 1, local + 1.0, 0.0))
    tile = tile.astype(bf16)
    for g in range(groups):
        out[g, count // SUB] = tile


def routed(ids, block_slot, grads, shards, blocks, groups):
    count = ids.shape[1]
    return pl.pallas_call(
        functools.partial(route_kernel, shards, blocks, groups),
        out_shape=jax.ShapeDtypeStruct((groups, count // SUB + 1, SUB, LANE), bf16),
        in_specs=[VMEM] * 3,
        out_specs=VMEM,
        scratch_shapes=[pltpu.VMEM(grads.shape, f32)],
        compiler_params=LIMIT,
        name="route",
    )(ids, block_slot, grads)


def bucket_kernel(shards, who, recv, dense, out):
    groups = recv.shape[0]
    tiles = dense.shape[1]
    count = LANE
    local_rows = jnp.zeros((shards, LANE), f32)
    for g in range(groups):
        tile = recv[g, count // SUB].astype(f32)
        place = tile[0:1].astype(jnp.int32)
        picker = (iota((shards * CAP, count), 0) == place).astype(f32).astype(bf16)
        rows = recv[g, 0 : count // SUB].astype(f32).reshape(count, LANE).astype(bf16)
        out[:, g] = dot(picker, rows, 1, 0).reshape(shards, SUB, LANE).astype(bf16)
        owner = place >> log_two(CAP)
        lane = (place & (CAP - 1)) + g * CAP + who[2] * (LANE // 2)
        local = jnp.where(iota((shards, count), 0) == owner, tile[1:2], 0.0).astype(bf16)
        spot = (iota((LANE, count), 0) == lane).astype(f32).astype(bf16)
        local_rows += dot(local, spot, 1, 1)
    sub = subs()
    for s in range(shards):
        out[s, groups : groups + tiles - 1] = dense[s, 0 : tiles - 1]
        tile = dense[s, tiles - 1].astype(f32)
        tile = jnp.where(sub == meta_row(s), local_rows[s : s + 1], tile)
        out[s, groups + tiles - 1] = tile.astype(bf16)


def meta_row(s):
    return (2 * (s % 4) + 2) % SUB


def bucketed(who, recv, dense):
    shards, tiles = dense.shape[:2]
    return pl.pallas_call(
        functools.partial(bucket_kernel, shards),
        out_shape=jax.ShapeDtypeStruct((shards, recv.shape[0] + tiles, SUB, LANE), bf16),
        in_specs=[SMEM, VMEM, VMEM],
        out_specs=VMEM,
        compiler_params=LIMIT,
        name="bucket",
    )(who, recv, dense)


def act(pre):
    gate = 0.5 * jnp.tanh(0.5 * pre) + 0.5
    hidden = pre * gate
    return hidden.astype(bf16), gate + hidden * (1.0 - gate)


def tower_kernel(
    shards, x, cot, w_one_in, w_two_in, w_three_in, out, g_one, g_two, g_three, w_two, w_two_t
):
    step = pl.program_id(0)

    @pl.when(step == 0)
    def _():
        g_one[...] = jnp.zeros_like(g_one)
        g_two[...] = jnp.zeros_like(g_two)
        g_three[...] = jnp.zeros_like(g_three)
        w_two[...] = w_two_in[...].astype(bf16)
        w_two_t[...] = w_two_in[...].T.astype(bf16)

    xs = x[...]
    cots = cot[...]
    hidden_one, slope_one = act(dot(w_one_in[...].astype(bf16), xs, 0, 0))
    hidden_two, slope_two = act(dot(w_two_t[...], hidden_one, 1, 0))
    g_three[...] += dot(hidden_two, cots, 1, 0)
    back_two = (dot(w_three_in[...].astype(bf16), cots, 1, 1) * slope_two).astype(bf16)
    g_two[...] += dot(hidden_one, back_two, 1, 1)
    back_one = (dot(w_two[...], back_two, 1, 0) * slope_one).astype(bf16)
    g_one[0 : xs.shape[0], :] += dot(xs, back_one, 1, 1)

    @pl.when(step == pl.num_programs(0) - 1)
    def _():
        rows_two = g_two.shape[0] // shards
        rows_three = g_three.shape[0] // shards
        halves = g_two.shape[1] // LANE
        for s in range(shards):
            at = 0
            for h in range(halves):
                for r in range(0, rows_two, SUB):
                    out[s, at] = g_two[
                        s * rows_two + r : s * rows_two + r + SUB, h * LANE : (h + 1) * LANE
                    ].astype(bf16)
                    at += 1
            for r in range(0, rows_three, SUB):
                out[s, at] = g_three[s * rows_three + r : s * rows_three + r + SUB, :].astype(bf16)
                at += 1
            c, r = s // 4 // 2, s // 4 % 2
            out[s, at] = g_one[r * SUB : (r + 1) * SUB, c * LANE : (c + 1) * LANE].astype(bf16)


def tower(x, cot, w_one, w_two, w_three, shards, tiles, step=512):
    din, samples = x.shape
    h_one, h_two = w_two.shape
    width = w_three.shape[1]
    whole = lambda shape: pl.BlockSpec(shape, lambda i: tuple(0 for _ in shape))
    macs = samples * (2 * din * h_one + 3 * h_one * h_two + 2 * h_two * width)
    return pl.pallas_call(
        functools.partial(tower_kernel, shards),
        grid=(samples // step,),
        out_shape=jax.ShapeDtypeStruct((shards, tiles, SUB, LANE), bf16),
        in_specs=[
            pl.BlockSpec((din, step), lambda i: (0, i)),
            pl.BlockSpec((step, width), lambda i: (i, 0)),
            whole((din, h_one)),
            whole((h_one, h_two)),
            whole((h_two, width)),
        ],
        out_specs=whole((shards, tiles, SUB, LANE)),
        scratch_shapes=[
            pltpu.VMEM((2 * SUB, h_one), f32),
            pltpu.VMEM((h_one, h_two), f32),
            pltpu.VMEM((h_two, width), f32),
            pltpu.VMEM((h_one, h_two), bf16),
            pltpu.VMEM((h_two, h_one), bf16),
        ],
        compiler_params=LIMIT,
        cost_estimate=pl.CostEstimate(
            flops=2 * macs, bytes_accessed=4 * samples * width, transcendentals=samples * h_one
        ),
        name="tower",
    )(x, cot, w_one, w_two, w_three)


def lamb_step(weight, first_in, second_in, gradient):
    first_out = beta_one * first_in + (1.0 - beta_one) * gradient
    second_out = beta_two * second_in + (1.0 - beta_two) * gradient * gradient
    update = (
        first_out / corr_first / (jnp.sqrt(second_out / corr_second) + adam_eps)
        + decay_rate * weight
    )
    return update, first_out, second_out


def split_rows(rows):
    tile = jnp.zeros((SUB, LANE), f32)
    sub = subs()
    for i, row in enumerate(rows):
        high = row.astype(bf16).astype(f32)
        tile = jnp.where(sub == 2 * i, high, tile)
        tile = jnp.where(sub == 2 * i + 1, row - high, tile)
    return tile.astype(bf16)


def table_hot(slot_table):
    return slot_table[...] == iota((slot_table.shape[0], LANE), 1)


def own_kernel(tiles, who, slot_table, recv, table, first, second, out, hit_out):
    shards = recv.shape[0]
    groups = out.shape[0]
    blocks = slot_table.shape[0]
    sub = subs()
    meta = meta_row(who[1])
    total = jnp.zeros((blocks, LANE), f32)
    hits = jnp.zeros((blocks, LANE), f32)
    slot = iota((blocks, LANE), 0) + 1
    for s in range(0, shards, 2):
        tile = recv[s, groups + tiles - 1].astype(f32) + recv[s + 1, groups + tiles - 1].astype(f32)
        place = jnp.sum(jnp.where(sub == meta, tile, 0.0), axis=0, keepdims=True)
        match = (slot == place.astype(jnp.int32)).astype(f32)
        rows = recv[s : s + 2, 0:groups].astype(f32).reshape(LANE, LANE).astype(bf16)
        total += dot(match.astype(bf16), rows, 1, 0)
        hits += match
    hits = dot(hits.astype(bf16), jnp.ones((LANE, LANE), bf16), 1, 0)
    hit_out[...] = hits
    sent = total.reshape(blocks // SUB, SUB, LANE).astype(bf16)
    column = pl.ds(who[0], blocks, stride=groups)
    weight = table[column, :]
    update, unused, unused_too = lamb_step(
        weight, first[column, :], second[column, :], sent.astype(f32).reshape(blocks, LANE)
    )
    update = jnp.where(hits > 0.5, update, 0.0)
    hot = table_hot(slot_table)
    sums = []
    for v in (weight, update):
        row = jnp.sum(v * v, axis=1, keepdims=True)
        sums.append(jnp.sum(jnp.where(hot, row, 0.0), axis=0, keepdims=True))
    both = split_rows(sums)
    dense = recv[0, groups:].astype(f32)
    for s in range(1, shards):
        dense = dense + recv[s, groups:].astype(f32)
    dense = dense.astype(bf16)
    for g in range(groups):
        out[g, 0 : blocks // SUB] = sent
        out[g, blocks // SUB : blocks // SUB + tiles] = dense
        out[g, blocks // SUB + tiles] = both


def owned(who, slot_table, recv, table, first, second, groups, tiles):
    blocks = slot_table.shape[0]
    return pl.pallas_call(
        functools.partial(own_kernel, tiles),
        out_shape=(
            jax.ShapeDtypeStruct((groups, blocks // SUB + tiles + 1, SUB, LANE), bf16),
            jax.ShapeDtypeStruct((blocks, LANE), f32),
        ),
        in_specs=[SMEM] + [VMEM] * 5,
        out_specs=(VMEM,) * 2,
        compiler_params=LIMIT,
        name="own",
    )(who, slot_table, recv, table, first, second)


def pack_kernel(tiles, recv, out):
    groups = recv.shape[0]
    start = recv.shape[1] - tiles - 1
    lines = recv[0, start:].astype(f32)
    for g in range(1, groups):
        lines = lines + recv[g, start:].astype(f32)
    dense = lines[0:tiles].astype(bf16)
    both = lines[tiles]
    both = split_rows((both[0:1] + both[1:2], both[2:3] + both[3:4]))
    for s in range(out.shape[0]):
        out[s, 0:tiles] = dense
        out[s, tiles] = both


def packed(recv, shards, tiles):
    return pl.pallas_call(
        functools.partial(pack_kernel, tiles),
        out_shape=jax.ShapeDtypeStruct((shards, tiles + 1, SUB, LANE), bf16),
        in_specs=[VMEM],
        out_specs=VMEM,
        compiler_params=LIMIT,
        name="pack",
    )(recv)


def slots_kernel(recv, hit, table, first, second, new_first, new_second, update_out):
    groups = recv.shape[0]
    blocks = hit.shape[0]
    touched = hit[...] > 0.5
    for g in range(groups):
        column = pl.ds(g, blocks, stride=groups)
        grad = recv[g, 0 : blocks // SUB].astype(f32).reshape(blocks, LANE)
        old_first, old_second = first[column, :], second[column, :]
        update, first_out, second_out = lamb_step(table[column, :], old_first, old_second, grad)
        new_first[column, :] = jnp.where(touched, first_out, old_first)
        new_second[column, :] = jnp.where(touched, second_out, old_second)
        update_out[column, :] = jnp.where(touched, update, 0.0)


def slots(recv, hit, table, first, second):
    shape = jax.ShapeDtypeStruct(table.shape, f32)
    return pl.pallas_call(
        slots_kernel,
        out_shape=(shape,) * 3,
        in_specs=[VMEM] * 5,
        out_specs=(VMEM,) * 3,
        cost_estimate=pl.CostEstimate(
            flops=2000 * table.size, bytes_accessed=24 * table.size, transcendentals=table.size
        ),
        compiler_params=LIMIT,
        name="slots",
    )(recv, hit, table, first, second)


def lamb_whole(weight, first_in, second_in, gradient):
    update, first_out, second_out = lamb_step(weight, first_in, second_in, gradient)
    ratio = jnp.sqrt(jnp.sum(weight * weight, keepdims=True)) / (
        jnp.sqrt(jnp.sum(update * update, keepdims=True)) + ratio_eps
    )
    return (weight - learn_rate * ratio * update, first_out, second_out)


def last_kernel(
    slot_table,
    recv,
    table,
    update,
    w_one,
    w_two,
    w_three,
    first_one,
    first_two,
    first_three,
    second_one,
    second_two,
    second_three,
    new_table,
    new_w_one,
    new_w_two,
    new_w_three,
    new_first_one,
    new_first_two,
    new_first_three,
    new_second_one,
    new_second_two,
    new_second_three,
    g_one,
    g_two,
    g_three,
):
    shards = recv.shape[0]
    tiles = recv.shape[1] - 1
    both = recv[0, tiles].astype(f32)
    for s in range(1, shards):
        both = both + recv[s, tiles].astype(f32)
    weight_sq = both[0:1] + both[1:2]
    update_sq = both[2:3] + both[3:4]
    ratio = learn_rate * (jnp.sqrt(weight_sq) / (jnp.sqrt(update_sq) + ratio_eps))
    ratio = jnp.sum(jnp.where(table_hot(slot_table), ratio, 0.0), axis=1, keepdims=True)
    blocks = slot_table.shape[0]
    groups = table.shape[0] // blocks
    for g in range(groups):
        column = pl.ds(g, blocks, stride=groups)
        new_table[column, :] = table[column, :] - ratio * update[column, :]
    pair = subs() // 2
    rows_two = g_two.shape[0] // shards
    rows_three = g_three.shape[0] // shards
    halves = g_two.shape[1] // LANE
    for s in range(shards):
        at = 0
        for h in range(halves):
            for r in range(0, rows_two, SUB):
                g_two[s * rows_two + r : s * rows_two + r + SUB, h * LANE : (h + 1) * LANE] = recv[
                    s, at
                ].astype(f32)
                at += 1
        for r in range(0, rows_three, SUB):
            g_three[s * rows_three + r : s * rows_three + r + SUB, :] = recv[s, at].astype(f32)
            at += 1
    for k in range(shards // 4):
        tile = jnp.zeros((SUB, LANE), f32)
        for a in range(4):
            tile = jnp.where(pair == a, recv[4 * k + a, tiles - 1].astype(f32), tile)
        c, r = k // 2, k % 2
        g_one[r * SUB : (r + 1) * SUB, c * LANE : (c + 1) * LANE] = tile
    for w, f, v, g, nw, nf, nv in (
        (w_one, first_one, second_one, g_one, new_w_one, new_first_one, new_second_one),
        (w_two, first_two, second_two, g_two, new_w_two, new_first_two, new_second_two),
        (w_three, first_three, second_three, g_three, new_w_three, new_first_three, new_second_three),
    ):
        nw[...], nf[...], nv[...] = lamb_whole(w[...], f[...], v[...], g[0 : w.shape[0], :])


def last(slot_table, recv, table, update, weights):
    outs = (table,) + weights
    return pl.pallas_call(
        last_kernel,
        out_shape=tuple(jax.ShapeDtypeStruct(a.shape, f32) for a in outs),
        in_specs=[VMEM] * 13,
        out_specs=(VMEM,) * 10,
        scratch_shapes=[
            pltpu.VMEM((2 * SUB, weights[0].shape[1]), f32),
            pltpu.VMEM(weights[1].shape, f32),
            pltpu.VMEM(weights[2].shape, f32),
        ],
        compiler_params=LIMIT,
        name="last",
    )(slot_table, recv, table, update, *weights)


def exchange(value, axis):
    return lax.all_to_all(value, axis, split_axis=0, concat_axis=0, tiled=True)


def body(
    table,
    table_first,
    table_second,
    slot_table,
    touched,
    emb_grads,
    block_slot,
    dense_x,
    dense_cot,
    w_one,
    w_two,
    w_three,
    first_one,
    first_two,
    first_three,
    second_one,
    second_two,
    second_three,
):
    shards = lax.axis_size(SHARD)
    groups = lax.axis_size("grp")
    blocks = table.shape[0]
    tiles = (w_two.size + w_three.size) // (shards * SUB * LANE) + 1
    who = jnp.stack([lax.axis_index("grp"), lax.axis_index(SHARD), lax.axis_index(SHARD[2])])
    who = who.astype(jnp.int32)
    flat = lambda a: a.reshape(-1, LANE)
    slot_column = slot_table[:, None]

    recv = exchange(
        routed(touched, flat(block_slot), flat(emb_grads), shards, blocks, groups), "grp"
    )
    dense = tower(dense_x, dense_cot, w_one, w_two, w_three, shards, tiles)
    recv = exchange(bucketed(who, recv, dense), SHARD)
    rows = flat(table), flat(table_first), flat(table_second)
    mine, hit = owned(who, slot_column, recv, *rows, groups, tiles)
    whole = exchange(mine, "grp")
    spread = exchange(packed(whole, shards, tiles), SHARD)
    new_first, new_second, update = slots(whole, hit, *rows)
    weights = (
        w_one,
        w_two,
        w_three,
        first_one,
        first_two,
        first_three,
        second_one,
        second_two,
        second_three,
    )
    new_table, *rest = last(slot_column, spread, rows[0], update, weights)
    back = [a.reshape(table.shape) for a in (new_table, new_first, new_second)]
    return (*back, *rest)


def solution(mesh):
    finer = Mesh(
        mesh.devices.reshape(mesh.shape["grp"], 4, 4, 2), ("grp", "shard_0", "shard_1", "shard_2")
    )
    rows = P(SHARD, None, None)
    placed = (
        rows,
        rows,
        rows,
        P(SHARD),
        P("grp", SHARD),
        P("grp", SHARD, None, None),
        P(),
        P(None, GRP_SHARD),
        P(GRP_SHARD, None),
    ) + (P(),) * 9
    return jax.shard_map(
        body,
        mesh=finer,
        in_specs=placed,
        out_specs=(rows, rows, rows) + (P(),) * 9,
        check_vma=False,
    )
```

time: 112 us -> 98 us (0.88)
  Pallas kernels: 32.9 us -> 20.2 us
  starting transfers between devices: 29.9 us -> 23 us
  local copies, waits for them, and re-layouts: 3.26 us -> 9.68 us
  waiting for transfers between devices: 26.4 us -> 23.3 us
  blocking collectives: 18 us -> 20 us
    pallas_call x6, Pallas kernels: 20.2 us -> 8.92 us  [the longest x1 2.66 us: last(): pl.pallas_call(last_kernel, out_shape=tuple((jax.ShapeDtypeStruct(a.shape...]
    unnamed x17 -> x42, local copies, waits for them, and re-layouts: 1.63 us -> 9.56 us
    all_to_all x4 -> x3, starting transfers between devices: 29.9 us -> 23 us  [exchange(): return lax.all_to_all(value, axis, split_axis=0, concat_axis=0, tiled=True)]
    all_to_all x4 -> x3, waiting for transfers between devices: 26.4 us -> 23.3 us  [exchange(): return lax.all_to_all(value, axis, split_axis=0, concat_axis=0, tiled=True)]
    all_to_all x1, blocking collectives: 18 us -> 20 us  [exchange(): return lax.all_to_all(value, axis, split_axis=0, concat_axis=0, tiled=True)]
    convert_element_type x2 -> x0, local copies, waits for them, and re-layouts: 1.63 us -> none  [the longest x1 0.84 us: tower(): w_two.astype(bf16)]
    pallas_call x1, Pallas kernels: 12.7 us -> 11.3 us  [tower(): pl.pallas_call(functools.partial(tower_kernel, shards), grid=(samples //...]
  transfers between devices with their start and end apart: 4 -> 3, of which waited for: 3 -> 2; matrix products, arithmetic and copies ran while one was open for 2% -> 0% of each run, Pallas kernels for 18% -> 13%
where the time goes in v2:
time: 98 us; the launch traced here: 97.1 us
  waiting for transfers between devices  23.3 us (24%)
  starting transfers between devices  23 us (23%)
  Pallas kernels  20.2 us (21%)
  blocking collectives  20 us (20%)
  local copies, waits for them, and re-layouts  9.68 us (10%)
    all_to_all x3, waiting for transfers between devices, exchange(): return lax.all_to_all(value, axis, split_axis=0, concat_axis=0, tiled=True)  23.3 us
    all_to_all x3, starting transfers between devices, exchange(): return lax.all_to_all(value, axis, split_axis=0, concat_axis=0, tiled=True)  23 us
    all_to_all x1, blocking collectives, exchange(): return lax.all_to_all(value, axis, split_axis=0, concat_axis=0, tiled=True)  20 us
    pallas_call x1, Pallas kernels, tower(): pl.pallas_call(functools.partial(tower_kernel, shards), grid=(samples //...  11.3 us
    unnamed x42, local copies, waits for them, and re-layouts  9.56 us
    pallas_call x1, Pallas kernels, last(): pl.pallas_call(last_kernel, out_shape=tuple((jax.ShapeDtypeStruct(a.shape...  2.66 us
  transfers between devices with their start and end apart: 3, of which 2 were waited for; matrix products, arithmetic and copies ran while one was open for 0% of the time, Pallas kernels for 13%

profile of v2, /device:TPU:1, one launch (start us, length us, event | category | flops | bytes accessed | tf_op | source)
XLA Modules:
  0.0 97.1 jit_solution(6790302016599935808)
XLA Ops:
  0.6 0.0 copy-start.17
  0.7 0.6 copy-done.17
  1.3 0.0 copy-start.8
  1.3 0.9 copy-done.8
  2.3 0.0 copy-start.16
  2.3 0.7 copy-done.16
  3.0 0.0 copy-start.3
  3.0 1.0 %route.1 = bf16[8,17,8,128]{3,2,1,0:T(8,128)(2,1)} custom-call(s32[1,128]{1,0:T(1,128)S(1)} %copy-done.17, s32[32,128]{1,0:T(8,128)S(1)} %bitcast.20, bf16[1024,128]{1,0:T(8,128)(2,1)S(1)} %bitcast.19), custom_call_target="tpu_custom_call" | custom-call | tf_op jit(solution)/shard_map/route/pallas_call | solution.py:81
  4.0 0.0 copy-start.9
  4.0 0.0 copy-start.19
  4.0 9.1 %all-to-all-start = ((bf16[8,17,8,128]{3,2,1,0:T(8,128)(2,1)}), bf16[8,17,8,128]{3,2,1,0:T(8,128)(2,1)S(1)}, u32[]{:S(2)}, u32[]{:S(2)}) async-start(bf16[8,17,8,128]{3,2,1,0:T(8,128)(2,1)} %route.1), calls=%async_computation | async-start | bytes 557056 | tf_op jit(solution)/shard_map/all_to_all | solution.py:445
  13.1 0.0 copy-start.12
  13.2 0.1 pad_add_fusion.who
  13.2 0.0 copy-done.3
  13.2 0.0 copy-done.9
  13.2 0.0 copy-done.19
  13.2 0.7 copy-done.12
  13.9 0.0 copy-start.18
  13.9 1.2 %copy-done.18 = bf16[4096,128]{1,0:T(8,128)(2,1)S(1)} copy-done((bf16[4096,128]{1,0:T(8,128)(2,1)S(1)}, bf16[4096,128]{1,0:T(8,128)(2,1)}, u32[]{:S(2)}) %copy-start.18) | copy-done | bytes 1048600
  15.1 11.3 %tower.1.dense = bf16[32,6,8,128]{3,2,1,0:T(8,128)(2,1)S(1)} custom-call(bf16[13,4096]{1,0:T(8,128)(2,1)S(1)} %copy-done.19, bf16[4096,128]{1,0:T(8,128)(2,1)S(1)} %copy-done.18, f32[13,512]{1,0:T(8,128)S(1)} %copy-done.12, f32[512,256]{1,0:T(8,128)S(1)} %copy-done.3, f32[256,128]{1,0:T(8,128)S(1)} %copy-done.9), custom_call_target="tpu_custom_call" | custom-call | flops 3867148288 | bytes 2097152 | tf_op jit(solution)/shard_map/tower/pallas_call | solution.py:187
  26.4 0.0 all-to-all-done.recv
  26.4 1.9 %bucket.1 = bf16[32,14,8,128]{3,2,1,0:T(8,128)(2,1)} custom-call(s32[3]{0:T(128)S(1)} %pad_add_fusion.who, bf16[8,17,8,128]{3,2,1,0:T(8,128)(2,1)S(1)} %all-to-all-done.recv, bf16[32,6,8,128]{3,2,1,0:T(8,128)(2,1)S(1)} %tower.1.dense), custom_call_target="tpu_custom_call" | custom-call | tf_op jit(solution)/shard_map/bucket/pallas_call | solution.py:122
  28.3 0.0 copy-start
  28.3 0.0 copy-start.1
  28.3 0.0 copy-start.2
  28.3 8.2 %all-to-all-start.1 = ((bf16[32,14,8,128]{3,2,1,0:T(8,128)(2,1)}), bf16[32,14,8,128]{3,2,1,0:T(8,128)(2,1)S(1)}, u32[]{:S(2)}, u32[]{:S(2)}) async-start(bf16[32,14,8,128]{3,2,1,0:T(8,128)(2,1)} %bucket.1), calls=%async_computation.1 | async-start | bytes 1835008 | tf_op jit(solution)/shard_map/all_to_all | solution.py:445
  36.5 0.0 copy-start.20
  36.5 0.6 copy-done.20
  37.2 0.1 copy.31.slot_table
  37.3 14.9 %all-to-all-done.1.recv = bf16[32,14,8,128]{3,2,1,0:T(8,128)(2,1)S(1)} async-done(((bf16[32,14,8,128]{3,2,1,0:T(8,128)(2,1)}), bf16[32,14,8,128]{3,2,1,0:T(8,128)(2,1)S(1)}, u32[]{:S(2)}, u32[]{:S(2)}) %all-to-all-start.1) | async-done | bytes 917536 | tf_op jit(solution)/shard_map/all_to_all | solution.py:445
  52.2 0.0 copy-done
  52.2 0.0 copy-done.1
  52.2 0.0 copy-done.2
  52.2 1.1 %own.1 = (bf16[8,23,8,128]{3,2,1,0:T(8,128)(2,1)S(1)}, f32[128,128]{1,0:T(8,128)S(1)}) custom-call(s32[3]{0:T(128)S(1)} %pad_add_fusion.who, s32[128,1]{1,0:T(8,128)S(1)} %copy.31.slot_table, bf16[32,14,8,128]{3,2,1,0:T(8,128)(2,1)S(1)} %all-to-all-done.1.recv, f32[1024,128]{1,0:T(8,128)S(1)} %bitcast.12, f32[1024,128]{1,0:T(8,128)S(1)} %bitcast.15, ...), custom_call_target="tpu_custom_call" | custom-call | tf_op jit(solution)/shard_map/own/pallas_call | solution.py:281
  53.2 20.0 %all_to_all.20.recv = bf16[8,23,8,128]{3,2,1,0:T(8,128)(2,1)S(1)} all-to-all(bf16[8,23,8,128]{3,2,1,0:T(8,128)(2,1)S(1)} %get-tuple-element.27), channel_id=1, replica_groups=mesh['grp'=8,'shard_0'=4,'shard_1'=4,'shard_2'=2] {'grp'}, dimensions={0} | all-to-all | bytes 753664 | tf_op jit(solution)/shard_map/all_to_all | solution.py:445
  73.3 0.8 pack.1
  74.1 5.7 %all-to-all-start.3 = ((bf16[32,7,8,128]{3,2,1,0:T(8,128)(2,1)}), bf16[32,7,8,128]{3,2,1,0:T(8,128)(2,1)S(1)}, u32[]{:S(2)}, u32[]{:S(2)}) async-start(bf16[32,7,8,128]{3,2,1,0:T(8,128)(2,1)} %pack.1), calls=%async_computation.3 | async-start | bytes 917504 | tf_op jit(solution)/shard_map/all_to_all | solution.py:445
  79.8 0.0 copy-start.10
  79.8 0.0 copy-start.11
  79.8 0.0 copy-start.13
  79.8 0.0 copy-start.14
  79.8 1.5 %slots.1 = (f32[1024,128]{1,0:T(8,128)}, f32[1024,128]{1,0:T(8,128)}, f32[1024,128]{1,0:T(8,128)S(1)}) custom-call(bf16[8,23,8,128]{3,2,1,0:T(8,128)(2,1)S(1)} %all_to_all.20.recv, f32[128,128]{1,0:T(8,128)S(1)} %get-tuple-element.28.hit, f32[1024,128]{1,0:T(8,128)S(1)} %bitcast.13, f32[1024,128]{1,0:T(8,128)S(1)} %bitcast.16, f32[1024,128]{1,0:T(8,128)S(1)} %bitcast.18), custom_call_target="tpu_custom_call" | custom-call | flops 262144000 | bytes 3145728 | tf_op jit(solution)/shard_map/slots/pallas_call | solution.py:335
  81.3 0.0 copy-start.6
  81.3 0.8 copy-done.6
  82.1 8.5 %all-to-all-done.3.recv = bf16[32,7,8,128]{3,2,1,0:T(8,128)(2,1)S(1)} async-done(((bf16[32,7,8,128]{3,2,1,0:T(8,128)(2,1)}), bf16[32,7,8,128]{3,2,1,0:T(8,128)(2,1)S(1)}, u32[]{:S(2)}, u32[]{:S(2)}) %all-to-all-start.3) | async-done | bytes 458784 | tf_op jit(solution)/shard_map/all_to_all | solution.py:445
  90.5 0.0 copy-done.10
  90.5 0.0 copy-done.11
  90.5 0.0 copy-done.13
  90.6 0.0 copy-done.14
  90.6 0.0 copy-start.4
  90.6 1.0 %copy-done.4 = f32[512,256]{1,0:T(8,128)S(1)} copy-done((f32[512,256]{1,0:T(8,128)S(1)}, f32[512,256]{1,0:T(8,128)}, u32[]{:S(2)}) %copy-start.4) | copy-done | bytes 524312
  91.6 0.0 copy-start.5
  91.6 1.0 %copy-done.5 = f32[512,256]{1,0:T(8,128)S(1)} copy-done((f32[512,256]{1,0:T(8,128)S(1)}, f32[512,256]{1,0:T(8,128)}, u32[]{:S(2)}) %copy-start.5) | copy-done | bytes 524312
  92.7 0.0 copy-start.7
  92.7 1.0 %copy-done.7 = f32[1024,128]{1,0:T(8,128)S(1)} copy-done((f32[1024,128]{1,0:T(8,128)S(1)}, f32[1024,128]{1,0:T(8,128)}, u32[]{:S(2)}) %copy-start.7) | copy-done | bytes 524312
  93.7 0.0 copy-start.15
  93.7 0.8 copy-done.15
  94.5 2.7 %last.1 = (f32[1024,128]{1,0:T(8,128)}, f32[13,512]{1,0:T(8,128)}, f32[512,256]{1,0:T(8,128)}, f32[256,128]{1,0:T(8,128)}, f32[13,512]{1,0:T(8,128)}, /*index=5*...) custom-call(s32[128,1]{1,0:T(8,128)S(1)} %copy.31.slot_table, ...), custom_call_target="tpu_custom_call" | custom-call | tf_op jit(solution)/shard_map/last/pallas_call | solution.py:429
Async XLA Ops:
  0.6 0.7 copy-start.17
  1.3 0.9 copy-start.8
  2.3 0.7 copy-start.16
  3.0 10.3 %copy-start.3 = (f32[512,256]{1,0:T(8,128)S(1)}, f32[512,256]{1,0:T(8,128)}, u32[]{:S(2)}) copy-start(f32[512,256]{1,0:T(8,128)} %w_two.1) | copy-start | bytes 1572868
  4.0 9.2 %copy-start.9 = (f32[256,128]{1,0:T(8,128)S(1)}, f32[256,128]{1,0:T(8,128)}, u32[]{:S(2)}) copy-start(f32[256,128]{1,0:T(8,128)} %w_three.1) | copy-start | bytes 393220
  4.0 9.2 %copy-start.19 = (bf16[13,4096]{1,0:T(8,128)(2,1)S(1)}, bf16[13,4096]{1,0:T(8,128)(2,1)}, u32[]{:S(2)}) copy-start(bf16[13,4096]{1,0:T(8,128)(2,1)} %x.1) | copy-start | bytes 319492
  4.0 22.4 %all-to-all-start = ((bf16[8,17,8,128]{3,2,1,0:T(8,128)(2,1)}), bf16[8,17,8,128]{3,2,1,0:T(8,128)(2,1)S(1)}, u32[]{:S(2)}, u32[]{:S(2)}) async-start(bf16[8,17,8,128]{3,2,1,0:T(8,128)(2,1)} %route.1), calls=%async_computation | async-start | bytes 557056 | tf_op jit(solution)/shard_map/all_to_all | solution.py:445
  13.1 0.8 copy-start.12
  13.9 1.2 %copy-start.18 = (bf16[4096,128]{1,0:T(8,128)(2,1)S(1)}, bf16[4096,128]{1,0:T(8,128)(2,1)}, u32[]{:S(2)}) copy-start(bf16[4096,128]{1,0:T(8,128)(2,1)} %cot.1) | copy-start | bytes 3145732
  28.3 23.8 %copy-start = (f32[128,8,128]{2,1,0:T(8,128)S(1)}, f32[128,8,128]{2,1,0:T(8,128)}, u32[]{:S(2)}) copy-start(f32[128,8,128]{2,1,0:T(8,128)} %param.18) | copy-start | bytes 1572868
  28.3 23.8 %copy-start.1 = (f32[128,8,128]{2,1,0:T(8,128)S(1)}, f32[128,8,128]{2,1,0:T(8,128)}, u32[]{:S(2)}) copy-start(f32[128,8,128]{2,1,0:T(8,128)} %param.19) | copy-start | bytes 1572868
  28.3 23.8 %copy-start.2 = (f32[128,8,128]{2,1,0:T(8,128)S(1)}, f32[128,8,128]{2,1,0:T(8,128)}, u32[]{:S(2)}) copy-start(f32[128,8,128]{2,1,0:T(8,128)} %param.20) | copy-start | bytes 1572868
  28.3 23.8 %all-to-all-start.1 = ((bf16[32,14,8,128]{3,2,1,0:T(8,128)(2,1)}), bf16[32,14,8,128]{3,2,1,0:T(8,128)(2,1)S(1)}, u32[]{:S(2)}, u32[]{:S(2)}) async-start(bf16[32,14,8,128]{3,2,1,0:T(8,128)(2,1)} %bucket.1), calls=%async_computation.1 | async-start | bytes 1835008 | tf_op jit(solution)/shard_map/all_to_all | solution.py:445
  36.5 0.7 copy-start.20
  74.1 16.5 %all-to-all-start.3 = ((bf16[32,7,8,128]{3,2,1,0:T(8,128)(2,1)}), bf16[32,7,8,128]{3,2,1,0:T(8,128)(2,1)S(1)}, u32[]{:S(2)}, u32[]{:S(2)}) async-start(bf16[32,7,8,128]{3,2,1,0:T(8,128)(2,1)} %pack.1), calls=%async_computation.3 | async-start | bytes 917504 | tf_op jit(solution)/shard_map/all_to_all | solution.py:445
  79.8 10.8 %copy-start.10 = (f32[256,128]{1,0:T(8,128)S(1)}, f32[256,128]{1,0:T(8,128)}, u32[]{:S(2)}) copy-start(f32[256,128]{1,0:T(8,128)} %first_three.1) | copy-start | bytes 393220
  79.8 10.8 %copy-start.11 = (f32[256,128]{1,0:T(8,128)S(1)}, f32[256,128]{1,0:T(8,128)}, u32[]{:S(2)}) copy-start(f32[256,128]{1,0:T(8,128)} %second_three.1) | copy-start | bytes 393220
  79.8 10.8 %copy-start.13 = (f32[13,512]{1,0:T(8,128)S(1)}, f32[13,512]{1,0:T(8,128)}, u32[]{:S(2)}) copy-start(f32[13,512]{1,0:T(8,128)} %w_one.1) | copy-start | bytes 79876
  79.8 10.8 %copy-start.14 = (f32[13,512]{1,0:T(8,128)S(1)}, f32[13,512]{1,0:T(8,128)}, u32[]{:S(2)}) copy-start(f32[13,512]{1,0:T(8,128)} %first_one.1) | copy-start | bytes 79876
  81.3 0.8 copy-start.6
  90.6 1.0 %copy-start.4 = (f32[512,256]{1,0:T(8,128)S(1)}, f32[512,256]{1,0:T(8,128)}, u32[]{:S(2)}) copy-start(f32[512,256]{1,0:T(8,128)} %first_two.1) | copy-start | bytes 1572868
  91.6 1.0 %copy-start.5 = (f32[512,256]{1,0:T(8,128)S(1)}, f32[512,256]{1,0:T(8,128)}, u32[]{:S(2)}) copy-start(f32[512,256]{1,0:T(8,128)} %second_two.1) | copy-start | bytes 1572868
  92.7 1.0 %copy-start.7 = (f32[1024,128]{1,0:T(8,128)S(1)}, f32[1024,128]{1,0:T(8,128)}, u32[]{:S(2)}) copy-start(f32[1024,128]{1,0:T(8,128)} %copy-done.6) | copy-start | bytes 1572868
  93.7 0.8 copy-start.15

commit v3 on v2

--- a/solution.py
+++ b/solution.py
@@ -27,9 +27,11 @@
 bf16 = jnp.bfloat16
 VMEM = pl.BlockSpec(memory_space=pltpu.VMEM)
 SMEM = pl.BlockSpec(memory_space=pltpu.SMEM)
+HBM = pl.BlockSpec(memory_space=pltpu.HBM)
 
 
 LIMIT = pltpu.CompilerParams(vmem_limit_bytes=20 * 2**20)
+WIDE = pltpu.CompilerParams(vmem_limit_bytes=53000 * 2**10)
 
 
 def iota(shape, dim):
@@ -84,7 +86,6 @@
         in_specs=[VMEM] * 3,
         out_specs=VMEM,
         scratch_shapes=[pltpu.VMEM(grads.shape, f32)],
-        compiler_params=LIMIT,
         name="route",
     )(ids, block_slot, grads)
 
@@ -129,84 +130,128 @@
     )(who, recv, dense)
 
 
-def act(pre):
-    gate = 0.5 * jnp.tanh(0.5 * pre) + 0.5
-    hidden = pre * gate
-    return hidden.astype(bf16), gate + hidden * (1.0 - gate)
+def act(half):
+    bend = jnp.tanh(half)
+    product = half * bend
+    return (product + half).astype(bf16), (1.0 + bend) + (half - product * bend)
 
 
 def tower_kernel(
-    shards, x, cot, w_one_in, w_two_in, w_three_in, out, g_one, g_two, g_three, w_two, w_two_t
+    shards,
+    parts,
+    x_in,
+    cot_in,
+    w_one_in,
+    w_two_in,
+    w_three_in,
+    out,
+    x,
+    cot,
+    raw_one,
+    raw_two,
+    raw_three,
+    w_one,
+    w_two,
+    w_two_t,
+    w_three,
+    g_one,
+    g_two,
+    g_three,
+    sem,
+    cot_sem,
 ):
-    step = pl.program_id(0)
-
-    @pl.when(step == 0)
-    def _():
-        g_one[...] = jnp.zeros_like(g_one)
-        g_two[...] = jnp.zeros_like(g_two)
-        g_three[...] = jnp.zeros_like(g_three)
-        w_two[...] = w_two_in[...].astype(bf16)
-        w_two_t[...] = w_two_in[...].T.astype(bf16)
-
-    xs = x[...]
-    cots = cot[...]
-    hidden_one, slope_one = act(dot(w_one_in[...].astype(bf16), xs, 0, 0))
-    hidden_two, slope_two = act(dot(w_two_t[...], hidden_one, 1, 0))
-    g_three[...] += dot(hidden_two, cots, 1, 0)
-    back_two = (dot(w_three_in[...].astype(bf16), cots, 1, 1) * slope_two).astype(bf16)
-    g_two[...] += dot(hidden_one, back_two, 1, 1)
-    back_one = (dot(w_two[...], back_two, 1, 0) * slope_one).astype(bf16)
-    g_one[0 : xs.shape[0], :] += dot(xs, back_one, 1, 1)
-
-    @pl.when(step == pl.num_programs(0) - 1)
-    def _():
-        rows_two = g_two.shape[0] // shards
-        rows_three = g_three.shape[0] // shards
-        halves = g_two.shape[1] // LANE
-        for s in range(shards):
-            at = 0
-            for h in range(halves):
-                for r in range(0, rows_two, SUB):
-                    out[s, at] = g_two[
-                        s * rows_two + r : s * rows_two + r + SUB, h * LANE : (h + 1) * LANE
-                    ].astype(bf16)
-                    at += 1
-            for r in range(0, rows_three, SUB):
-                out[s, at] = g_three[s * rows_three + r : s * rows_three + r + SUB, :].astype(bf16)
+    step = x.shape[1] // parts
+    copies = [
+        pltpu.make_async_copy(a, b, sem.at[i])
+        for i, (a, b) in enumerate(
+            ((w_one_in, raw_one), (x_in, x), (w_two_in, raw_two), (w_three_in, raw_three))
+        )
+    ]
+    chunks = [
+        pltpu.make_async_copy(
+            cot_in.at[pl.ds(k * step, step), :], cot.at[pl.ds(k * step, step), :], cot_sem.at[k]
+        )
+        for k in range(parts)
+    ]
+    for c in copies + chunks:
+        c.start()
+    copies[0].wait()
+    w_one[...] = (0.5 * raw_one[...]).astype(bf16)
+    copies[1].wait()
+    copies[2].wait()
+    w_two[...] = (0.5 * raw_two[...]).astype(bf16)
+    w_two_t[...] = (0.5 * raw_two[...]).T.astype(bf16)
+    copies[3].wait()
+    w_three[...] = (0.5 * raw_three[...]).astype(bf16)
+    sums = None
+    for k in range(parts):
+        xs = x[:, k * step : (k + 1) * step]
+        hidden_one, slope_one = act(dot(w_one[...], xs, 0, 0))
+        hidden_two, slope_two = act(dot(w_two_t[...], hidden_one, 1, 0))
+        chunks[k].wait()
+        cots = cot[k * step : (k + 1) * step, :]
+        three = dot(hidden_two, cots, 1, 0)
+        back_two = (dot(w_three[...], cots, 1, 1) * slope_two).astype(bf16)
+        two = dot(hidden_one, back_two, 1, 1)
+        back_one = (dot(w_two[...], back_two, 1, 0) * slope_one).astype(bf16)
+        one = dot(xs, back_one, 1, 1)
+        if k == 0:
+            g_one[0 : x.shape[0], :] = one
+            g_two[...] = two
+            g_three[...] = three
+        else:
+            g_one[0 : x.shape[0], :] += one
+            g_two[...] += two
+            g_three[...] += three
+    g_one[x.shape[0] :, :] = jnp.zeros((g_one.shape[0] - x.shape[0], g_one.shape[1]), f32)
+    rows_two = g_two.shape[0] // shards
+    rows_three = g_three.shape[0] // shards
+    halves = g_two.shape[1] // LANE
+    for s in range(shards):
+        at = 0
+        for h in range(halves):
+            for r in range(0, rows_two, SUB):
+                out[s, at] = g_two[
+                    s * rows_two + r : s * rows_two + r + SUB, h * LANE : (h + 1) * LANE
+                ].astype(bf16)
                 at += 1
-            c, r = s // 4 // 2, s // 4 % 2
-            out[s, at] = g_one[r * SUB : (r + 1) * SUB, c * LANE : (c + 1) * LANE].astype(bf16)
-
-
-def tower(x, cot, w_one, w_two, w_three, shards, tiles, step=512):
+        for r in range(0, rows_three, SUB):
+            out[s, at] = g_three[s * rows_three + r : s * rows_three + r + SUB, :].astype(bf16)
+            at += 1
+        c, r = s // 4 // 2, s // 4 % 2
+        out[s, at] = g_one[r * SUB : (r + 1) * SUB, c * LANE : (c + 1) * LANE].astype(bf16)
+
+
+def tower(x, cot, w_one, w_two, w_three, shards, tiles, parts=4):
     din, samples = x.shape
     h_one, h_two = w_two.shape
     width = w_three.shape[1]
-    whole = lambda shape: pl.BlockSpec(shape, lambda i: tuple(0 for _ in shape))
     macs = samples * (2 * din * h_one + 3 * h_one * h_two + 2 * h_two * width)
     return pl.pallas_call(
-        functools.partial(tower_kernel, shards),
-        grid=(samples // step,),
+        functools.partial(tower_kernel, shards, parts),
         out_shape=jax.ShapeDtypeStruct((shards, tiles, SUB, LANE), bf16),
-        in_specs=[
-            pl.BlockSpec((din, step), lambda i: (0, i)),
-            pl.BlockSpec((step, width), lambda i: (i, 0)),
-            whole((din, h_one)),
-            whole((h_one, h_two)),
-            whole((h_two, width)),
-        ],
-        out_specs=whole((shards, tiles, SUB, LANE)),
+        in_specs=[HBM] * 5,
+        out_specs=VMEM,
         scratch_shapes=[
+            pltpu.VMEM(x.shape, bf16),
+            pltpu.VMEM(cot.shape, bf16),
+            pltpu.VMEM(w_one.shape, f32),
+            pltpu.VMEM(w_two.shape, f32),
+            pltpu.VMEM(w_three.shape, f32),
+            pltpu.VMEM(w_one.shape, bf16),
+            pltpu.VMEM(w_two.shape, bf16),
+            pltpu.VMEM((h_two, h_one), bf16),
+            pltpu.VMEM(w_three.shape, bf16),
             pltpu.VMEM((2 * SUB, h_one), f32),
             pltpu.VMEM((h_one, h_two), f32),
             pltpu.VMEM((h_two, width), f32),
-            pltpu.VMEM((h_one, h_two), bf16),
-            pltpu.VMEM((h_two, h_one), bf16),
+            pltpu.SemaphoreType.DMA((4,)),
+            pltpu.SemaphoreType.DMA((parts,)),
         ],
-        compiler_params=LIMIT,
         cost_estimate=pl.CostEstimate(
             flops=2 * macs, bytes_accessed=4 * samples * width, transcendentals=samples * h_one
         ),
+        compiler_params=pltpu.CompilerParams(vmem_limit_bytes=54000 * 2**10),
         name="tower",
     )(x, cot, w_one, w_two, w_three)
 
@@ -316,18 +361,51 @@
     )(recv)
 
 
-def slots_kernel(recv, hit, table, first, second, new_first, new_second, update_out):
+def slots_kernel(
+    recv,
+    hit,
+    table_in,
+    first_in,
+    second_in,
+    new_first_out,
+    new_second_out,
+    update_out,
+    table,
+    first,
+    second,
+    update,
+    sem,
+    out_sem,
+):
     groups = recv.shape[0]
     blocks = hit.shape[0]
+    copies = [
+        pltpu.make_async_copy(a, b, sem.at[i])
+        for i, (a, b) in enumerate(((table_in, table), (first_in, first), (second_in, second)))
+    ]
+    for c in copies:
+        c.start()
     touched = hit[...] > 0.5
+    for c in copies:
+        c.wait()
     for g in range(groups):
         column = pl.ds(g, blocks, stride=groups)
         grad = recv[g, 0 : blocks // SUB].astype(f32).reshape(blocks, LANE)
         old_first, old_second = first[column, :], second[column, :]
-        update, first_out, second_out = lamb_step(table[column, :], old_first, old_second, grad)
-        new_first[column, :] = jnp.where(touched, first_out, old_first)
-        new_second[column, :] = jnp.where(touched, second_out, old_second)
-        update_out[column, :] = jnp.where(touched, update, 0.0)
+        change, first_out, second_out = lamb_step(table[column, :], old_first, old_second, grad)
+        first[column, :] = jnp.where(touched, first_out, old_first)
+        second[column, :] = jnp.where(touched, second_out, old_second)
+        update[column, :] = jnp.where(touched, change, 0.0)
+    copies = [
+        pltpu.make_async_copy(a, b, out_sem.at[i])
+        for i, (a, b) in enumerate(
+            ((update, update_out), (first, new_first_out), (second, new_second_out))
+        )
+    ]
+    for c in copies:
+        c.start()
+    for c in copies:
+        c.wait()
 
 
 def slots(recv, hit, table, first, second):
@@ -335,12 +413,14 @@
     return pl.pallas_call(
         slots_kernel,
         out_shape=(shape,) * 3,
-        in_specs=[VMEM] * 5,
-        out_specs=(VMEM,) * 3,
+        in_specs=[VMEM] * 2 + [HBM] * 3,
+        out_specs=(HBM,) * 3,
+        scratch_shapes=[pltpu.VMEM(table.shape, f32)] * 4
+        + [pltpu.SemaphoreType.DMA((3,)), pltpu.SemaphoreType.DMA((3,))],
         cost_estimate=pl.CostEstimate(
             flops=2000 * table.size, bytes_accessed=24 * table.size, transcendentals=table.size
         ),
-        compiler_params=LIMIT,
+        compiler_params=WIDE,
         name="slots",
     )(recv, hit, table, first, second)
 
@@ -353,34 +433,13 @@
     return (weight - learn_rate * ratio * update, first_out, second_out)
 
 
-def last_kernel(
-    slot_table,
-    recv,
-    table,
-    update,
-    w_one,
-    w_two,
-    w_three,
-    first_one,
-    first_two,
-    first_three,
-    second_one,
-    second_two,
-    second_three,
-    new_table,
-    new_w_one,
-    new_w_two,
-    new_w_three,
-    new_first_one,
-    new_first_two,
-    new_first_three,
-    new_second_one,
-    new_second_two,
-    new_second_three,
-    g_one,
-    g_two,
-    g_three,
-):
+def last_kernel(slot_table, recv, *refs):
+    ins, outs, scratch = refs[:11], refs[11:21], refs[21:]
+    held, made, (g_one, g_two, g_three, sem, out_sem) = scratch[:11], scratch[11:21], scratch[21:]
+    arrive = [pltpu.make_async_copy(a, b, sem.at[i]) for i, (a, b) in enumerate(zip(ins, held))]
+    leave = [pltpu.make_async_copy(a, b, out_sem.at[i]) for i, (a, b) in enumerate(zip(made, outs))]
+    for i in (3, 6, 9, 0, 1, 4, 7, 10, 2, 5, 8):
+        arrive[i].start()
     shards = recv.shape[0]
     tiles = recv.shape[1] - 1
     both = recv[0, tiles].astype(f32)
@@ -391,10 +450,7 @@
     ratio = learn_rate * (jnp.sqrt(weight_sq) / (jnp.sqrt(update_sq) + ratio_eps))
     ratio = jnp.sum(jnp.where(table_hot(slot_table), ratio, 0.0), axis=1, keepdims=True)
     blocks = slot_table.shape[0]
-    groups = table.shape[0] // blocks
-    for g in range(groups):
-        column = pl.ds(g, blocks, stride=groups)
-        new_table[column, :] = table[column, :] - ratio * update[column, :]
+    groups = ins[0].shape[0] // blocks
     pair = subs() // 2
     rows_two = g_two.shape[0] // shards
     rows_three = g_three.shape[0] // shards
@@ -416,29 +472,50 @@
             tile = jnp.where(pair == a, recv[4 * k + a, tiles - 1].astype(f32), tile)
         c, r = k // 2, k % 2
         g_one[r * SUB : (r + 1) * SUB, c * LANE : (c + 1) * LANE] = tile
-    for w, f, v, g, nw, nf, nv in (
-        (w_one, first_one, second_one, g_one, new_w_one, new_first_one, new_second_one),
-        (w_two, first_two, second_two, g_two, new_w_two, new_first_two, new_second_two),
-        (w_three, first_three, second_three, g_three, new_w_three, new_first_three, new_second_three),
-    ):
-        nw[...], nf[...], nv[...] = lamb_whole(w[...], f[...], v[...], g[0 : w.shape[0], :])
+
+    def dense(n, gradient):
+        for i in (2 + n, 5 + n, 8 + n):
+            arrive[i].wait()
+        weight, first, second = held[2 + n], held[5 + n], held[8 + n]
+        made[1 + n][...], made[4 + n][...], made[7 + n][...] = lamb_whole(
+            weight[...], first[...], second[...], gradient[0 : weight.shape[0], :]
+        )
+        for i in (1 + n, 4 + n, 7 + n):
+            leave[i].start()
+
+    dense(1, g_two)
+    arrive[0].wait()
+    arrive[1].wait()
+    table, update = held[:2]
+    for g in range(groups):
+        column = pl.ds(g, blocks, stride=groups)
+        made[0][column, :] = table[column, :] - ratio * update[column, :]
+    leave[0].start()
+    dense(2, g_three)
+    dense(0, g_one)
+    for c in leave:
+        c.wait()
 
 
 def last(slot_table, recv, table, update, weights):
+    ins = (table, update) + weights
     outs = (table,) + weights
     return pl.pallas_call(
         last_kernel,
         out_shape=tuple(jax.ShapeDtypeStruct(a.shape, f32) for a in outs),
-        in_specs=[VMEM] * 13,
-        out_specs=(VMEM,) * 10,
-        scratch_shapes=[
+        in_specs=[VMEM] * 2 + [HBM] * 11,
+        out_specs=(HBM,) * 10,
+        scratch_shapes=[pltpu.VMEM(a.shape, f32) for a in ins + outs]
+        + [
             pltpu.VMEM((2 * SUB, weights[0].shape[1]), f32),
             pltpu.VMEM(weights[1].shape, f32),
             pltpu.VMEM(weights[2].shape, f32),
+            pltpu.SemaphoreType.DMA((len(ins),)),
+            pltpu.SemaphoreType.DMA((len(outs),)),
         ],
-        compiler_params=LIMIT,
+        compiler_params=WIDE,
         name="last",
-    )(slot_table, recv, table, update, *weights)
+    )(slot_table, recv, *ins)
 
 
 def exchange(value, axis):

time: 98 us -> 91 us (0.929)
  local copies, waits for them, and re-layouts: 9.68 us -> 1.47 us
  Pallas kernels: 20.2 us -> 22.3 us
  blocking collectives: 20 us -> 18.1 us
  starting transfers between devices: 23 us -> 24.3 us
    unnamed x42 -> x24, local copies, waits for them, and re-layouts: 9.56 us -> 1.36 us
    all_to_all x1, blocking collectives: 20 us -> 18.1 us  [exchange(): return lax.all_to_all(value, axis, split_axis=0, concat_axis=0, tiled=True)]
    all_to_all x3, starting transfers between devices: 23 us -> 24.3 us  [exchange(): return lax.all_to_all(value, axis, split_axis=0, concat_axis=0, tiled=True)]
    pallas_call x1, Pallas kernels: 2.66 us -> 3.95 us  [last(): pl.pallas_call(last_kernel, out_shape=tuple((jax.ShapeDtypeStruct(a.shape...]
    pallas_call x1, Pallas kernels: 1.04 us -> 2.08 us  [routed(): pl.pallas_call(functools.partial(route_kernel, shards, blocks, groups), o...]
  transfers between devices with their start and end apart: 3 -> 3, of which waited for: 2 -> 3; matrix products, arithmetic and copies ran while one was open for 0% -> 0% of each run, Pallas kernels for 13% -> 14%
where the time goes in v3:
time: 91 us; the launch traced here: 90.4 us
  starting transfers between devices  24.3 us (27%)
  waiting for transfers between devices  23.2 us (25%)
  Pallas kernels  22.3 us (25%)
  blocking collectives  18.1 us (20%)
  local copies, waits for them, and re-layouts  1.47 us (2%)
  between operations  0.93 us (1%)
    all_to_all x3, starting transfers between devices, exchange(): return lax.all_to_all(value, axis, split_axis=0, concat_axis=0, tiled=True)  24.3 us
    all_to_all x3, waiting for transfers between devices, exchange(): return lax.all_to_all(value, axis, split_axis=0, concat_axis=0, tiled=True)  23.2 us
    all_to_all x1, blocking collectives, exchange(): return lax.all_to_all(value, axis, split_axis=0, concat_axis=0, tiled=True)  18.1 us
    pallas_call x1, Pallas kernels, tower(): pl.pallas_call(functools.partial(tower_kernel, shards, parts), out_shape=...  9.5 us
    pallas_call x1, Pallas kernels, last(): pl.pallas_call(last_kernel, out_shape=tuple((jax.ShapeDtypeStruct(a.shape...  3.95 us
    pallas_call x1, Pallas kernels, slots(): pl.pallas_call(slots_kernel, out_shape=(shape,) * 3, in_specs=[VMEM] * 2...  2.97 us
    pallas_call x1, Pallas kernels, routed(): pl.pallas_call(functools.partial(route_kernel, shards, blocks, groups), o...  2.08 us
    pallas_call x1, Pallas kernels, bucketed(): pl.pallas_call(functools.partial(bucket_kernel, shards), out_shape=jax.Sh...  1.88 us
  transfers between devices with their start and end apart: 3, of which 3 were waited for; matrix products, arithmetic and copies ran while one was open for 0% of the time, Pallas kernels for 14%

profile of v3, /device:TPU:1, one launch (start us, length us, event | category | flops | bytes accessed | tf_op | source)
XLA Modules:
  0.0 90.4 jit_solution(628599781220496730)
XLA Ops:
  0.6 0.0 copy-start.3
  0.7 2.1 %route.1 = bf16[8,17,8,128]{3,2,1,0:T(8,128)(2,1)} custom-call(s32[1,128]{1,0:T(1,128)} %ids.1, s32[32,128]{1,0:T(8,128)} %bitcast.20, bf16[1024,128]{1,0:T(8,128)(2,1)} %bitcast.19), custom_call_target="tpu_custom_call" | custom-call | tf_op jit(solution)/shard_map/route/pallas_call | solution.py:83
  2.7 0.0 copy-start.4
  2.7 0.0 copy-start.10
  2.7 9.1 %all-to-all-start = ((bf16[8,17,8,128]{3,2,1,0:T(8,128)(2,1)}), bf16[8,17,8,128]{3,2,1,0:T(8,128)(2,1)S(1)}, u32[]{:S(2)}, u32[]{:S(2)}) async-start(bf16[8,17,8,128]{3,2,1,0:T(8,128)(2,1)} %route.1), calls=%async_computation | async-start | bytes 557056 | tf_op jit(solution)/shard_map/all_to_all | solution.py:522
  11.9 0.0 copy-start.7
  11.9 0.1 pad_add_fusion.who
  12.0 0.0 copy-done.3
  12.0 0.0 copy-done.4
  12.0 0.0 copy-done.10
  12.0 0.7 copy-done.7
  12.6 9.5 %tower.1.dense = bf16[32,6,8,128]{3,2,1,0:T(8,128)(2,1)S(1)} custom-call(bf16[13,4096]{1,0:T(8,128)(2,1)S(1)} %copy-done.10, bf16[4096,128]{1,0:T(8,128)(2,1)} %cot_in.1, f32[13,512]{1,0:T(8,128)S(1)} %copy-done.7, f32[512,256]{1,0:T(8,128)S(1)} %copy-done.3, f32[256,128]{1,0:T(8,128)S(1)} %copy-done.4), custom_call_target="tpu_custom_call" | custom-call | flops 3867148288 | bytes 2097152 | tf_op jit(solution)/shard_map/tower/pallas_call | solution.py:230
  22.1 0.6 all-to-all-done.recv
  22.8 1.9 %bucket.1 = bf16[32,14,8,128]{3,2,1,0:T(8,128)(2,1)} custom-call(s32[3]{0:T(128)S(1)} %pad_add_fusion.who, bf16[8,17,8,128]{3,2,1,0:T(8,128)(2,1)S(1)} %all-to-all-done.recv, bf16[32,6,8,128]{3,2,1,0:T(8,128)(2,1)S(1)} %tower.1.dense), custom_call_target="tpu_custom_call" | custom-call | tf_op jit(solution)/shard_map/bucket/pallas_call | solution.py:123
  24.6 0.0 copy-start
  24.6 0.0 copy-start.1
  24.6 0.0 copy-start.2
  24.6 9.5 %all-to-all-start.1 = ((bf16[32,14,8,128]{3,2,1,0:T(8,128)(2,1)}), bf16[32,14,8,128]{3,2,1,0:T(8,128)(2,1)S(1)}, u32[]{:S(2)}, u32[]{:S(2)}) async-start(bf16[32,14,8,128]{3,2,1,0:T(8,128)(2,1)} %bucket.1), calls=%async_computation.1 | async-start | bytes 1835008 | tf_op jit(solution)/shard_map/all_to_all | solution.py:522
  34.2 0.0 copy-start.11
  34.2 0.6 copy-done.11
  34.8 0.1 copy.31.slot_table
  34.9 14.9 %all-to-all-done.1.recv = bf16[32,14,8,128]{3,2,1,0:T(8,128)(2,1)S(1)} async-done(((bf16[32,14,8,128]{3,2,1,0:T(8,128)(2,1)}), bf16[32,14,8,128]{3,2,1,0:T(8,128)(2,1)S(1)}, u32[]{:S(2)}, u32[]{:S(2)}) %all-to-all-start.1) | async-done | bytes 917536 | tf_op jit(solution)/shard_map/all_to_all | solution.py:522
  49.8 0.0 copy-done
  49.8 0.0 copy-done.1
  49.8 0.0 copy-done.2
  49.8 1.1 %own.1 = (bf16[8,23,8,128]{3,2,1,0:T(8,128)(2,1)S(1)}, f32[128,128]{1,0:T(8,128)S(1)}) custom-call(s32[3]{0:T(128)S(1)} %pad_add_fusion.who, s32[128,1]{1,0:T(8,128)S(1)} %copy.31.slot_table, bf16[32,14,8,128]{3,2,1,0:T(8,128)(2,1)S(1)} %all-to-all-done.1.recv, f32[1024,128]{1,0:T(8,128)S(1)} %bitcast.12, f32[1024,128]{1,0:T(8,128)S(1)} %bitcast.15, ...), custom_call_target="tpu_custom_call" | custom-call | tf_op jit(solution)/shard_map/own/pallas_call | solution.py:326
  50.9 18.1 %all_to_all.20.recv = bf16[8,23,8,128]{3,2,1,0:T(8,128)(2,1)S(1)} all-to-all(bf16[8,23,8,128]{3,2,1,0:T(8,128)(2,1)S(1)} %get-tuple-element.27), channel_id=1, replica_groups=mesh['grp'=8,'shard_0'=4,'shard_1'=4,'shard_2'=2] {'grp'}, dimensions={0} | all-to-all | bytes 753664 | tf_op jit(solution)/shard_map/all_to_all | solution.py:522
  69.0 0.8 pack.1
  69.8 5.7 %all-to-all-start.3 = ((bf16[32,7,8,128]{3,2,1,0:T(8,128)(2,1)}), bf16[32,7,8,128]{3,2,1,0:T(8,128)(2,1)S(1)}, u32[]{:S(2)}, u32[]{:S(2)}) async-start(bf16[32,7,8,128]{3,2,1,0:T(8,128)(2,1)} %pack.1), calls=%async_computation.3 | async-start | bytes 917504 | tf_op jit(solution)/shard_map/all_to_all | solution.py:522
  75.5 0.0 copy-start.5
  75.5 0.0 copy-start.6
  75.5 0.0 copy-start.8
  75.5 0.0 copy-start.9
  75.5 3.0 %slots.1 = (f32[1024,128]{1,0:T(8,128)}, f32[1024,128]{1,0:T(8,128)}, f32[1024,128]{1,0:T(8,128)S(1)}) custom-call(bf16[8,23,8,128]{3,2,1,0:T(8,128)(2,1)S(1)} %all_to_all.20.recv, f32[128,128]{1,0:T(8,128)S(1)} %get-tuple-element.28.hit, f32[1024,128]{1,0:T(8,128)S(1)} %bitcast.13, f32[1024,128]{1,0:T(8,128)S(1)} %bitcast.16, f32[1024,128]{1,0:T(8,128)} %bitcast.17), custom_call_target="tpu_custom_call" | custom-call | flops 262144000 | bytes 3145728 | tf_op jit(solution)/shard_map/slots/pallas_call | solution.py:413
  78.5 7.7 %all-to-all-done.3.recv = bf16[32,7,8,128]{3,2,1,0:T(8,128)(2,1)S(1)} async-done(((bf16[32,7,8,128]{3,2,1,0:T(8,128)(2,1)}), bf16[32,7,8,128]{3,2,1,0:T(8,128)(2,1)S(1)}, u32[]{:S(2)}, u32[]{:S(2)}) %all-to-all-start.3) | async-done | bytes 458784 | tf_op jit(solution)/shard_map/all_to_all | solution.py:522
  86.3 0.0 copy-done.5
  86.3 0.0 copy-done.6
  86.3 0.0 copy-done.8
  86.3 0.0 copy-done.9
  86.3 4.0 %last.1 = (f32[1024,128]{1,0:T(8,128)}, f32[13,512]{1,0:T(8,128)}, f32[512,256]{1,0:T(8,128)}, f32[256,128]{1,0:T(8,128)}, f32[13,512]{1,0:T(8,128)}, /*index=5*...) custom-call(s32[128,1]{1,0:T(8,128)S(1)} %copy.31.slot_table, ...), custom_call_target="tpu_custom_call" | custom-call | tf_op jit(solution)/shard_map/last/pallas_call | solution.py:503
Async XLA Ops:
  0.6 11.3 %copy-start.3 = (f32[512,256]{1,0:T(8,128)S(1)}, f32[512,256]{1,0:T(8,128)}, u32[]{:S(2)}) copy-start(f32[512,256]{1,0:T(8,128)} %refs_3_.1) | copy-start | bytes 1572868
  2.7 9.2 %copy-start.4 = (f32[256,128]{1,0:T(8,128)S(1)}, f32[256,128]{1,0:T(8,128)}, u32[]{:S(2)}) copy-start(f32[256,128]{1,0:T(8,128)} %refs_4_.1) | copy-start | bytes 393220
  2.7 9.2 %copy-start.10 = (bf16[13,4096]{1,0:T(8,128)(2,1)S(1)}, bf16[13,4096]{1,0:T(8,128)(2,1)}, u32[]{:S(2)}) copy-start(bf16[13,4096]{1,0:T(8,128)(2,1)} %x_in.1) | copy-start | bytes 319492
  2.7 20.0 %all-to-all-start = ((bf16[8,17,8,128]{3,2,1,0:T(8,128)(2,1)}), bf16[8,17,8,128]{3,2,1,0:T(8,128)(2,1)S(1)}, u32[]{:S(2)}, u32[]{:S(2)}) async-start(bf16[8,17,8,128]{3,2,1,0:T(8,128)(2,1)} %route.1), calls=%async_computation | async-start | bytes 557056 | tf_op jit(solution)/shard_map/all_to_all | solution.py:522
  11.9 0.8 copy-start.7
  24.6 25.2 %copy-start = (f32[128,8,128]{2,1,0:T(8,128)S(1)}, f32[128,8,128]{2,1,0:T(8,128)}, u32[]{:S(2)}) copy-start(f32[128,8,128]{2,1,0:T(8,128)} %param.18) | copy-start | bytes 1572868
  24.6 25.2 %copy-start.1 = (f32[128,8,128]{2,1,0:T(8,128)S(1)}, f32[128,8,128]{2,1,0:T(8,128)}, u32[]{:S(2)}) copy-start(f32[128,8,128]{2,1,0:T(8,128)} %param.19) | copy-start | bytes 1572868
  24.6 25.2 %copy-start.2 = (f32[128,8,128]{2,1,0:T(8,128)S(1)}, f32[128,8,128]{2,1,0:T(8,128)}, u32[]{:S(2)}) copy-start(f32[128,8,128]{2,1,0:T(8,128)} %param.20) | copy-start | bytes 1572868
  24.6 25.2 %all-to-all-start.1 = ((bf16[32,14,8,128]{3,2,1,0:T(8,128)(2,1)}), bf16[32,14,8,128]{3,2,1,0:T(8,128)(2,1)S(1)}, u32[]{:S(2)}, u32[]{:S(2)}) async-start(bf16[32,14,8,128]{3,2,1,0:T(8,128)(2,1)} %bucket.1), calls=%async_computation.1 | async-start | bytes 1835008 | tf_op jit(solution)/shard_map/all_to_all | solution.py:522
  34.2 0.7 copy-start.11
  69.8 16.5 %all-to-all-start.3 = ((bf16[32,7,8,128]{3,2,1,0:T(8,128)(2,1)}), bf16[32,7,8,128]{3,2,1,0:T(8,128)(2,1)S(1)}, u32[]{:S(2)}, u32[]{:S(2)}) async-start(bf16[32,7,8,128]{3,2,1,0:T(8,128)(2,1)} %pack.1), calls=%async_computation.3 | async-start | bytes 917504 | tf_op jit(solution)/shard_map/all_to_all | solution.py:522
  75.5 10.8 %copy-start.5 = (f32[256,128]{1,0:T(8,128)S(1)}, f32[256,128]{1,0:T(8,128)}, u32[]{:S(2)}) copy-start(f32[256,128]{1,0:T(8,128)} %refs_7_.1) | copy-start | bytes 393220
  75.5 10.8 %copy-start.6 = (f32[256,128]{1,0:T(8,128)S(1)}, f32[256,128]{1,0:T(8,128)}, u32[]{:S(2)}) copy-start(f32[256,128]{1,0:T(8,128)} %refs_10_.1) | copy-start | bytes 393220
  75.5 10.8 %copy-start.8 = (f32[13,512]{1,0:T(8,128)S(1)}, f32[13,512]{1,0:T(8,128)}, u32[]{:S(2)}) copy-start(f32[13,512]{1,0:T(8,128)} %refs_5_.1) | copy-start | bytes 79876
  75.5 10.8 %copy-start.9 = (f32[13,512]{1,0:T(8,128)S(1)}, f32[13,512]{1,0:T(8,128)}, u32[]{:S(2)}) copy-start(f32[13,512]{1,0:T(8,128)} %refs_8_.1) | copy-start | bytes 79876

commit v4 on v3

--- a/solution.py
+++ b/solution.py
@@ -90,17 +90,25 @@
     )(ids, block_slot, grads)
 
 
-def bucket_kernel(shards, who, recv, dense, out):
+def bucket_kernel(shards, who, recv, dense, out, rows_out, last_out, sem):
     groups = recv.shape[0]
     tiles = dense.shape[1]
     count = LANE
+    copies = [
+        pltpu.make_async_copy(
+            dense.at[:, 0 : tiles - 1], out.at[:, groups : groups + tiles - 1], sem.at[groups]
+        )
+    ]
+    copies[0].start()
     local_rows = jnp.zeros((shards, LANE), f32)
     for g in range(groups):
         tile = recv[g, count // SUB].astype(f32)
         place = tile[0:1].astype(jnp.int32)
         picker = (iota((shards * CAP, count), 0) == place).astype(f32).astype(bf16)
         rows = recv[g, 0 : count // SUB].astype(f32).reshape(count, LANE).astype(bf16)
-        out[:, g] = dot(picker, rows, 1, 0).reshape(shards, SUB, LANE).astype(bf16)
+        rows_out[:, g] = dot(picker, rows, 1, 0).reshape(shards, SUB, LANE).astype(bf16)
+        copies.append(pltpu.make_async_copy(rows_out.at[:, g], out.at[:, g], sem.at[g]))
+        copies[-1].start()
         owner = place >> log_two(CAP)
         lane = (place & (CAP - 1)) + g * CAP + who[2] * (LANE // 2)
         local = jnp.where(iota((shards, count), 0) == owner, tile[1:2], 0.0).astype(bf16)
@@ -108,10 +116,15 @@
         local_rows += dot(local, spot, 1, 1)
     sub = subs()
     for s in range(shards):
-        out[s, groups : groups + tiles - 1] = dense[s, 0 : tiles - 1]
         tile = dense[s, tiles - 1].astype(f32)
         tile = jnp.where(sub == meta_row(s), local_rows[s : s + 1], tile)
-        out[s, groups + tiles - 1] = tile.astype(bf16)
+        last_out[s] = tile.astype(bf16)
+    copies.append(
+        pltpu.make_async_copy(last_out, out.at[:, groups + tiles - 1], sem.at[groups + 1])
+    )
+    copies[-1].start()
+    for c in copies:
+        c.wait()
 
 
 def meta_row(s):
@@ -120,11 +133,17 @@
 
 def bucketed(who, recv, dense):
     shards, tiles = dense.shape[:2]
+    groups = recv.shape[0]
     return pl.pallas_call(
         functools.partial(bucket_kernel, shards),
-        out_shape=jax.ShapeDtypeStruct((shards, recv.shape[0] + tiles, SUB, LANE), bf16),
+        out_shape=jax.ShapeDtypeStruct((shards, groups + tiles, SUB, LANE), bf16),
         in_specs=[SMEM, VMEM, VMEM],
-        out_specs=VMEM,
+        out_specs=HBM,
+        scratch_shapes=[
+            pltpu.VMEM((shards, groups, SUB, LANE), bf16),
+            pltpu.VMEM((shards, SUB, LANE), bf16),
+            pltpu.SemaphoreType.DMA((groups + 2,)),
+        ],
         compiler_params=LIMIT,
         name="bucket",
     )(who, recv, dense)
@@ -259,21 +278,24 @@
 def lamb_step(weight, first_in, second_in, gradient):
     first_out = beta_one * first_in + (1.0 - beta_one) * gradient
     second_out = beta_two * second_in + (1.0 - beta_two) * gradient * gradient
-    update = (
-        first_out / corr_first / (jnp.sqrt(second_out / corr_second) + adam_eps)
-        + decay_rate * weight
-    )
+    update = (first_out * (1.0 / corr_first)) / (
+        jnp.sqrt(second_out * (1.0 / corr_second)) + adam_eps
+    ) + decay_rate * weight
     return update, first_out, second_out
 
 
-def split_rows(rows):
-    tile = jnp.zeros((SUB, LANE), f32)
-    sub = subs()
-    for i, row in enumerate(rows):
-        high = row.astype(bf16).astype(f32)
-        tile = jnp.where(sub == 2 * i, high, tile)
-        tile = jnp.where(sub == 2 * i + 1, row - high, tile)
-    return tile.astype(bf16)
+def with_sums(tile, piece, rows):
+    row = (subs() - 2 * (piece % 4) - 2) & (SUB - 1)
+    for i, value in enumerate(rows):
+        high = value.astype(bf16).astype(f32)
+        tile = jnp.where(row == 2 * i, high, tile)
+        tile = jnp.where(row == 2 * i + 1, value - high, tile)
+    return tile
+
+
+def sums_in(tile, piece):
+    row = ((subs() - 2 * (piece % 4) - 2) & (SUB - 1)) // 2
+    return [jnp.sum(jnp.where(row == i, tile, 0.0), axis=0, keepdims=True) for i in range(2)]
 
 
 def table_hot(slot_table):
@@ -310,15 +332,15 @@
     for v in (weight, update):
         row = jnp.sum(v * v, axis=1, keepdims=True)
         sums.append(jnp.sum(jnp.where(hot, row, 0.0), axis=0, keepdims=True))
-    both = split_rows(sums)
     dense = recv[0, groups:].astype(f32)
     for s in range(1, shards):
         dense = dense + recv[s, groups:].astype(f32)
-    dense = dense.astype(bf16)
+    mixed = with_sums(dense[tiles - 1], who[1], sums).astype(bf16)
+    dense = dense[: tiles - 1].astype(bf16)
     for g in range(groups):
         out[g, 0 : blocks // SUB] = sent
-        out[g, blocks // SUB : blocks // SUB + tiles] = dense
-        out[g, blocks // SUB + tiles] = both
+        out[g, blocks // SUB : blocks // SUB + tiles - 1] = dense
+        out[g, blocks // SUB + tiles - 1] = mixed
 
 
 def owned(who, slot_table, recv, table, first, second, groups, tiles):
@@ -326,7 +348,7 @@
     return pl.pallas_call(
         functools.partial(own_kernel, tiles),
         out_shape=(
-            jax.ShapeDtypeStruct((groups, blocks // SUB + tiles + 1, SUB, LANE), bf16),
+            jax.ShapeDtypeStruct((groups, blocks // SUB + tiles, SUB, LANE), bf16),
             jax.ShapeDtypeStruct((blocks, LANE), f32),
         ),
         in_specs=[SMEM] + [VMEM] * 5,
@@ -336,29 +358,29 @@
     )(who, slot_table, recv, table, first, second)
 
 
-def pack_kernel(tiles, recv, out):
+def pack_kernel(tiles, who, recv, out):
     groups = recv.shape[0]
-    start = recv.shape[1] - tiles - 1
+    start = recv.shape[1] - tiles
     lines = recv[0, start:].astype(f32)
     for g in range(1, groups):
         lines = lines + recv[g, start:].astype(f32)
-    dense = lines[0:tiles].astype(bf16)
-    both = lines[tiles]
-    both = split_rows((both[0:1] + both[1:2], both[2:3] + both[3:4]))
+    dense = lines[: tiles - 1].astype(bf16)
+    mixed = lines[tiles - 1]
+    mixed = with_sums(mixed, who[1], sums_in(mixed, who[1])).astype(bf16)
     for s in range(out.shape[0]):
-        out[s, 0:tiles] = dense
-        out[s, tiles] = both
-
-
-def packed(recv, shards, tiles):
+        out[s, 0 : tiles - 1] = dense
+        out[s, tiles - 1] = mixed
+
+
+def packed(who, recv, shards, tiles):
     return pl.pallas_call(
         functools.partial(pack_kernel, tiles),
-        out_shape=jax.ShapeDtypeStruct((shards, tiles + 1, SUB, LANE), bf16),
-        in_specs=[VMEM],
+        out_shape=jax.ShapeDtypeStruct((shards, tiles, SUB, LANE), bf16),
+        in_specs=[SMEM, VMEM],
         out_specs=VMEM,
         compiler_params=LIMIT,
         name="pack",
-    )(recv)
+    )(who, recv)
 
 
 def slots_kernel(
@@ -438,19 +460,24 @@
     held, made, (g_one, g_two, g_three, sem, out_sem) = scratch[:11], scratch[11:21], scratch[21:]
     arrive = [pltpu.make_async_copy(a, b, sem.at[i]) for i, (a, b) in enumerate(zip(ins, held))]
     leave = [pltpu.make_async_copy(a, b, out_sem.at[i]) for i, (a, b) in enumerate(zip(made, outs))]
-    for i in (3, 6, 9, 0, 1, 4, 7, 10, 2, 5, 8):
+    for i in (0, 1, 3, 6, 9, 4, 7, 10, 2, 5, 8):
         arrive[i].start()
-    shards = recv.shape[0]
-    tiles = recv.shape[1] - 1
-    both = recv[0, tiles].astype(f32)
-    for s in range(1, shards):
-        both = both + recv[s, tiles].astype(f32)
-    weight_sq = both[0:1] + both[1:2]
-    update_sq = both[2:3] + both[3:4]
+    shards, tiles = recv.shape[:2]
+    pieces = [sum(recv[s, tiles - 1].astype(f32) for s in range(a, shards, 4)) for a in range(4)]
+    pieces = [sums_in(p, a) for a, p in enumerate(pieces)]
+    weight_sq = sum(p[0] for p in pieces)
+    update_sq = sum(p[1] for p in pieces)
     ratio = learn_rate * (jnp.sqrt(weight_sq) / (jnp.sqrt(update_sq) + ratio_eps))
     ratio = jnp.sum(jnp.where(table_hot(slot_table), ratio, 0.0), axis=1, keepdims=True)
     blocks = slot_table.shape[0]
     groups = ins[0].shape[0] // blocks
+    arrive[0].wait()
+    arrive[1].wait()
+    table, update = held[:2]
+    for g in range(groups):
+        column = pl.ds(g, blocks, stride=groups)
+        made[0][column, :] = table[column, :] - ratio * update[column, :]
+    leave[0].start()
     pair = subs() // 2
     rows_two = g_two.shape[0] // shards
     rows_three = g_three.shape[0] // shards
@@ -484,13 +511,6 @@
             leave[i].start()
 
     dense(1, g_two)
-    arrive[0].wait()
-    arrive[1].wait()
-    table, update = held[:2]
-    for g in range(groups):
-        column = pl.ds(g, blocks, stride=groups)
-        made[0][column, :] = table[column, :] - ratio * update[column, :]
-    leave[0].start()
     dense(2, g_three)
     dense(0, g_one)
     for c in leave:
@@ -559,7 +579,7 @@
     rows = flat(table), flat(table_first), flat(table_second)
     mine, hit = owned(who, slot_column, recv, *rows, groups, tiles)
     whole = exchange(mine, "grp")
-    spread = exchange(packed(whole, shards, tiles), SHARD)
+    spread = exchange(packed(who, whole, shards, tiles), SHARD)
     new_first, new_second, update = slots(whole, hit, *rows)
     weights = (
         w_one,

time: 91 us -> 90.3 us (level)
  no operation moved by 1% of the time
where the time goes in v4:
time: 90.3 us; the launch traced here: 89.7 us
  starting transfers between devices  24.1 us (27%)
  waiting for transfers between devices  22.6 us (25%)
  Pallas kernels  22.5 us (25%)
  blocking collectives  18 us (20%)
  local copies, waits for them, and re-layouts  1.48 us (2%)
  between operations  0.96 us (1%)
    all_to_all x3, starting transfers between devices, exchange(): return lax.all_to_all(value, axis, split_axis=0, concat_axis=0, tiled=True)  24.1 us
    all_to_all x3, waiting for transfers between devices, exchange(): return lax.all_to_all(value, axis, split_axis=0, concat_axis=0, tiled=True)  22.6 us
    all_to_all x1, blocking collectives, exchange(): return lax.all_to_all(value, axis, split_axis=0, concat_axis=0, tiled=True)  18 us
    pallas_call x1, Pallas kernels, tower(): pl.pallas_call(functools.partial(tower_kernel, shards, parts), out_shape=...  9.5 us
    pallas_call x1, Pallas kernels, last(): pl.pallas_call(last_kernel, out_shape=tuple((jax.ShapeDtypeStruct(a.shape...  3.85 us
    pallas_call x1, Pallas kernels, slots(): pl.pallas_call(slots_kernel, out_shape=(shape,) * 3, in_specs=[VMEM] * 2...  2.97 us
    pallas_call x1, Pallas kernels, routed(): pl.pallas_call(functools.partial(route_kernel, shards, blocks, groups), o...  2.08 us
  transfers between devices with their start and end apart: 3, of which 3 were waited for; matrix products, arithmetic and copies ran while one was open for 0% of the time, Pallas kernels for 14%

profile of v4, /device:TPU:1, one launch (start us, length us, event | category | flops | bytes accessed | tf_op | source)
XLA Modules:
  0.0 89.7 jit_solution(16392037541904090479)
XLA Ops:
  0.6 0.0 copy-start.3
  0.7 2.1 %route.1 = bf16[8,17,8,128]{3,2,1,0:T(8,128)(2,1)} custom-call(s32[1,128]{1,0:T(1,128)} %ids.1, s32[32,128]{1,0:T(8,128)} %bitcast.20, bf16[1024,128]{1,0:T(8,128)(2,1)} %bitcast.19), custom_call_target="tpu_custom_call" | custom-call | tf_op jit(solution)/shard_map/route/pallas_call | solution.py:83
  2.7 0.0 copy-start.4
  2.7 0.0 copy-start.10
  2.7 9.1 %all-to-all-start = ((bf16[8,17,8,128]{3,2,1,0:T(8,128)(2,1)}), bf16[8,17,8,128]{3,2,1,0:T(8,128)(2,1)S(1)}, u32[]{:S(2)}, u32[]{:S(2)}) async-start(bf16[8,17,8,128]{3,2,1,0:T(8,128)(2,1)} %route.1), calls=%async_computation | async-start | bytes 557056 | tf_op jit(solution)/shard_map/all_to_all | solution.py:542
  11.9 0.0 copy-start.7
  11.9 0.1 pad_add_fusion.who
  12.0 0.0 copy-done.3
  12.0 0.0 copy-done.4
  12.0 0.0 copy-done.10
  12.0 0.7 copy-done.7
  12.6 9.5 %tower.1.dense = bf16[32,6,8,128]{3,2,1,0:T(8,128)(2,1)S(1)} custom-call(bf16[13,4096]{1,0:T(8,128)(2,1)S(1)} %copy-done.10, bf16[4096,128]{1,0:T(8,128)(2,1)} %cot_in.1, f32[13,512]{1,0:T(8,128)S(1)} %copy-done.7, f32[512,256]{1,0:T(8,128)S(1)} %copy-done.3, f32[256,128]{1,0:T(8,128)S(1)} %copy-done.4), custom_call_target="tpu_custom_call" | custom-call | flops 3867148288 | bytes 2097152 | tf_op jit(solution)/shard_map/tower/pallas_call | solution.py:249
  22.1 0.6 all-to-all-done.recv
  22.8 1.7 %bucket.1 = bf16[32,14,8,128]{3,2,1,0:T(8,128)(2,1)} custom-call(s32[3]{0:T(128)S(1)} %pad_add_fusion.who, bf16[8,17,8,128]{3,2,1,0:T(8,128)(2,1)S(1)} %all-to-all-done.recv, bf16[32,6,8,128]{3,2,1,0:T(8,128)(2,1)S(1)} %tower.1.dense), custom_call_target="tpu_custom_call" | custom-call | tf_op jit(solution)/shard_map/bucket/pallas_call | solution.py:137
  24.5 0.0 copy-start
  24.5 0.0 copy-start.1
  24.5 0.0 copy-start.2
  24.5 9.5 %all-to-all-start.1 = ((bf16[32,14,8,128]{3,2,1,0:T(8,128)(2,1)}), bf16[32,14,8,128]{3,2,1,0:T(8,128)(2,1)S(1)}, u32[]{:S(2)}, u32[]{:S(2)}) async-start(bf16[32,14,8,128]{3,2,1,0:T(8,128)(2,1)} %bucket.1), calls=%async_computation.1 | async-start | bytes 1835008 | tf_op jit(solution)/shard_map/all_to_all | solution.py:542
  34.1 0.0 copy-start.11
  34.1 0.6 copy-done.11
  34.7 0.1 copy.31.slot_table
  34.8 14.9 %all-to-all-done.1.recv = bf16[32,14,8,128]{3,2,1,0:T(8,128)(2,1)S(1)} async-done(((bf16[32,14,8,128]{3,2,1,0:T(8,128)(2,1)}), bf16[32,14,8,128]{3,2,1,0:T(8,128)(2,1)S(1)}, u32[]{:S(2)}, u32[]{:S(2)}) %all-to-all-start.1) | async-done | bytes 917536 | tf_op jit(solution)/shard_map/all_to_all | solution.py:542
  49.7 0.0 copy-done
  49.7 0.0 copy-done.1
  49.7 0.0 copy-done.2
  49.7 1.1 %own.1 = (bf16[8,22,8,128]{3,2,1,0:T(8,128)(2,1)S(1)}, f32[128,128]{1,0:T(8,128)S(1)}) custom-call(s32[3]{0:T(128)S(1)} %pad_add_fusion.who, s32[128,1]{1,0:T(8,128)S(1)} %copy.31.slot_table, bf16[32,14,8,128]{3,2,1,0:T(8,128)(2,1)S(1)} %all-to-all-done.1.recv, f32[1024,128]{1,0:T(8,128)S(1)} %bitcast.12, f32[1024,128]{1,0:T(8,128)S(1)} %bitcast.15, ...), custom_call_target="tpu_custom_call" | custom-call | tf_op jit(solution)/shard_map/own/pallas_call | solution.py:348
  50.8 18.0 %all_to_all.20.recv = bf16[8,22,8,128]{3,2,1,0:T(8,128)(2,1)S(1)} all-to-all(bf16[8,22,8,128]{3,2,1,0:T(8,128)(2,1)S(1)} %get-tuple-element.27), channel_id=1, replica_groups=mesh['grp'=8,'shard_0'=4,'shard_1'=4,'shard_2'=2] {'grp'}, dimensions={0} | all-to-all | bytes 720896 | tf_op jit(solution)/shard_map/all_to_all | solution.py:542
  68.7 1.3 %pack.1 = bf16[32,6,8,128]{3,2,1,0:T(8,128)(2,1)} custom-call(s32[3]{0:T(128)S(1)} %pad_add_fusion.who, bf16[8,22,8,128]{3,2,1,0:T(8,128)(2,1)S(1)} %all_to_all.20.recv), custom_call_target="tpu_custom_call" | custom-call | tf_op jit(solution)/shard_map/pack/pallas_call | solution.py:376
  70.1 5.5 %all-to-all-start.3 = ((bf16[32,6,8,128]{3,2,1,0:T(8,128)(2,1)}), bf16[32,6,8,128]{3,2,1,0:T(8,128)(2,1)S(1)}, u32[]{:S(2)}, u32[]{:S(2)}) async-start(bf16[32,6,8,128]{3,2,1,0:T(8,128)(2,1)} %pack.1), calls=%async_computation.3 | async-start | bytes 786432 | tf_op jit(solution)/shard_map/all_to_all | solution.py:542
  75.5 0.0 copy-start.5
  75.6 0.0 copy-start.6
  75.6 0.0 copy-start.8
  75.6 0.0 copy-start.9
  75.6 3.0 %slots.1 = (f32[1024,128]{1,0:T(8,128)}, f32[1024,128]{1,0:T(8,128)}, f32[1024,128]{1,0:T(8,128)S(1)}) custom-call(bf16[8,22,8,128]{3,2,1,0:T(8,128)(2,1)S(1)} %all_to_all.20.recv, f32[128,128]{1,0:T(8,128)S(1)} %get-tuple-element.28.hit, f32[1024,128]{1,0:T(8,128)S(1)} %bitcast.13, f32[1024,128]{1,0:T(8,128)S(1)} %bitcast.16, f32[1024,128]{1,0:T(8,128)} %bitcast.17), custom_call_target="tpu_custom_call" | custom-call | flops 262144000 | bytes 3145728 | tf_op jit(solution)/shard_map/slots/pallas_call | solution.py:435
  78.6 7.1 %all-to-all-done.3.recv = bf16[32,6,8,128]{3,2,1,0:T(8,128)(2,1)S(1)} async-done(((bf16[32,6,8,128]{3,2,1,0:T(8,128)(2,1)}), bf16[32,6,8,128]{3,2,1,0:T(8,128)(2,1)S(1)}, u32[]{:S(2)}, u32[]{:S(2)}) %all-to-all-start.3) | async-done | bytes 393248 | tf_op jit(solution)/shard_map/all_to_all | solution.py:542
  85.7 0.0 copy-done.5
  85.7 0.0 copy-done.6
  85.7 0.0 copy-done.8
  85.7 0.0 copy-done.9
  85.7 3.9 %last.1 = (f32[1024,128]{1,0:T(8,128)}, f32[13,512]{1,0:T(8,128)}, f32[512,256]{1,0:T(8,128)}, f32[256,128]{1,0:T(8,128)}, f32[13,512]{1,0:T(8,128)}, /*index=5*...) custom-call(s32[128,1]{1,0:T(8,128)S(1)} %copy.31.slot_table, ...), custom_call_target="tpu_custom_call" | custom-call | tf_op jit(solution)/shard_map/last/pallas_call | solution.py:523
Async XLA Ops:
  0.6 11.3 %copy-start.3 = (f32[512,256]{1,0:T(8,128)S(1)}, f32[512,256]{1,0:T(8,128)}, u32[]{:S(2)}) copy-start(f32[512,256]{1,0:T(8,128)} %refs_3_.1) | copy-start | bytes 1572868
  2.7 9.2 %copy-start.4 = (f32[256,128]{1,0:T(8,128)S(1)}, f32[256,128]{1,0:T(8,128)}, u32[]{:S(2)}) copy-start(f32[256,128]{1,0:T(8,128)} %refs_4_.1) | copy-start | bytes 393220
  2.7 9.2 %copy-start.10 = (bf16[13,4096]{1,0:T(8,128)(2,1)S(1)}, bf16[13,4096]{1,0:T(8,128)(2,1)}, u32[]{:S(2)}) copy-start(bf16[13,4096]{1,0:T(8,128)(2,1)} %x_in.1) | copy-start | bytes 319492
  2.7 20.0 %all-to-all-start = ((bf16[8,17,8,128]{3,2,1,0:T(8,128)(2,1)}), bf16[8,17,8,128]{3,2,1,0:T(8,128)(2,1)S(1)}, u32[]{:S(2)}, u32[]{:S(2)}) async-start(bf16[8,17,8,128]{3,2,1,0:T(8,128)(2,1)} %route.1), calls=%async_computation | async-start | bytes 557056 | tf_op jit(solution)/shard_map/all_to_all | solution.py:542
  11.9 0.8 copy-start.7
  24.5 25.2 %copy-start = (f32[128,8,128]{2,1,0:T(8,128)S(1)}, f32[128,8,128]{2,1,0:T(8,128)}, u32[]{:S(2)}) copy-start(f32[128,8,128]{2,1,0:T(8,128)} %param.18) | copy-start | bytes 1572868
  24.5 25.2 %copy-start.1 = (f32[128,8,128]{2,1,0:T(8,128)S(1)}, f32[128,8,128]{2,1,0:T(8,128)}, u32[]{:S(2)}) copy-start(f32[128,8,128]{2,1,0:T(8,128)} %param.19) | copy-start | bytes 1572868
  24.5 25.2 %copy-start.2 = (f32[128,8,128]{2,1,0:T(8,128)S(1)}, f32[128,8,128]{2,1,0:T(8,128)}, u32[]{:S(2)}) copy-start(f32[128,8,128]{2,1,0:T(8,128)} %param.20) | copy-start | bytes 1572868
  24.5 25.2 %all-to-all-start.1 = ((bf16[32,14,8,128]{3,2,1,0:T(8,128)(2,1)}), bf16[32,14,8,128]{3,2,1,0:T(8,128)(2,1)S(1)}, u32[]{:S(2)}, u32[]{:S(2)}) async-start(bf16[32,14,8,128]{3,2,1,0:T(8,128)(2,1)} %bucket.1), calls=%async_computation.1 | async-start | bytes 1835008 | tf_op jit(solution)/shard_map/all_to_all | solution.py:542
  34.1 0.7 copy-start.11
  70.1 15.6 %all-to-all-start.3 = ((bf16[32,6,8,128]{3,2,1,0:T(8,128)(2,1)}), bf16[32,6,8,128]{3,2,1,0:T(8,128)(2,1)S(1)}, u32[]{:S(2)}, u32[]{:S(2)}) async-start(bf16[32,6,8,128]{3,2,1,0:T(8,128)(2,1)} %pack.1), calls=%async_computation.3 | async-start | bytes 786432 | tf_op jit(solution)/shard_map/all_to_all | solution.py:542
  75.5 10.1 %copy-start.5 = (f32[256,128]{1,0:T(8,128)S(1)}, f32[256,128]{1,0:T(8,128)}, u32[]{:S(2)}) copy-start(f32[256,128]{1,0:T(8,128)} %refs_7_.1) | copy-start | bytes 393220
  75.6 10.1 %copy-start.6 = (f32[256,128]{1,0:T(8,128)S(1)}, f32[256,128]{1,0:T(8,128)}, u32[]{:S(2)}) copy-start(f32[256,128]{1,0:T(8,128)} %refs_10_.1) | copy-start | bytes 393220
  75.6 10.1 %copy-start.8 = (f32[13,512]{1,0:T(8,128)S(1)}, f32[13,512]{1,0:T(8,128)}, u32[]{:S(2)}) copy-start(f32[13,512]{1,0:T(8,128)} %refs_5_.1) | copy-start | bytes 79876
  75.6 10.1 %copy-start.9 = (f32[13,512]{1,0:T(8,128)S(1)}, f32[13,512]{1,0:T(8,128)}, u32[]{:S(2)}) copy-start(f32[13,512]{1,0:T(8,128)} %refs_8_.1) | copy-start | bytes 79876

commit v5 on v4

--- a/solution.py
+++ b/solution.py
@@ -13,6 +13,7 @@
 GRP_SHARD = ("grp", "shard_0", "shard_1", "shard_2")
 SUB = 8
 LANE = 128
+META_ROW = 2
 
 beta_one = 0.9
 beta_two = 0.999
@@ -40,6 +41,10 @@
 
 def subs():
     return iota((SUB, LANE), 0)
+
+
+def turned(tile, rows):
+    return pltpu.roll(tile, rows % SUB, 0) if rows % SUB else tile
 
 
 def dot(a, b, ca, cb):
@@ -90,7 +95,7 @@
     )(ids, block_slot, grads)
 
 
-def bucket_kernel(shards, who, recv, dense, out, rows_out, last_out, sem):
+def bucket_kernel(shards, offset, recv, dense, out, rows_out, last_out, sem):
     groups = recv.shape[0]
     tiles = dense.shape[1]
     count = LANE
@@ -110,14 +115,14 @@
         copies.append(pltpu.make_async_copy(rows_out.at[:, g], out.at[:, g], sem.at[g]))
         copies[-1].start()
         owner = place >> log_two(CAP)
-        lane = (place & (CAP - 1)) + g * CAP + who[2] * (LANE // 2)
+        lane = (place & (CAP - 1)) + g * CAP + offset[...]
         local = jnp.where(iota((shards, count), 0) == owner, tile[1:2], 0.0).astype(bf16)
         spot = (iota((LANE, count), 0) == lane).astype(f32).astype(bf16)
         local_rows += dot(local, spot, 1, 1)
     sub = subs()
     for s in range(shards):
         tile = dense[s, tiles - 1].astype(f32)
-        tile = jnp.where(sub == meta_row(s), local_rows[s : s + 1], tile)
+        tile = jnp.where(sub == META_ROW, local_rows[s : s + 1], tile)
         last_out[s] = tile.astype(bf16)
     copies.append(
         pltpu.make_async_copy(last_out, out.at[:, groups + tiles - 1], sem.at[groups + 1])
@@ -127,17 +132,13 @@
         c.wait()
 
 
-def meta_row(s):
-    return (2 * (s % 4) + 2) % SUB
-
-
-def bucketed(who, recv, dense):
+def bucketed(offset, recv, dense):
     shards, tiles = dense.shape[:2]
     groups = recv.shape[0]
     return pl.pallas_call(
         functools.partial(bucket_kernel, shards),
         out_shape=jax.ShapeDtypeStruct((shards, groups + tiles, SUB, LANE), bf16),
-        in_specs=[SMEM, VMEM, VMEM],
+        in_specs=[VMEM] * 3,
         out_specs=HBM,
         scratch_shapes=[
             pltpu.VMEM((shards, groups, SUB, LANE), bf16),
@@ -146,7 +147,7 @@
         ],
         compiler_params=LIMIT,
         name="bucket",
-    )(who, recv, dense)
+    )(offset, recv, dense)
 
 
 def act(half):
@@ -238,7 +239,8 @@
             out[s, at] = g_three[s * rows_three + r : s * rows_three + r + SUB, :].astype(bf16)
             at += 1
         c, r = s // 4 // 2, s // 4 % 2
-        out[s, at] = g_one[r * SUB : (r + 1) * SUB, c * LANE : (c + 1) * LANE].astype(bf16)
+        tile = g_one[r * SUB : (r + 1) * SUB, c * LANE : (c + 1) * LANE]
+        out[s, at] = turned(tile, -2 * (s % 4)).astype(bf16)
 
 
 def tower(x, cot, w_one, w_two, w_three, shards, tiles, parts=4):
@@ -284,36 +286,33 @@
     return update, first_out, second_out
 
 
-def with_sums(tile, piece, rows):
-    row = (subs() - 2 * (piece % 4) - 2) & (SUB - 1)
+def with_sums(tile, rows):
+    sub = subs()
     for i, value in enumerate(rows):
         high = value.astype(bf16).astype(f32)
-        tile = jnp.where(row == 2 * i, high, tile)
-        tile = jnp.where(row == 2 * i + 1, value - high, tile)
+        tile = jnp.where(sub == 2 * i + 2, high, tile)
+        tile = jnp.where(sub == 2 * i + 3, value - high, tile)
     return tile
 
 
-def sums_in(tile, piece):
-    row = ((subs() - 2 * (piece % 4) - 2) & (SUB - 1)) // 2
-    return [jnp.sum(jnp.where(row == i, tile, 0.0), axis=0, keepdims=True) for i in range(2)]
+def sums_in(tile):
+    return [tile[i : i + 1] + tile[i + 1 : i + 2] for i in (2, 4)]
 
 
 def table_hot(slot_table):
     return slot_table[...] == iota((slot_table.shape[0], LANE), 1)
 
 
-def own_kernel(tiles, who, slot_table, recv, table, first, second, out, hit_out):
+def own_kernel(tiles, slot_table, recv, table, first, second, out, hit_out):
     shards = recv.shape[0]
     groups = out.shape[0]
     blocks = slot_table.shape[0]
-    sub = subs()
-    meta = meta_row(who[1])
     total = jnp.zeros((blocks, LANE), f32)
     hits = jnp.zeros((blocks, LANE), f32)
     slot = iota((blocks, LANE), 0) + 1
     for s in range(0, shards, 2):
         tile = recv[s, groups + tiles - 1].astype(f32) + recv[s + 1, groups + tiles - 1].astype(f32)
-        place = jnp.sum(jnp.where(sub == meta, tile, 0.0), axis=0, keepdims=True)
+        place = tile[META_ROW : META_ROW + 1]
         match = (slot == place.astype(jnp.int32)).astype(f32)
         rows = recv[s : s + 2, 0:groups].astype(f32).reshape(LANE, LANE).astype(bf16)
         total += dot(match.astype(bf16), rows, 1, 0)
@@ -321,10 +320,9 @@
     hits = dot(hits.astype(bf16), jnp.ones((LANE, LANE), bf16), 1, 0)
     hit_out[...] = hits
     sent = total.reshape(blocks // SUB, SUB, LANE).astype(bf16)
-    column = pl.ds(who[0], blocks, stride=groups)
-    weight = table[column, :]
+    weight = table[...]
     update, unused, unused_too = lamb_step(
-        weight, first[column, :], second[column, :], sent.astype(f32).reshape(blocks, LANE)
+        weight, first[...], second[...], sent.astype(f32).reshape(blocks, LANE)
     )
     update = jnp.where(hits > 0.5, update, 0.0)
     hot = table_hot(slot_table)
@@ -335,7 +333,7 @@
     dense = recv[0, groups:].astype(f32)
     for s in range(1, shards):
         dense = dense + recv[s, groups:].astype(f32)
-    mixed = with_sums(dense[tiles - 1], who[1], sums).astype(bf16)
+    mixed = with_sums(dense[tiles - 1], sums).astype(bf16)
     dense = dense[: tiles - 1].astype(bf16)
     for g in range(groups):
         out[g, 0 : blocks // SUB] = sent
@@ -343,7 +341,7 @@
         out[g, blocks // SUB + tiles - 1] = mixed
 
 
-def owned(who, slot_table, recv, table, first, second, groups, tiles):
+def owned(slot_table, recv, table, first, second, groups, tiles):
     blocks = slot_table.shape[0]
     return pl.pallas_call(
         functools.partial(own_kernel, tiles),
@@ -351,14 +349,14 @@
             jax.ShapeDtypeStruct((groups, blocks // SUB + tiles, SUB, LANE), bf16),
             jax.ShapeDtypeStruct((blocks, LANE), f32),
         ),
-        in_specs=[SMEM] + [VMEM] * 5,
+        in_specs=[VMEM] * 5,
         out_specs=(VMEM,) * 2,
         compiler_params=LIMIT,
         name="own",
-    )(who, slot_table, recv, table, first, second)
-
-
-def pack_kernel(tiles, who, recv, out):
+    )(slot_table, recv, table, first, second)
+
+
+def pack_kernel(tiles, recv, out):
     groups = recv.shape[0]
     start = recv.shape[1] - tiles
     lines = recv[0, start:].astype(f32)
@@ -366,21 +364,21 @@
         lines = lines + recv[g, start:].astype(f32)
     dense = lines[: tiles - 1].astype(bf16)
     mixed = lines[tiles - 1]
-    mixed = with_sums(mixed, who[1], sums_in(mixed, who[1])).astype(bf16)
+    mixed = with_sums(mixed, sums_in(mixed)).astype(bf16)
     for s in range(out.shape[0]):
         out[s, 0 : tiles - 1] = dense
         out[s, tiles - 1] = mixed
 
 
-def packed(who, recv, shards, tiles):
+def packed(recv, shards, tiles):
     return pl.pallas_call(
         functools.partial(pack_kernel, tiles),
         out_shape=jax.ShapeDtypeStruct((shards, tiles, SUB, LANE), bf16),
-        in_specs=[SMEM, VMEM],
+        in_specs=[VMEM],
         out_specs=VMEM,
         compiler_params=LIMIT,
         name="pack",
-    )(who, recv)
+    )(recv)
 
 
 def slots_kernel(
@@ -463,10 +461,10 @@
     for i in (0, 1, 3, 6, 9, 4, 7, 10, 2, 5, 8):
         arrive[i].start()
     shards, tiles = recv.shape[:2]
-    pieces = [sum(recv[s, tiles - 1].astype(f32) for s in range(a, shards, 4)) for a in range(4)]
-    pieces = [sums_in(p, a) for a, p in enumerate(pieces)]
-    weight_sq = sum(p[0] for p in pieces)
-    update_sq = sum(p[1] for p in pieces)
+    pieces = recv[0, tiles - 1].astype(f32)
+    for s in range(1, shards):
+        pieces = pieces + recv[s, tiles - 1].astype(f32)
+    weight_sq, update_sq = sums_in(pieces)
     ratio = learn_rate * (jnp.sqrt(weight_sq) / (jnp.sqrt(update_sq) + ratio_eps))
     ratio = jnp.sum(jnp.where(table_hot(slot_table), ratio, 0.0), axis=1, keepdims=True)
     blocks = slot_table.shape[0]
@@ -496,7 +494,8 @@
     for k in range(shards // 4):
         tile = jnp.zeros((SUB, LANE), f32)
         for a in range(4):
-            tile = jnp.where(pair == a, recv[4 * k + a, tiles - 1].astype(f32), tile)
+            piece = turned(recv[4 * k + a, tiles - 1].astype(f32), 2 * a)
+            tile = jnp.where(pair == a, piece, tile)
         c, r = k // 2, k % 2
         g_one[r * SUB : (r + 1) * SUB, c * LANE : (c + 1) * LANE] = tile
 
@@ -566,8 +565,9 @@
     groups = lax.axis_size("grp")
     blocks = table.shape[0]
     tiles = (w_two.size + w_three.size) // (shards * SUB * LANE) + 1
-    who = jnp.stack([lax.axis_index("grp"), lax.axis_index(SHARD), lax.axis_index(SHARD[2])])
-    who = who.astype(jnp.int32)
+    group = lax.axis_index("grp")
+    offset = jnp.full((1, LANE), lax.axis_index(SHARD[2]) * (LANE // 2), jnp.int32)
+    column = lambda a: lax.dynamic_index_in_dim(a, group, 1, keepdims=False)
     flat = lambda a: a.reshape(-1, LANE)
     slot_column = slot_table[:, None]
 
@@ -575,11 +575,12 @@
         routed(touched, flat(block_slot), flat(emb_grads), shards, blocks, groups), "grp"
     )
     dense = tower(dense_x, dense_cot, w_one, w_two, w_three, shards, tiles)
-    recv = exchange(bucketed(who, recv, dense), SHARD)
+    recv = exchange(bucketed(offset, recv, dense), SHARD)
     rows = flat(table), flat(table_first), flat(table_second)
-    mine, hit = owned(who, slot_column, recv, *rows, groups, tiles)
+    columns = [column(a) for a in (table, table_first, table_second)]
+    mine, hit = owned(slot_column, recv, *columns, groups, tiles)
     whole = exchange(mine, "grp")
-    spread = exchange(packed(who, whole, shards, tiles), SHARD)
+    spread = exchange(packed(whole, shards, tiles), SHARD)
     new_first, new_second, update = slots(whole, hit, *rows)
     weights = (
         w_one,

time: 90.3 us -> 87.9 us (0.973)
  Pallas kernels: 22.5 us -> 20.9 us
    dynamic_slice x0 -> x2, local copies, waits for them, and re-layouts: none -> 1.19 us  [body(): column = lambda a: lax.dynamic_index_in_dim(a, group, 1, keepdims=False)]
  transfers between devices with their start and end apart: 3 -> 3, of which waited for: 3 -> 3; matrix products, arithmetic and copies ran while one was open for 0% -> 1% of each run, Pallas kernels for 14% -> 14%
where the time goes in v5:
time: 87.9 us; the launch traced here: 87.3 us
  starting transfers between devices  24.1 us (27%)
  waiting for transfers between devices  22.1 us (25%)
  Pallas kernels  20.9 us (24%)
  blocking collectives  17.3 us (20%)
  local copies, waits for them, and re-layouts  2.01 us (2%)
  between operations  0.98 us (1%)
    all_to_all x3, starting transfers between devices, exchange(): return lax.all_to_all(value, axis, split_axis=0, concat_axis=0, tiled=True)  24.1 us
    all_to_all x3, waiting for transfers between devices, exchange(): return lax.all_to_all(value, axis, split_axis=0, concat_axis=0, tiled=True)  22.1 us
    all_to_all x1, blocking collectives, exchange(): return lax.all_to_all(value, axis, split_axis=0, concat_axis=0, tiled=True)  17.3 us
    pallas_call x1, Pallas kernels, tower(): pl.pallas_call(functools.partial(tower_kernel, shards, parts), out_shape=...  9.54 us
    pallas_call x1, Pallas kernels, last(): pl.pallas_call(last_kernel, out_shape=tuple((jax.ShapeDtypeStruct(a.shape...  3.85 us
    pallas_call x1, Pallas kernels, slots(): pl.pallas_call(slots_kernel, out_shape=(shape,) * 3, in_specs=[VMEM] * 2...  2.97 us
    pallas_call x1, Pallas kernels, routed(): pl.pallas_call(functools.partial(route_kernel, shards, blocks, groups), o...  2.08 us
  transfers between devices with their start and end apart: 3, of which 3 were waited for; matrix products, arithmetic and copies ran while one was open for 1% of the time, Pallas kernels for 14%

profile of v5, /device:TPU:1, one launch (start us, length us, event | category | flops | bytes accessed | tf_op | source)
XLA Modules:
  0.0 87.3 jit_solution(8457273703081013585)
XLA Ops:
  0.6 0.0 copy-start.2
  0.7 2.1 %route.1 = bf16[8,17,8,128]{3,2,1,0:T(8,128)(2,1)} custom-call(s32[1,128]{1,0:T(1,128)} %ids.1, s32[32,128]{1,0:T(8,128)} %bitcast.20, bf16[1024,128]{1,0:T(8,128)(2,1)} %bitcast.19), custom_call_target="tpu_custom_call" | custom-call | tf_op jit(solution)/shard_map/route/pallas_call | solution.py:88
  2.7 0.0 copy-start.3
  2.7 0.0 copy-start.6
  2.7 0.0 copy-start.9
  2.7 9.1 %all-to-all-start = ((bf16[8,17,8,128]{3,2,1,0:T(8,128)(2,1)}), bf16[8,17,8,128]{3,2,1,0:T(8,128)(2,1)S(1)}, u32[]{:S(2)}, u32[]{:S(2)}) async-start(bf16[8,17,8,128]{3,2,1,0:T(8,128)(2,1)} %route.1), calls=%async_computation | async-start | bytes 557056 | tf_op jit(solution)/shard_map/all_to_all | solution.py:541
  11.9 0.0 copy-done.2
  11.9 0.0 copy-done.3
  11.9 0.0 copy-done.6
  11.9 0.0 copy-done.9
  11.9 9.5 %tower.1.dense = bf16[32,6,8,128]{3,2,1,0:T(8,128)(2,1)S(1)} custom-call(bf16[13,4096]{1,0:T(8,128)(2,1)S(1)} %copy-done.9, bf16[4096,128]{1,0:T(8,128)(2,1)} %cot_in.1, f32[13,512]{1,0:T(8,128)S(1)} %copy-done.6, f32[512,256]{1,0:T(8,128)S(1)} %copy-done.2, f32[256,128]{1,0:T(8,128)S(1)} %copy-done.3), custom_call_target="tpu_custom_call" | custom-call | flops 3867148288 | bytes 2097152 | tf_op jit(solution)/shard_map/tower/pallas_call | solution.py:251
  21.5 1.3 %all-to-all-done.recv = bf16[8,17,8,128]{3,2,1,0:T(8,128)(2,1)S(1)} async-done(((bf16[8,17,8,128]{3,2,1,0:T(8,128)(2,1)}), bf16[8,17,8,128]{3,2,1,0:T(8,128)(2,1)S(1)}, u32[]{:S(2)}, u32[]{:S(2)}) %all-to-all-start) | async-done | bytes 278560 | tf_op jit(solution)/shard_map/all_to_all | solution.py:541
  22.8 1.2 %bucket.1 = bf16[32,14,8,128]{3,2,1,0:T(8,128)(2,1)} custom-call(s32[1,128]{1,0:T(1,128)S(1)} %broadcast_in_dim.7.offset, bf16[8,17,8,128]{3,2,1,0:T(8,128)(2,1)S(1)} %all-to-all-done.recv, bf16[32,6,8,128]{3,2,1,0:T(8,128)(2,1)S(1)} %tower.1.dense), custom_call_target="tpu_custom_call" | custom-call | tf_op jit(solution)/shard_map/bucket/pallas_call | solution.py:138
  23.9 0.0 copy-start
  24.0 0.0 copy-start.1
  24.0 9.5 %all-to-all-start.1 = ((bf16[32,14,8,128]{3,2,1,0:T(8,128)(2,1)}), bf16[32,14,8,128]{3,2,1,0:T(8,128)(2,1)S(1)}, u32[]{:S(2)}, u32[]{:S(2)}) async-start(bf16[32,14,8,128]{3,2,1,0:T(8,128)(2,1)} %bucket.1), calls=%async_computation.1 | async-start | bytes 1835008 | tf_op jit(solution)/shard_map/all_to_all | solution.py:541
  33.5 0.0 copy-start.10
  33.5 0.6 copy-done.10
  34.2 0.1 copy.31.slot_table
  34.3 0.0 copy-done
  34.3 0.1 constant_dynamic-slice_fusion.2
  34.3 0.0 copy-done.1
  34.4 1.1 %constant_dynamic-slice_fusion = (f32[128,1,128]{2,1,0:T(1,128)S(1)}, f32[128,1,128]{2,1,0:T(1,128)S(1)}) fusion(f32[128,8,128]{2,1,0:T(8,128)} %param.20, s32[]{:T(128)S(6)} %select_n.6, f32[128,8,128]{2,1,0:T(8,128)S(1)} %copy-done.1), kind=kLoop, calls=%fused_computation | loop fusion | bytes 262148 | tf_op jit(solution)/shard_map/jit(dynamic_index_in_dim)/dynamic_slice | solution.py:570
  35.5 13.7 %all-to-all-done.1.recv = bf16[32,14,8,128]{3,2,1,0:T(8,128)(2,1)S(1)} async-done(((bf16[32,14,8,128]{3,2,1,0:T(8,128)(2,1)}), bf16[32,14,8,128]{3,2,1,0:T(8,128)(2,1)S(1)}, u32[]{:S(2)}, u32[]{:S(2)}) %all-to-all-start.1) | async-done | bytes 917536 | tf_op jit(solution)/shard_map/all_to_all | solution.py:541
  49.1 0.5 own.1
  49.6 17.3 %all_to_all.20.recv = bf16[8,22,8,128]{3,2,1,0:T(8,128)(2,1)S(1)} all-to-all(bf16[8,22,8,128]{3,2,1,0:T(8,128)(2,1)S(1)} %get-tuple-element.27), channel_id=1, replica_groups=mesh['grp'=8,'shard_0'=4,'shard_1'=4,'shard_2'=2] {'grp'}, dimensions={0} | all-to-all | bytes 720896 | tf_op jit(solution)/shard_map/all_to_all | solution.py:541
  66.9 0.8 pack.1
  67.7 5.5 %all-to-all-start.3 = ((bf16[32,6,8,128]{3,2,1,0:T(8,128)(2,1)}), bf16[32,6,8,128]{3,2,1,0:T(8,128)(2,1)S(1)}, u32[]{:S(2)}, u32[]{:S(2)}) async-start(bf16[32,6,8,128]{3,2,1,0:T(8,128)(2,1)} %pack.1), calls=%async_computation.3 | async-start | bytes 786432 | tf_op jit(solution)/shard_map/all_to_all | solution.py:541
  73.2 0.0 copy-start.4
  73.2 0.0 copy-start.5
  73.2 0.0 copy-start.7
  73.2 0.0 copy-start.8
  73.2 3.0 %slots.1 = (f32[1024,128]{1,0:T(8,128)}, f32[1024,128]{1,0:T(8,128)}, f32[1024,128]{1,0:T(8,128)S(1)}) custom-call(bf16[8,22,8,128]{3,2,1,0:T(8,128)(2,1)S(1)} %all_to_all.20.recv, f32[128,128]{1,0:T(8,128)S(1)} %get-tuple-element.28.hit, f32[1024,128]{1,0:T(8,128)S(1)} %bitcast.12, f32[1024,128]{1,0:T(8,128)S(1)} %bitcast.14, f32[1024,128]{1,0:T(8,128)} %bitcast.18), custom_call_target="tpu_custom_call" | custom-call | flops 262144000 | bytes 3145728 | tf_op jit(solution)/shard_map/slots/pallas_call | solution.py:433
  76.2 7.1 %all-to-all-done.3.recv = bf16[32,6,8,128]{3,2,1,0:T(8,128)(2,1)S(1)} async-done(((bf16[32,6,8,128]{3,2,1,0:T(8,128)(2,1)}), bf16[32,6,8,128]{3,2,1,0:T(8,128)(2,1)S(1)}, u32[]{:S(2)}, u32[]{:S(2)}) %all-to-all-start.3) | async-done | bytes 393248 | tf_op jit(solution)/shard_map/all_to_all | solution.py:541
  83.3 0.0 copy-done.4
  83.3 0.0 copy-done.5
  83.3 0.0 copy-done.7
  83.3 0.0 copy-done.8
  83.3 3.9 %last.1 = (f32[1024,128]{1,0:T(8,128)}, f32[13,512]{1,0:T(8,128)}, f32[512,256]{1,0:T(8,128)}, f32[256,128]{1,0:T(8,128)}, f32[13,512]{1,0:T(8,128)}, /*index=5*...) custom-call(s32[128,1]{1,0:T(8,128)S(1)} %copy.31.slot_table, ...), custom_call_target="tpu_custom_call" | custom-call | tf_op jit(solution)/shard_map/last/pallas_call | solution.py:522
  (1 shorter events, 0.0 us)
Async XLA Ops:
  0.6 11.2 %copy-start.2 = (f32[512,256]{1,0:T(8,128)S(1)}, f32[512,256]{1,0:T(8,128)}, u32[]{:S(2)}) copy-start(f32[512,256]{1,0:T(8,128)} %refs_3_.1) | copy-start | bytes 1572868
  2.7 9.1 %copy-start.3 = (f32[256,128]{1,0:T(8,128)S(1)}, f32[256,128]{1,0:T(8,128)}, u32[]{:S(2)}) copy-start(f32[256,128]{1,0:T(8,128)} %refs_4_.1) | copy-start | bytes 393220
  2.7 9.2 %copy-start.6 = (f32[13,512]{1,0:T(8,128)S(1)}, f32[13,512]{1,0:T(8,128)}, u32[]{:S(2)}) copy-start(f32[13,512]{1,0:T(8,128)} %refs_2_.1) | copy-start | bytes 79876
  2.7 9.2 %copy-start.9 = (bf16[13,4096]{1,0:T(8,128)(2,1)S(1)}, bf16[13,4096]{1,0:T(8,128)(2,1)}, u32[]{:S(2)}) copy-start(bf16[13,4096]{1,0:T(8,128)(2,1)} %x_in.1) | copy-start | bytes 319492
  2.7 20.0 %all-to-all-start = ((bf16[8,17,8,128]{3,2,1,0:T(8,128)(2,1)}), bf16[8,17,8,128]{3,2,1,0:T(8,128)(2,1)S(1)}, u32[]{:S(2)}, u32[]{:S(2)}) async-start(bf16[8,17,8,128]{3,2,1,0:T(8,128)(2,1)} %route.1), calls=%async_computation | async-start | bytes 557056 | tf_op jit(solution)/shard_map/all_to_all | solution.py:541
  23.9 10.3 %copy-start = (f32[128,8,128]{2,1,0:T(8,128)S(1)}, f32[128,8,128]{2,1,0:T(8,128)}, u32[]{:S(2)}) copy-start(f32[128,8,128]{2,1,0:T(8,128)} %param.18) | copy-start | bytes 1572868
  24.0 10.4 %copy-start.1 = (f32[128,8,128]{2,1,0:T(8,128)S(1)}, f32[128,8,128]{2,1,0:T(8,128)}, u32[]{:S(2)}) copy-start(f32[128,8,128]{2,1,0:T(8,128)} %param.19) | copy-start | bytes 1572868
  24.0 25.2 %all-to-all-start.1 = ((bf16[32,14,8,128]{3,2,1,0:T(8,128)(2,1)}), bf16[32,14,8,128]{3,2,1,0:T(8,128)(2,1)S(1)}, u32[]{:S(2)}, u32[]{:S(2)}) async-start(bf16[32,14,8,128]{3,2,1,0:T(8,128)(2,1)} %bucket.1), calls=%async_computation.1 | async-start | bytes 1835008 | tf_op jit(solution)/shard_map/all_to_all | solution.py:541
  33.5 0.7 copy-start.10
  67.7 15.6 %all-to-all-start.3 = ((bf16[32,6,8,128]{3,2,1,0:T(8,128)(2,1)}), bf16[32,6,8,128]{3,2,1,0:T(8,128)(2,1)S(1)}, u32[]{:S(2)}, u32[]{:S(2)}) async-start(bf16[32,6,8,128]{3,2,1,0:T(8,128)(2,1)} %pack.1), calls=%async_computation.3 | async-start | bytes 786432 | tf_op jit(solution)/shard_map/all_to_all | solution.py:541
  73.2 10.1 %copy-start.4 = (f32[256,128]{1,0:T(8,128)S(1)}, f32[256,128]{1,0:T(8,128)}, u32[]{:S(2)}) copy-start(f32[256,128]{1,0:T(8,128)} %refs_7_.1) | copy-start | bytes 393220
  73.2 10.1 %copy-start.5 = (f32[256,128]{1,0:T(8,128)S(1)}, f32[256,128]{1,0:T(8,128)}, u32[]{:S(2)}) copy-start(f32[256,128]{1,0:T(8,128)} %refs_10_.1) | copy-start | bytes 393220
  73.2 10.1 %copy-start.7 = (f32[13,512]{1,0:T(8,128)S(1)}, f32[13,512]{1,0:T(8,128)}, u32[]{:S(2)}) copy-start(f32[13,512]{1,0:T(8,128)} %refs_5_.1) | copy-start | bytes 79876
  73.2 10.1 %copy-start.8 = (f32[13,512]{1,0:T(8,128)S(1)}, f32[13,512]{1,0:T(8,128)}, u32[]{:S(2)}) copy-start(f32[13,512]{1,0:T(8,128)} %refs_8_.1) | copy-start | bytes 79876

commit v6 on v5

--- a/solution.py
+++ b/solution.py
@@ -55,12 +55,10 @@
     return n.bit_length() - 1
 
 
-def route_kernel(shards, blocks, groups, ids, block_slot, grads, out, wide):
+def route_kernel(shards, blocks, groups, ids, block_slot, grads_in, out_hbm, grads, wide, out, sem):
     count = ids.shape[1]
-    wide[...] = grads[...].astype(f32)
-    for g in range(groups):
-        rows = wide[pl.ds(g, count, stride=groups), :]
-        out[g, 0 : count // SUB] = rows.reshape(count // SUB, SUB, LANE).astype(bf16)
+    arrive = pltpu.make_async_copy(grads_in, grads, sem.at[groups])
+    arrive.start()
     table_rows = block_slot.shape[0]
     high = ids[...] >> log_two(LANE)
     low = ids[...] & (LANE - 1)
@@ -79,18 +77,33 @@
     sub = iota((SUB, count), 0)
     tile = jnp.where(sub == 0, owner * CAP + rank, jnp.where(sub == 1, local + 1.0, 0.0))
     tile = tile.astype(bf16)
+    arrive.wait()
+    wide[...] = grads[...].astype(f32)
+    leave = []
     for g in range(groups):
+        rows = wide[pl.ds(g, count, stride=groups), :]
+        out[g, 0 : count // SUB] = rows.reshape(count // SUB, SUB, LANE).astype(bf16)
         out[g, count // SUB] = tile
+        leave.append(pltpu.make_async_copy(out.at[g], out_hbm.at[g], sem.at[g]))
+        leave[-1].start()
+    for c in leave:
+        c.wait()
 
 
 def routed(ids, block_slot, grads, shards, blocks, groups):
     count = ids.shape[1]
+    shape = (groups, count // SUB + 1, SUB, LANE)
     return pl.pallas_call(
         functools.partial(route_kernel, shards, blocks, groups),
-        out_shape=jax.ShapeDtypeStruct((groups, count // SUB + 1, SUB, LANE), bf16),
-        in_specs=[VMEM] * 3,
-        out_specs=VMEM,
-        scratch_shapes=[pltpu.VMEM(grads.shape, f32)],
+        out_shape=jax.ShapeDtypeStruct(shape, bf16),
+        in_specs=[VMEM, VMEM, HBM],
+        out_specs=HBM,
+        scratch_shapes=[
+            pltpu.VMEM(grads.shape, bf16),
+            pltpu.VMEM(grads.shape, f32),
+            pltpu.VMEM(shape, bf16),
+            pltpu.SemaphoreType.DMA((groups + 1,)),
+        ],
         name="route",
     )(ids, block_slot, grads)
 
@@ -203,26 +216,36 @@
     w_two_t[...] = (0.5 * raw_two[...]).T.astype(bf16)
     copies[3].wait()
     w_three[...] = (0.5 * raw_three[...]).astype(bf16)
-    sums = None
-    for k in range(parts):
-        xs = x[:, k * step : (k + 1) * step]
-        hidden_one, slope_one = act(dot(w_one[...], xs, 0, 0))
-        hidden_two, slope_two = act(dot(w_two_t[...], hidden_one, 1, 0))
+    samples = lambda k: slice(k * step, (k + 1) * step)
+    first, second = {}, {}
+
+    def layer_one(k):
+        first[k] = act(dot(w_one[...], x[:, samples(k)], 0, 0))
+
+    def layer_two(k):
+        hidden, slope = act(dot(w_two_t[...], first[k][0], 1, 0))
         chunks[k].wait()
-        cots = cot[k * step : (k + 1) * step, :]
-        three = dot(hidden_two, cots, 1, 0)
-        back_two = (dot(w_three[...], cots, 1, 1) * slope_two).astype(bf16)
-        two = dot(hidden_one, back_two, 1, 1)
+        back = dot(w_three[...], cot[samples(k), :], 1, 1) * slope
+        second[k] = hidden, back.astype(bf16)
+
+    def add(k, total, value):
+        total[...] = value if k == 0 else total[...] + value
+
+    def gradients(k):
+        hidden_one, slope_one = first.pop(k)
+        hidden_two, back_two = second.pop(k)
+        add(k, g_three, dot(hidden_two, cot[samples(k), :], 1, 0))
+        add(k, g_two, dot(hidden_one, back_two, 1, 1))
         back_one = (dot(w_two[...], back_two, 1, 0) * slope_one).astype(bf16)
-        one = dot(xs, back_one, 1, 1)
-        if k == 0:
-            g_one[0 : x.shape[0], :] = one
-            g_two[...] = two
-            g_three[...] = three
-        else:
-            g_one[0 : x.shape[0], :] += one
-            g_two[...] += two
-            g_three[...] += three
+        add(k, g_one.at[0 : x.shape[0], :], dot(x[:, samples(k)], back_one, 1, 1))
+
+    for k in range(parts + 2):
+        if k < parts:
+            layer_one(k)
+        if k > 1:
+            gradients(k - 2)
+        if 0 < k <= parts:
+            layer_two(k - 1)
     g_one[x.shape[0] :, :] = jnp.zeros((g_one.shape[0] - x.shape[0], g_one.shape[1]), f32)
     rows_two = g_two.shape[0] // shards
     rows_three = g_three.shape[0] // shards
@@ -243,7 +266,7 @@
         out[s, at] = turned(tile, -2 * (s % 4)).astype(bf16)
 
 
-def tower(x, cot, w_one, w_two, w_three, shards, tiles, parts=4):
+def tower(x, cot, w_one, w_two, w_three, shards, tiles, parts=8):
     din, samples = x.shape
     h_one, h_two = w_two.shape
     width = w_three.shape[1]
@@ -389,11 +412,10 @@
     second_in,
     new_first_out,
     new_second_out,
-    update_out,
+    update,
     table,
     first,
     second,
-    update,
     sem,
     out_sem,
 ):
@@ -416,15 +438,13 @@
         first[column, :] = jnp.where(touched, first_out, old_first)
         second[column, :] = jnp.where(touched, second_out, old_second)
         update[column, :] = jnp.where(touched, change, 0.0)
-    copies = [
+    leave = [
         pltpu.make_async_copy(a, b, out_sem.at[i])
-        for i, (a, b) in enumerate(
-            ((update, update_out), (first, new_first_out), (second, new_second_out))
-        )
+        for i, (a, b) in enumerate(((first, new_first_out), (second, new_second_out)))
     ]
-    for c in copies:
+    for c in leave:
         c.start()
-    for c in copies:
+    for c in leave:
         c.wait()
 
 
@@ -434,9 +454,9 @@
         slots_kernel,
         out_shape=(shape,) * 3,
         in_specs=[VMEM] * 2 + [HBM] * 3,
-        out_specs=(HBM,) * 3,
-        scratch_shapes=[pltpu.VMEM(table.shape, f32)] * 4
-        + [pltpu.SemaphoreType.DMA((3,)), pltpu.SemaphoreType.DMA((3,))],
+        out_specs=(HBM,) * 2 + (VMEM,),
+        scratch_shapes=[pltpu.VMEM(table.shape, f32)] * 3
+        + [pltpu.SemaphoreType.DMA((3,)), pltpu.SemaphoreType.DMA((2,))],
         cost_estimate=pl.CostEstimate(
             flops=2000 * table.size, bytes_accessed=24 * table.size, transcendentals=table.size
         ),
@@ -453,12 +473,12 @@
     return (weight - learn_rate * ratio * update, first_out, second_out)
 
 
-def last_kernel(slot_table, recv, *refs):
-    ins, outs, scratch = refs[:11], refs[11:21], refs[21:]
-    held, made, (g_one, g_two, g_three, sem, out_sem) = scratch[:11], scratch[11:21], scratch[21:]
+def last_kernel(slot_table, recv, table, update, *refs):
+    ins, outs, scratch = refs[:9], refs[9:19], refs[19:]
+    held, made, (g_one, g_two, g_three, sem, out_sem) = scratch[:9], scratch[9:19], scratch[19:]
     arrive = [pltpu.make_async_copy(a, b, sem.at[i]) for i, (a, b) in enumerate(zip(ins, held))]
     leave = [pltpu.make_async_copy(a, b, out_sem.at[i]) for i, (a, b) in enumerate(zip(made, outs))]
-    for i in (0, 1, 3, 6, 9, 4, 7, 10, 2, 5, 8):
+    for i in (1, 4, 7, 2, 5, 8, 0, 3, 6):
         arrive[i].start()
     shards, tiles = recv.shape[:2]
     pieces = recv[0, tiles - 1].astype(f32)
@@ -468,10 +488,7 @@
     ratio = learn_rate * (jnp.sqrt(weight_sq) / (jnp.sqrt(update_sq) + ratio_eps))
     ratio = jnp.sum(jnp.where(table_hot(slot_table), ratio, 0.0), axis=1, keepdims=True)
     blocks = slot_table.shape[0]
-    groups = ins[0].shape[0] // blocks
-    arrive[0].wait()
-    arrive[1].wait()
-    table, update = held[:2]
+    groups = table.shape[0] // blocks
     for g in range(groups):
         column = pl.ds(g, blocks, stride=groups)
         made[0][column, :] = table[column, :] - ratio * update[column, :]
@@ -500,9 +517,9 @@
         g_one[r * SUB : (r + 1) * SUB, c * LANE : (c + 1) * LANE] = tile
 
     def dense(n, gradient):
-        for i in (2 + n, 5 + n, 8 + n):
+        for i in (n, 3 + n, 6 + n):
             arrive[i].wait()
-        weight, first, second = held[2 + n], held[5 + n], held[8 + n]
+        weight, first, second = held[n], held[3 + n], held[6 + n]
         made[1 + n][...], made[4 + n][...], made[7 + n][...] = lamb_whole(
             weight[...], first[...], second[...], gradient[0 : weight.shape[0], :]
         )
@@ -517,24 +534,23 @@
 
 
 def last(slot_table, recv, table, update, weights):
-    ins = (table, update) + weights
     outs = (table,) + weights
     return pl.pallas_call(
         last_kernel,
         out_shape=tuple(jax.ShapeDtypeStruct(a.shape, f32) for a in outs),
-        in_specs=[VMEM] * 2 + [HBM] * 11,
+        in_specs=[VMEM] * 4 + [HBM] * 9,
         out_specs=(HBM,) * 10,
-        scratch_shapes=[pltpu.VMEM(a.shape, f32) for a in ins + outs]
+        scratch_shapes=[pltpu.VMEM(a.shape, f32) for a in weights + outs]
         + [
             pltpu.VMEM((2 * SUB, weights[0].shape[1]), f32),
             pltpu.VMEM(weights[1].shape, f32),
             pltpu.VMEM(weights[2].shape, f32),
-            pltpu.SemaphoreType.DMA((len(ins),)),
+            pltpu.SemaphoreType.DMA((len(weights),)),
             pltpu.SemaphoreType.DMA((len(outs),)),
         ],
         compiler_params=WIDE,
         name="last",
-    )(slot_table, recv, *ins)
+    )(slot_table, recv, table, update, *weights)
 
 
 def exchange(value, axis):

time: 87.9 us -> 88.9 us (1.011)
  no operation moved by 1% of the time
where the time goes in v6:
time: 88.9 us; the launch traced here: 88.4 us
  starting transfers between devices  24.1 us (27%)
  waiting for transfers between devices  22 us (25%)
  Pallas kernels  21.4 us (24%)
  blocking collectives  17.8 us (20%)
  local copies, waits for them, and re-layouts  2.02 us (2%)
  between operations  1.01 us (1%)
    all_to_all x3, starting transfers between devices, exchange(): return lax.all_to_all(value, axis, split_axis=0, concat_axis=0, tiled=True)  24.1 us
    all_to_all x3, waiting for transfers between devices, exchange(): return lax.all_to_all(value, axis, split_axis=0, concat_axis=0, tiled=True)  22 us
    all_to_all x1, blocking collectives, exchange(): return lax.all_to_all(value, axis, split_axis=0, concat_axis=0, tiled=True)  17.8 us
    pallas_call x1, Pallas kernels, tower(): pl.pallas_call(functools.partial(tower_kernel, shards, parts), out_shape=...  10.1 us
    pallas_call x1, Pallas kernels, last(): pl.pallas_call(last_kernel, out_shape=tuple((jax.ShapeDtypeStruct(a.shape...  3.76 us
    pallas_call x1, Pallas kernels, routed(): pl.pallas_call(functools.partial(route_kernel, shards, blocks, groups), o...  2.56 us
    pallas_call x1, Pallas kernels, slots(): pl.pallas_call(slots_kernel, out_shape=(shape,) * 3, in_specs=[VMEM] * 2...  2.49 us
  transfers between devices with their start and end apart: 3, of which 3 were waited for; matrix products, arithmetic and copies ran while one was open for 1% of the time, Pallas kernels for 14%

profile of v6, /device:TPU:1, one launch (start us, length us, event | category | flops | bytes accessed | tf_op | source)
XLA Modules:
  0.0 88.4 jit_solution(12560988416518322016)
XLA Ops:
  0.6 0.0 copy-start.2
  0.7 2.6 %route.1 = bf16[8,17,8,128]{3,2,1,0:T(8,128)(2,1)} custom-call(s32[1,128]{1,0:T(1,128)} %ids.1, s32[32,128]{1,0:T(8,128)} %bitcast.20, bf16[1024,128]{1,0:T(8,128)(2,1)} %bitcast.19), custom_call_target="tpu_custom_call" | custom-call | tf_op jit(solution)/shard_map/route/pallas_call | solution.py:96
  3.2 0.0 copy-start.3
  3.2 0.0 copy-start.6
  3.2 0.0 copy-start.9
  3.3 9.1 %all-to-all-start = ((bf16[8,17,8,128]{3,2,1,0:T(8,128)(2,1)}), bf16[8,17,8,128]{3,2,1,0:T(8,128)(2,1)S(1)}, u32[]{:S(2)}, u32[]{:S(2)}) async-start(bf16[8,17,8,128]{3,2,1,0:T(8,128)(2,1)} %route.1), calls=%async_computation | async-start | bytes 557056 | tf_op jit(solution)/shard_map/all_to_all | solution.py:557
  12.4 0.0 copy-done.2
  12.4 0.0 copy-done.3
  12.4 0.0 copy-done.6
  12.4 0.0 copy-done.9
  12.4 10.1 %tower.1.dense = bf16[32,6,8,128]{3,2,1,0:T(8,128)(2,1)S(1)} custom-call(bf16[13,4096]{1,0:T(8,128)(2,1)S(1)} %copy-done.9, bf16[4096,128]{1,0:T(8,128)(2,1)} %cot_in.1, f32[13,512]{1,0:T(8,128)S(1)} %copy-done.6, f32[512,256]{1,0:T(8,128)S(1)} %copy-done.2, f32[256,128]{1,0:T(8,128)S(1)} %copy-done.3), custom_call_target="tpu_custom_call" | custom-call | flops 3867148288 | bytes 2097152 | tf_op jit(solution)/shard_map/tower/pallas_call | solution.py:274
  22.6 0.7 all-to-all-done.recv
  23.3 1.2 %bucket.1 = bf16[32,14,8,128]{3,2,1,0:T(8,128)(2,1)} custom-call(s32[1,128]{1,0:T(1,128)S(1)} %broadcast_in_dim.7.offset, bf16[8,17,8,128]{3,2,1,0:T(8,128)(2,1)S(1)} %all-to-all-done.recv, bf16[32,6,8,128]{3,2,1,0:T(8,128)(2,1)S(1)} %tower.1.dense), custom_call_target="tpu_custom_call" | custom-call | tf_op jit(solution)/shard_map/bucket/pallas_call | solution.py:151
  24.5 0.0 copy-start
  24.5 0.0 copy-start.1
  24.5 9.5 %all-to-all-start.1 = ((bf16[32,14,8,128]{3,2,1,0:T(8,128)(2,1)}), bf16[32,14,8,128]{3,2,1,0:T(8,128)(2,1)S(1)}, u32[]{:S(2)}, u32[]{:S(2)}) async-start(bf16[32,14,8,128]{3,2,1,0:T(8,128)(2,1)} %bucket.1), calls=%async_computation.1 | async-start | bytes 1835008 | tf_op jit(solution)/shard_map/all_to_all | solution.py:557
  34.0 0.0 copy-start.10
  34.1 0.6 copy-done.10
  34.7 0.1 copy.31.slot_table
  34.8 0.0 copy-done
  34.8 0.1 constant_dynamic-slice_fusion.2
  34.9 0.0 copy-done.1
  34.9 1.1 %constant_dynamic-slice_fusion = (f32[128,1,128]{2,1,0:T(1,128)S(1)}, f32[128,1,128]{2,1,0:T(1,128)S(1)}) fusion(f32[128,8,128]{2,1,0:T(8,128)} %param.20, s32[]{:T(128)S(6)} %select_n.6, f32[128,8,128]{2,1,0:T(8,128)S(1)} %copy-done.1), kind=kLoop, calls=%fused_computation | loop fusion | bytes 262148 | tf_op jit(solution)/shard_map/jit(dynamic_index_in_dim)/dynamic_slice | solution.py:586
  36.0 13.7 %all-to-all-done.1.recv = bf16[32,14,8,128]{3,2,1,0:T(8,128)(2,1)S(1)} async-done(((bf16[32,14,8,128]{3,2,1,0:T(8,128)(2,1)}), bf16[32,14,8,128]{3,2,1,0:T(8,128)(2,1)S(1)}, u32[]{:S(2)}, u32[]{:S(2)}) %all-to-all-start.1) | async-done | bytes 917536 | tf_op jit(solution)/shard_map/all_to_all | solution.py:557
  49.7 0.5 own.1
  50.2 17.8 %all_to_all.20.recv = bf16[8,22,8,128]{3,2,1,0:T(8,128)(2,1)S(1)} all-to-all(bf16[8,22,8,128]{3,2,1,0:T(8,128)(2,1)S(1)} %get-tuple-element.27), channel_id=1, replica_groups=mesh['grp'=8,'shard_0'=4,'shard_1'=4,'shard_2'=2] {'grp'}, dimensions={0} | all-to-all | bytes 720896 | tf_op jit(solution)/shard_map/all_to_all | solution.py:557
  68.0 0.8 pack.1
  68.8 5.5 %all-to-all-start.3 = ((bf16[32,6,8,128]{3,2,1,0:T(8,128)(2,1)}), bf16[32,6,8,128]{3,2,1,0:T(8,128)(2,1)S(1)}, u32[]{:S(2)}, u32[]{:S(2)}) async-start(bf16[32,6,8,128]{3,2,1,0:T(8,128)(2,1)} %pack.1), calls=%async_computation.3 | async-start | bytes 786432 | tf_op jit(solution)/shard_map/all_to_all | solution.py:557
  74.3 0.0 copy-start.4
  74.3 0.0 copy-start.5
  74.3 0.0 copy-start.7
  74.3 0.0 copy-start.8
  74.3 2.5 %slots.1 = (f32[1024,128]{1,0:T(8,128)}, f32[1024,128]{1,0:T(8,128)}, f32[1024,128]{1,0:T(8,128)S(1)}) custom-call(bf16[8,22,8,128]{3,2,1,0:T(8,128)(2,1)S(1)} %all_to_all.20.recv, f32[128,128]{1,0:T(8,128)S(1)} %get-tuple-element.28.hit, f32[1024,128]{1,0:T(8,128)S(1)} %bitcast.12, f32[1024,128]{1,0:T(8,128)S(1)} %bitcast.14, f32[1024,128]{1,0:T(8,128)} %bitcast.18), custom_call_target="tpu_custom_call" | custom-call | flops 262144000 | bytes 3145728 | tf_op jit(solution)/shard_map/slots/pallas_call | solution.py:453
  76.8 7.6 %all-to-all-done.3.recv = bf16[32,6,8,128]{3,2,1,0:T(8,128)(2,1)S(1)} async-done(((bf16[32,6,8,128]{3,2,1,0:T(8,128)(2,1)}), bf16[32,6,8,128]{3,2,1,0:T(8,128)(2,1)S(1)}, u32[]{:S(2)}, u32[]{:S(2)}) %all-to-all-start.3) | async-done | bytes 393248 | tf_op jit(solution)/shard_map/all_to_all | solution.py:557
  84.4 0.0 copy-done.4
  84.4 0.0 copy-done.5
  84.4 0.0 copy-done.7
  84.4 0.0 copy-done.8
  84.4 3.8 %last.1 = (f32[1024,128]{1,0:T(8,128)}, f32[13,512]{1,0:T(8,128)}, f32[512,256]{1,0:T(8,128)}, f32[256,128]{1,0:T(8,128)}, f32[13,512]{1,0:T(8,128)}, /*index=5*...) custom-call(s32[128,1]{1,0:T(8,128)S(1)} %copy.31.slot_table, ...), custom_call_target="tpu_custom_call" | custom-call | tf_op jit(solution)/shard_map/last/pallas_call | solution.py:538
  (1 shorter events, 0.0 us)
Async XLA Ops:
  0.6 11.8 %copy-start.2 = (f32[512,256]{1,0:T(8,128)S(1)}, f32[512,256]{1,0:T(8,128)}, u32[]{:S(2)}) copy-start(f32[512,256]{1,0:T(8,128)} %refs_1_.1) | copy-start | bytes 1572868
  3.2 9.2 %copy-start.3 = (f32[256,128]{1,0:T(8,128)S(1)}, f32[256,128]{1,0:T(8,128)}, u32[]{:S(2)}) copy-start(f32[256,128]{1,0:T(8,128)} %refs_2_.1) | copy-start | bytes 393220
  3.2 9.2 %copy-start.6 = (f32[13,512]{1,0:T(8,128)S(1)}, f32[13,512]{1,0:T(8,128)}, u32[]{:S(2)}) copy-start(f32[13,512]{1,0:T(8,128)} %refs_0_.1) | copy-start | bytes 79876
  3.2 9.2 %copy-start.9 = (bf16[13,4096]{1,0:T(8,128)(2,1)S(1)}, bf16[13,4096]{1,0:T(8,128)(2,1)}, u32[]{:S(2)}) copy-start(bf16[13,4096]{1,0:T(8,128)(2,1)} %x_in.1) | copy-start | bytes 319492
  3.3 20.0 %all-to-all-start = ((bf16[8,17,8,128]{3,2,1,0:T(8,128)(2,1)}), bf16[8,17,8,128]{3,2,1,0:T(8,128)(2,1)S(1)}, u32[]{:S(2)}, u32[]{:S(2)}) async-start(bf16[8,17,8,128]{3,2,1,0:T(8,128)(2,1)} %route.1), calls=%async_computation | async-start | bytes 557056 | tf_op jit(solution)/shard_map/all_to_all | solution.py:557
  24.5 10.3 %copy-start = (f32[128,8,128]{2,1,0:T(8,128)S(1)}, f32[128,8,128]{2,1,0:T(8,128)}, u32[]{:S(2)}) copy-start(f32[128,8,128]{2,1,0:T(8,128)} %param.18) | copy-start | bytes 1572868
  24.5 10.4 %copy-start.1 = (f32[128,8,128]{2,1,0:T(8,128)S(1)}, f32[128,8,128]{2,1,0:T(8,128)}, u32[]{:S(2)}) copy-start(f32[128,8,128]{2,1,0:T(8,128)} %param.19) | copy-start | bytes 1572868
  24.5 25.2 %all-to-all-start.1 = ((bf16[32,14,8,128]{3,2,1,0:T(8,128)(2,1)}), bf16[32,14,8,128]{3,2,1,0:T(8,128)(2,1)S(1)}, u32[]{:S(2)}, u32[]{:S(2)}) async-start(bf16[32,14,8,128]{3,2,1,0:T(8,128)(2,1)} %bucket.1), calls=%async_computation.1 | async-start | bytes 1835008 | tf_op jit(solution)/shard_map/all_to_all | solution.py:557
  34.0 0.7 copy-start.10
  68.8 15.6 %all-to-all-start.3 = ((bf16[32,6,8,128]{3,2,1,0:T(8,128)(2,1)}), bf16[32,6,8,128]{3,2,1,0:T(8,128)(2,1)S(1)}, u32[]{:S(2)}, u32[]{:S(2)}) async-start(bf16[32,6,8,128]{3,2,1,0:T(8,128)(2,1)} %pack.1), calls=%async_computation.3 | async-start | bytes 786432 | tf_op jit(solution)/shard_map/all_to_all | solution.py:557
  74.3 10.1 %copy-start.4 = (f32[256,128]{1,0:T(8,128)S(1)}, f32[256,128]{1,0:T(8,128)}, u32[]{:S(2)}) copy-start(f32[256,128]{1,0:T(8,128)} %refs_5_.1) | copy-start | bytes 393220
  74.3 10.1 %copy-start.5 = (f32[256,128]{1,0:T(8,128)S(1)}, f32[256,128]{1,0:T(8,128)}, u32[]{:S(2)}) copy-start(f32[256,128]{1,0:T(8,128)} %refs_8_.1) | copy-start | bytes 393220
  74.3 10.1 %copy-start.7 = (f32[13,512]{1,0:T(8,128)S(1)}, f32[13,512]{1,0:T(8,128)}, u32[]{:S(2)}) copy-start(f32[13,512]{1,0:T(8,128)} %refs_3_.1) | copy-start | bytes 79876
  74.3 10.1 %copy-start.8 = (f32[13,512]{1,0:T(8,128)S(1)}, f32[13,512]{1,0:T(8,128)}, u32[]{:S(2)}) copy-start(f32[13,512]{1,0:T(8,128)} %refs_6_.1) | copy-start | bytes 79876

commit v7 on v5

--- a/solution.py
+++ b/solution.py
@@ -243,7 +243,7 @@
         out[s, at] = turned(tile, -2 * (s % 4)).astype(bf16)
 
 
-def tower(x, cot, w_one, w_two, w_three, shards, tiles, parts=4):
+def tower(x, cot, w_one, w_two, w_three, shards, tiles, parts=2):
     din, samples = x.shape
     h_one, h_two = w_two.shape
     width = w_three.shape[1]
@@ -389,11 +389,10 @@
     second_in,
     new_first_out,
     new_second_out,
-    update_out,
+    update,
     table,
     first,
     second,
-    update,
     sem,
     out_sem,
 ):
@@ -416,15 +415,13 @@
         first[column, :] = jnp.where(touched, first_out, old_first)
         second[column, :] = jnp.where(touched, second_out, old_second)
         update[column, :] = jnp.where(touched, change, 0.0)
-    copies = [
+    leave = [
         pltpu.make_async_copy(a, b, out_sem.at[i])
-        for i, (a, b) in enumerate(
-            ((update, update_out), (first, new_first_out), (second, new_second_out))
-        )
+        for i, (a, b) in enumerate(((first, new_first_out), (second, new_second_out)))
     ]
-    for c in copies:
+    for c in leave:
         c.start()
-    for c in copies:
+    for c in leave:
         c.wait()
 
 
@@ -434,9 +431,9 @@
         slots_kernel,
         out_shape=(shape,) * 3,
         in_specs=[VMEM] * 2 + [HBM] * 3,
-        out_specs=(HBM,) * 3,
-        scratch_shapes=[pltpu.VMEM(table.shape, f32)] * 4
-        + [pltpu.SemaphoreType.DMA((3,)), pltpu.SemaphoreType.DMA((3,))],
+        out_specs=(HBM,) * 2 + (VMEM,),
+        scratch_shapes=[pltpu.VMEM(table.shape, f32)] * 3
+        + [pltpu.SemaphoreType.DMA((3,)), pltpu.SemaphoreType.DMA((2,))],
         cost_estimate=pl.CostEstimate(
             flops=2000 * table.size, bytes_accessed=24 * table.size, transcendentals=table.size
         ),
@@ -453,12 +450,12 @@
     return (weight - learn_rate * ratio * update, first_out, second_out)
 
 
-def last_kernel(slot_table, recv, *refs):
-    ins, outs, scratch = refs[:11], refs[11:21], refs[21:]
-    held, made, (g_one, g_two, g_three, sem, out_sem) = scratch[:11], scratch[11:21], scratch[21:]
+def last_kernel(slot_table, recv, table, update, *refs):
+    ins, outs, scratch = refs[:9], refs[9:19], refs[19:]
+    held, made, (g_one, g_two, g_three, sem, out_sem) = scratch[:9], scratch[9:19], scratch[19:]
     arrive = [pltpu.make_async_copy(a, b, sem.at[i]) for i, (a, b) in enumerate(zip(ins, held))]
     leave = [pltpu.make_async_copy(a, b, out_sem.at[i]) for i, (a, b) in enumerate(zip(made, outs))]
-    for i in (0, 1, 3, 6, 9, 4, 7, 10, 2, 5, 8):
+    for i in (1, 4, 7, 2, 5, 8, 0, 3, 6):
         arrive[i].start()
     shards, tiles = recv.shape[:2]
     pieces = recv[0, tiles - 1].astype(f32)
@@ -468,10 +465,7 @@
     ratio = learn_rate * (jnp.sqrt(weight_sq) / (jnp.sqrt(update_sq) + ratio_eps))
     ratio = jnp.sum(jnp.where(table_hot(slot_table), ratio, 0.0), axis=1, keepdims=True)
     blocks = slot_table.shape[0]
-    groups = ins[0].shape[0] // blocks
-    arrive[0].wait()
-    arrive[1].wait()
-    table, update = held[:2]
+    groups = table.shape[0] // blocks
     for g in range(groups):
         column = pl.ds(g, blocks, stride=groups)
         made[0][column, :] = table[column, :] - ratio * update[column, :]
@@ -500,9 +494,9 @@
         g_one[r * SUB : (r + 1) * SUB, c * LANE : (c + 1) * LANE] = tile
 
     def dense(n, gradient):
-        for i in (2 + n, 5 + n, 8 + n):
+        for i in (n, 3 + n, 6 + n):
             arrive[i].wait()
-        weight, first, second = held[2 + n], held[5 + n], held[8 + n]
+        weight, first, second = held[n], held[3 + n], held[6 + n]
         made[1 + n][...], made[4 + n][...], made[7 + n][...] = lamb_whole(
             weight[...], first[...], second[...], gradient[0 : weight.shape[0], :]
         )
@@ -517,24 +511,23 @@
 
 
 def last(slot_table, recv, table, update, weights):
-    ins = (table, update) + weights
     outs = (table,) + weights
     return pl.pallas_call(
         last_kernel,
         out_shape=tuple(jax.ShapeDtypeStruct(a.shape, f32) for a in outs),
-        in_specs=[VMEM] * 2 + [HBM] * 11,
+        in_specs=[VMEM] * 4 + [HBM] * 9,
         out_specs=(HBM,) * 10,
-        scratch_shapes=[pltpu.VMEM(a.shape, f32) for a in ins + outs]
+        scratch_shapes=[pltpu.VMEM(a.shape, f32) for a in weights + outs]
         + [
             pltpu.VMEM((2 * SUB, weights[0].shape[1]), f32),
             pltpu.VMEM(weights[1].shape, f32),
             pltpu.VMEM(weights[2].shape, f32),
-            pltpu.SemaphoreType.DMA((len(ins),)),
+            pltpu.SemaphoreType.DMA((len(weights),)),
             pltpu.SemaphoreType.DMA((len(outs),)),
         ],
         compiler_params=WIDE,
         name="last",
-    )(slot_table, recv, *ins)
+    )(slot_table, recv, table, update, *weights)
 
 
 def exchange(value, axis):

time: 87.9 us -> 87.5 us (level)
  Pallas kernels: 20.9 us -> 20 us
  transfers between devices with their start and end apart: 3 -> 3, of which waited for: 3 -> 3; matrix products, arithmetic and copies ran while one was open for 1% -> 2% of each run, Pallas kernels for 14% -> 13%
where the time goes in v7:
time: 87.5 us; the launch traced here: 86.9 us
  starting transfers between devices  24.1 us (28%)
  waiting for transfers between devices  22.9 us (26%)
  Pallas kernels  20 us (23%)
  blocking collectives  16.9 us (19%)
  local copies, waits for them, and re-layouts  2.01 us (2%)
  between operations  0.98 us (1%)
    all_to_all x3, starting transfers between devices, exchange(): return lax.all_to_all(value, axis, split_axis=0, concat_axis=0, tiled=True)  24.1 us
    all_to_all x3, waiting for transfers between devices, exchange(): return lax.all_to_all(value, axis, split_axis=0, concat_axis=0, tiled=True)  22.9 us
    all_to_all x1, blocking collectives, exchange(): return lax.all_to_all(value, axis, split_axis=0, concat_axis=0, tiled=True)  16.9 us
    pallas_call x1, Pallas kernels, tower(): pl.pallas_call(functools.partial(tower_kernel, shards, parts), out_shape=...  9.2 us
    pallas_call x1, Pallas kernels, last(): pl.pallas_call(last_kernel, out_shape=tuple((jax.ShapeDtypeStruct(a.shape...  3.76 us
    pallas_call x1, Pallas kernels, slots(): pl.pallas_call(slots_kernel, out_shape=(shape,) * 3, in_specs=[VMEM] * 2...  2.49 us
    pallas_call x1, Pallas kernels, routed(): pl.pallas_call(functools.partial(route_kernel, shards, blocks, groups), o...  2.08 us
  transfers between devices with their start and end apart: 3, of which 3 were waited for; matrix products, arithmetic and copies ran while one was open for 2% of the time, Pallas kernels for 13%

profile of v7, /device:TPU:1, one launch (start us, length us, event | category | flops | bytes accessed | tf_op | source)
XLA Modules:
  0.0 86.9 jit_solution(15808446240161287822)
XLA Ops:
  0.6 0.0 copy-start.2
  0.7 2.1 %route.1 = bf16[8,17,8,128]{3,2,1,0:T(8,128)(2,1)} custom-call(s32[1,128]{1,0:T(1,128)} %ids.1, s32[32,128]{1,0:T(8,128)} %bitcast.20, bf16[1024,128]{1,0:T(8,128)(2,1)} %bitcast.19), custom_call_target="tpu_custom_call" | custom-call | tf_op jit(solution)/shard_map/route/pallas_call | solution.py:88
  2.7 0.0 copy-start.3
  2.7 0.0 copy-start.6
  2.7 0.0 copy-start.9
  2.7 9.1 %all-to-all-start = ((bf16[8,17,8,128]{3,2,1,0:T(8,128)(2,1)}), bf16[8,17,8,128]{3,2,1,0:T(8,128)(2,1)S(1)}, u32[]{:S(2)}, u32[]{:S(2)}) async-start(bf16[8,17,8,128]{3,2,1,0:T(8,128)(2,1)} %route.1), calls=%async_computation | async-start | bytes 557056 | tf_op jit(solution)/shard_map/all_to_all | solution.py:534
  11.9 0.0 copy-done.2
  11.9 0.0 copy-done.3
  11.9 0.0 copy-done.6
  11.9 0.0 copy-done.9
  11.9 9.2 %tower.1.dense = bf16[32,6,8,128]{3,2,1,0:T(8,128)(2,1)S(1)} custom-call(bf16[13,4096]{1,0:T(8,128)(2,1)S(1)} %copy-done.9, bf16[4096,128]{1,0:T(8,128)(2,1)} %cot_in.1, f32[13,512]{1,0:T(8,128)S(1)} %copy-done.6, f32[512,256]{1,0:T(8,128)S(1)} %copy-done.2, f32[256,128]{1,0:T(8,128)S(1)} %copy-done.3), custom_call_target="tpu_custom_call" | custom-call | flops 3867148288 | bytes 2097152 | tf_op jit(solution)/shard_map/tower/pallas_call | solution.py:251
  21.1 1.6 %all-to-all-done.recv = bf16[8,17,8,128]{3,2,1,0:T(8,128)(2,1)S(1)} async-done(((bf16[8,17,8,128]{3,2,1,0:T(8,128)(2,1)}), bf16[8,17,8,128]{3,2,1,0:T(8,128)(2,1)S(1)}, u32[]{:S(2)}, u32[]{:S(2)}) %all-to-all-start) | async-done | bytes 278560 | tf_op jit(solution)/shard_map/all_to_all | solution.py:534
  22.8 1.2 %bucket.1 = bf16[32,14,8,128]{3,2,1,0:T(8,128)(2,1)} custom-call(s32[1,128]{1,0:T(1,128)S(1)} %broadcast_in_dim.7.offset, bf16[8,17,8,128]{3,2,1,0:T(8,128)(2,1)S(1)} %all-to-all-done.recv, bf16[32,6,8,128]{3,2,1,0:T(8,128)(2,1)S(1)} %tower.1.dense), custom_call_target="tpu_custom_call" | custom-call | tf_op jit(solution)/shard_map/bucket/pallas_call | solution.py:138
  23.9 0.0 copy-start
  24.0 0.0 copy-start.1
  24.0 9.5 %all-to-all-start.1 = ((bf16[32,14,8,128]{3,2,1,0:T(8,128)(2,1)}), bf16[32,14,8,128]{3,2,1,0:T(8,128)(2,1)S(1)}, u32[]{:S(2)}, u32[]{:S(2)}) async-start(bf16[32,14,8,128]{3,2,1,0:T(8,128)(2,1)} %bucket.1), calls=%async_computation.1 | async-start | bytes 1835008 | tf_op jit(solution)/shard_map/all_to_all | solution.py:534
  33.5 0.0 copy-start.10
  33.5 0.6 copy-done.10
  34.2 0.1 copy.31.slot_table
  34.3 0.0 copy-done
  34.3 0.1 constant_dynamic-slice_fusion.2
  34.3 0.0 copy-done.1
  34.4 1.1 %constant_dynamic-slice_fusion = (f32[128,1,128]{2,1,0:T(1,128)S(1)}, f32[128,1,128]{2,1,0:T(1,128)S(1)}) fusion(f32[128,8,128]{2,1,0:T(8,128)} %param.20, s32[]{:T(128)S(6)} %select_n.6, f32[128,8,128]{2,1,0:T(8,128)S(1)} %copy-done.1), kind=kLoop, calls=%fused_computation | loop fusion | bytes 262148 | tf_op jit(solution)/shard_map/jit(dynamic_index_in_dim)/dynamic_slice | solution.py:563
  35.5 13.7 %all-to-all-done.1.recv = bf16[32,14,8,128]{3,2,1,0:T(8,128)(2,1)S(1)} async-done(((bf16[32,14,8,128]{3,2,1,0:T(8,128)(2,1)}), bf16[32,14,8,128]{3,2,1,0:T(8,128)(2,1)S(1)}, u32[]{:S(2)}, u32[]{:S(2)}) %all-to-all-start.1) | async-done | bytes 917536 | tf_op jit(solution)/shard_map/all_to_all | solution.py:534
  49.1 0.5 own.1
  49.6 16.9 %all_to_all.20.recv = bf16[8,22,8,128]{3,2,1,0:T(8,128)(2,1)S(1)} all-to-all(bf16[8,22,8,128]{3,2,1,0:T(8,128)(2,1)S(1)} %get-tuple-element.27), channel_id=1, replica_groups=mesh['grp'=8,'shard_0'=4,'shard_1'=4,'shard_2'=2] {'grp'}, dimensions={0} | all-to-all | bytes 720896 | tf_op jit(solution)/shard_map/all_to_all | solution.py:534
  66.6 0.8 pack.1
  67.4 5.5 %all-to-all-start.3 = ((bf16[32,6,8,128]{3,2,1,0:T(8,128)(2,1)}), bf16[32,6,8,128]{3,2,1,0:T(8,128)(2,1)S(1)}, u32[]{:S(2)}, u32[]{:S(2)}) async-start(bf16[32,6,8,128]{3,2,1,0:T(8,128)(2,1)} %pack.1), calls=%async_computation.3 | async-start | bytes 786432 | tf_op jit(solution)/shard_map/all_to_all | solution.py:534
  72.8 0.0 copy-start.4
  72.8 0.0 copy-start.5
  72.8 0.0 copy-start.7
  72.9 0.0 copy-start.8
  72.9 2.5 %slots.1 = (f32[1024,128]{1,0:T(8,128)}, f32[1024,128]{1,0:T(8,128)}, f32[1024,128]{1,0:T(8,128)S(1)}) custom-call(bf16[8,22,8,128]{3,2,1,0:T(8,128)(2,1)S(1)} %all_to_all.20.recv, f32[128,128]{1,0:T(8,128)S(1)} %get-tuple-element.28.hit, f32[1024,128]{1,0:T(8,128)S(1)} %bitcast.12, f32[1024,128]{1,0:T(8,128)S(1)} %bitcast.14, f32[1024,128]{1,0:T(8,128)} %bitcast.18), custom_call_target="tpu_custom_call" | custom-call | flops 262144000 | bytes 3145728 | tf_op jit(solution)/shard_map/slots/pallas_call | solution.py:430
  75.4 7.6 %all-to-all-done.3.recv = bf16[32,6,8,128]{3,2,1,0:T(8,128)(2,1)S(1)} async-done(((bf16[32,6,8,128]{3,2,1,0:T(8,128)(2,1)}), bf16[32,6,8,128]{3,2,1,0:T(8,128)(2,1)S(1)}, u32[]{:S(2)}, u32[]{:S(2)}) %all-to-all-start.3) | async-done | bytes 393248 | tf_op jit(solution)/shard_map/all_to_all | solution.py:534
  83.0 0.0 copy-done.4
  83.0 0.0 copy-done.5
  83.0 0.0 copy-done.7
  83.0 0.0 copy-done.8
  83.0 3.8 %last.1 = (f32[1024,128]{1,0:T(8,128)}, f32[13,512]{1,0:T(8,128)}, f32[512,256]{1,0:T(8,128)}, f32[256,128]{1,0:T(8,128)}, f32[13,512]{1,0:T(8,128)}, /*index=5*...) custom-call(s32[128,1]{1,0:T(8,128)S(1)} %copy.31.slot_table, ...), custom_call_target="tpu_custom_call" | custom-call | tf_op jit(solution)/shard_map/last/pallas_call | solution.py:515
  (1 shorter events, 0.0 us)
Async XLA Ops:
  0.6 11.2 %copy-start.2 = (f32[512,256]{1,0:T(8,128)S(1)}, f32[512,256]{1,0:T(8,128)}, u32[]{:S(2)}) copy-start(f32[512,256]{1,0:T(8,128)} %refs_1_.1) | copy-start | bytes 1572868
  2.7 9.1 %copy-start.3 = (f32[256,128]{1,0:T(8,128)S(1)}, f32[256,128]{1,0:T(8,128)}, u32[]{:S(2)}) copy-start(f32[256,128]{1,0:T(8,128)} %refs_2_.1) | copy-start | bytes 393220
  2.7 9.2 %copy-start.6 = (f32[13,512]{1,0:T(8,128)S(1)}, f32[13,512]{1,0:T(8,128)}, u32[]{:S(2)}) copy-start(f32[13,512]{1,0:T(8,128)} %refs_0_.1) | copy-start | bytes 79876
  2.7 9.2 %copy-start.9 = (bf16[13,4096]{1,0:T(8,128)(2,1)S(1)}, bf16[13,4096]{1,0:T(8,128)(2,1)}, u32[]{:S(2)}) copy-start(bf16[13,4096]{1,0:T(8,128)(2,1)} %x_in.1) | copy-start | bytes 319492
  2.7 20.0 %all-to-all-start = ((bf16[8,17,8,128]{3,2,1,0:T(8,128)(2,1)}), bf16[8,17,8,128]{3,2,1,0:T(8,128)(2,1)S(1)}, u32[]{:S(2)}, u32[]{:S(2)}) async-start(bf16[8,17,8,128]{3,2,1,0:T(8,128)(2,1)} %route.1), calls=%async_computation | async-start | bytes 557056 | tf_op jit(solution)/shard_map/all_to_all | solution.py:534
  23.9 10.3 %copy-start = (f32[128,8,128]{2,1,0:T(8,128)S(1)}, f32[128,8,128]{2,1,0:T(8,128)}, u32[]{:S(2)}) copy-start(f32[128,8,128]{2,1,0:T(8,128)} %param.18) | copy-start | bytes 1572868
  24.0 10.4 %copy-start.1 = (f32[128,8,128]{2,1,0:T(8,128)S(1)}, f32[128,8,128]{2,1,0:T(8,128)}, u32[]{:S(2)}) copy-start(f32[128,8,128]{2,1,0:T(8,128)} %param.19) | copy-start | bytes 1572868
  24.0 25.2 %all-to-all-start.1 = ((bf16[32,14,8,128]{3,2,1,0:T(8,128)(2,1)}), bf16[32,14,8,128]{3,2,1,0:T(8,128)(2,1)S(1)}, u32[]{:S(2)}, u32[]{:S(2)}) async-start(bf16[32,14,8,128]{3,2,1,0:T(8,128)(2,1)} %bucket.1), calls=%async_computation.1 | async-start | bytes 1835008 | tf_op jit(solution)/shard_map/all_to_all | solution.py:534
  33.5 0.7 copy-start.10
  67.4 15.6 %all-to-all-start.3 = ((bf16[32,6,8,128]{3,2,1,0:T(8,128)(2,1)}), bf16[32,6,8,128]{3,2,1,0:T(8,128)(2,1)S(1)}, u32[]{:S(2)}, u32[]{:S(2)}) async-start(bf16[32,6,8,128]{3,2,1,0:T(8,128)(2,1)} %pack.1), calls=%async_computation.3 | async-start | bytes 786432 | tf_op jit(solution)/shard_map/all_to_all | solution.py:534
  72.8 10.1 %copy-start.4 = (f32[256,128]{1,0:T(8,128)S(1)}, f32[256,128]{1,0:T(8,128)}, u32[]{:S(2)}) copy-start(f32[256,128]{1,0:T(8,128)} %refs_5_.1) | copy-start | bytes 393220
  72.8 10.1 %copy-start.5 = (f32[256,128]{1,0:T(8,128)S(1)}, f32[256,128]{1,0:T(8,128)}, u32[]{:S(2)}) copy-start(f32[256,128]{1,0:T(8,128)} %refs_8_.1) | copy-start | bytes 393220
  72.8 10.1 %copy-start.7 = (f32[13,512]{1,0:T(8,128)S(1)}, f32[13,512]{1,0:T(8,128)}, u32[]{:S(2)}) copy-start(f32[13,512]{1,0:T(8,128)} %refs_3_.1) | copy-start | bytes 79876
  72.9 10.1 %copy-start.8 = (f32[13,512]{1,0:T(8,128)S(1)}, f32[13,512]{1,0:T(8,128)}, u32[]{:S(2)}) copy-start(f32[13,512]{1,0:T(8,128)} %refs_6_.1) | copy-start | bytes 79876

commit v8 on v7

--- a/solution.py
+++ b/solution.py
@@ -206,10 +206,15 @@
     sums = None
     for k in range(parts):
         xs = x[:, k * step : (k + 1) * step]
-        hidden_one, slope_one = act(dot(w_one[...], xs, 0, 0))
+        if k == 0:
+            hidden_one, slope_one = act(dot(w_one[...], xs, 0, 0))
+        else:
+            hidden_one, slope_one = ahead
         hidden_two, slope_two = act(dot(w_two_t[...], hidden_one, 1, 0))
         chunks[k].wait()
         cots = cot[k * step : (k + 1) * step, :]
+        if k + 1 < parts:
+            ahead = act(dot(w_one[...], x[:, (k + 1) * step : (k + 2) * step], 0, 0))
         three = dot(hidden_two, cots, 1, 0)
         back_two = (dot(w_three[...], cots, 1, 1) * slope_two).astype(bf16)
         two = dot(hidden_one, back_two, 1, 1)

time: 87.5 us -> 87.1 us (level)
  no operation moved by 1% of the time
where the time goes in v8:
time: 87.1 us; the launch traced here: 86.6 us
  starting transfers between devices  24.1 us (28%)
  waiting for transfers between devices  23.2 us (27%)
  Pallas kernels  19.7 us (23%)
  blocking collectives  16.6 us (19%)
  local copies, waits for them, and re-layouts  2.01 us (2%)
  between operations  0.98 us (1%)
    all_to_all x3, starting transfers between devices, exchange(): return lax.all_to_all(value, axis, split_axis=0, concat_axis=0, tiled=True)  24.1 us
    all_to_all x3, waiting for transfers between devices, exchange(): return lax.all_to_all(value, axis, split_axis=0, concat_axis=0, tiled=True)  23.2 us
    all_to_all x1, blocking collectives, exchange(): return lax.all_to_all(value, axis, split_axis=0, concat_axis=0, tiled=True)  16.6 us
    pallas_call x1, Pallas kernels, tower(): pl.pallas_call(functools.partial(tower_kernel, shards, parts), out_shape=...  8.88 us
    pallas_call x1, Pallas kernels, last(): pl.pallas_call(last_kernel, out_shape=tuple((jax.ShapeDtypeStruct(a.shape...  3.76 us
    pallas_call x1, Pallas kernels, slots(): pl.pallas_call(slots_kernel, out_shape=(shape,) * 3, in_specs=[VMEM] * 2...  2.49 us
    pallas_call x1, Pallas kernels, routed(): pl.pallas_call(functools.partial(route_kernel, shards, blocks, groups), o...  2.08 us
  transfers between devices with their start and end apart: 3, of which 3 were waited for; matrix products, arithmetic and copies ran while one was open for 2% of the time, Pallas kernels for 13%

profile of v8, /device:TPU:1, one launch (start us, length us, event | category | flops | bytes accessed | tf_op | source)
XLA Modules:
  0.0 86.6 jit_solution(6141556359964004031)
XLA Ops:
  0.6 0.0 copy-start.2
  0.7 2.1 %route.1 = bf16[8,17,8,128]{3,2,1,0:T(8,128)(2,1)} custom-call(s32[1,128]{1,0:T(1,128)} %ids.1, s32[32,128]{1,0:T(8,128)} %bitcast.20, bf16[1024,128]{1,0:T(8,128)(2,1)} %bitcast.19), custom_call_target="tpu_custom_call" | custom-call | tf_op jit(solution)/shard_map/route/pallas_call | solution.py:88
  2.7 0.0 copy-start.3
  2.7 0.0 copy-start.6
  2.7 0.0 copy-start.9
  2.7 9.1 %all-to-all-start = ((bf16[8,17,8,128]{3,2,1,0:T(8,128)(2,1)}), bf16[8,17,8,128]{3,2,1,0:T(8,128)(2,1)S(1)}, u32[]{:S(2)}, u32[]{:S(2)}) async-start(bf16[8,17,8,128]{3,2,1,0:T(8,128)(2,1)} %route.1), calls=%async_computation | async-start | bytes 557056 | tf_op jit(solution)/shard_map/all_to_all | solution.py:539
  11.9 0.0 copy-done.2
  11.9 0.0 copy-done.3
  11.9 0.0 copy-done.6
  11.9 0.0 copy-done.9
  11.9 8.9 %tower.1.dense = bf16[32,6,8,128]{3,2,1,0:T(8,128)(2,1)S(1)} custom-call(bf16[13,4096]{1,0:T(8,128)(2,1)S(1)} %copy-done.9, bf16[4096,128]{1,0:T(8,128)(2,1)} %cot_in.1, f32[13,512]{1,0:T(8,128)S(1)} %copy-done.6, f32[512,256]{1,0:T(8,128)S(1)} %copy-done.2, f32[256,128]{1,0:T(8,128)S(1)} %copy-done.3), custom_call_target="tpu_custom_call" | custom-call | flops 3867148288 | bytes 2097152 | tf_op jit(solution)/shard_map/tower/pallas_call | solution.py:256
  20.8 2.0 %all-to-all-done.recv = bf16[8,17,8,128]{3,2,1,0:T(8,128)(2,1)S(1)} async-done(((bf16[8,17,8,128]{3,2,1,0:T(8,128)(2,1)}), bf16[8,17,8,128]{3,2,1,0:T(8,128)(2,1)S(1)}, u32[]{:S(2)}, u32[]{:S(2)}) %all-to-all-start) | async-done | bytes 278560 | tf_op jit(solution)/shard_map/all_to_all | solution.py:539
  22.8 1.2 %bucket.1 = bf16[32,14,8,128]{3,2,1,0:T(8,128)(2,1)} custom-call(s32[1,128]{1,0:T(1,128)S(1)} %broadcast_in_dim.7.offset, bf16[8,17,8,128]{3,2,1,0:T(8,128)(2,1)S(1)} %all-to-all-done.recv, bf16[32,6,8,128]{3,2,1,0:T(8,128)(2,1)S(1)} %tower.1.dense), custom_call_target="tpu_custom_call" | custom-call | tf_op jit(solution)/shard_map/bucket/pallas_call | solution.py:138
  23.9 0.0 copy-start
  24.0 0.0 copy-start.1
  24.0 9.5 %all-to-all-start.1 = ((bf16[32,14,8,128]{3,2,1,0:T(8,128)(2,1)}), bf16[32,14,8,128]{3,2,1,0:T(8,128)(2,1)S(1)}, u32[]{:S(2)}, u32[]{:S(2)}) async-start(bf16[32,14,8,128]{3,2,1,0:T(8,128)(2,1)} %bucket.1), calls=%async_computation.1 | async-start | bytes 1835008 | tf_op jit(solution)/shard_map/all_to_all | solution.py:539
  33.5 0.0 copy-start.10
  33.5 0.6 copy-done.10
  34.2 0.1 copy.31.slot_table
  34.3 0.0 copy-done
  34.3 0.1 constant_dynamic-slice_fusion.2
  34.3 0.0 copy-done.1
  34.4 1.1 %constant_dynamic-slice_fusion = (f32[128,1,128]{2,1,0:T(1,128)S(1)}, f32[128,1,128]{2,1,0:T(1,128)S(1)}) fusion(f32[128,8,128]{2,1,0:T(8,128)} %param.20, s32[]{:T(128)S(6)} %select_n.6, f32[128,8,128]{2,1,0:T(8,128)S(1)} %copy-done.1), kind=kLoop, calls=%fused_computation | loop fusion | bytes 262148 | tf_op jit(solution)/shard_map/jit(dynamic_index_in_dim)/dynamic_slice | solution.py:568
  35.5 13.7 %all-to-all-done.1.recv = bf16[32,14,8,128]{3,2,1,0:T(8,128)(2,1)S(1)} async-done(((bf16[32,14,8,128]{3,2,1,0:T(8,128)(2,1)}), bf16[32,14,8,128]{3,2,1,0:T(8,128)(2,1)S(1)}, u32[]{:S(2)}, u32[]{:S(2)}) %all-to-all-start.1) | async-done | bytes 917536 | tf_op jit(solution)/shard_map/all_to_all | solution.py:539
  49.1 0.5 own.1
  49.6 16.6 %all_to_all.20.recv = bf16[8,22,8,128]{3,2,1,0:T(8,128)(2,1)S(1)} all-to-all(bf16[8,22,8,128]{3,2,1,0:T(8,128)(2,1)S(1)} %get-tuple-element.27), channel_id=1, replica_groups=mesh['grp'=8,'shard_0'=4,'shard_1'=4,'shard_2'=2] {'grp'}, dimensions={0} | all-to-all | bytes 720896 | tf_op jit(solution)/shard_map/all_to_all | solution.py:539
  66.3 0.8 pack.1
  67.0 5.5 %all-to-all-start.3 = ((bf16[32,6,8,128]{3,2,1,0:T(8,128)(2,1)}), bf16[32,6,8,128]{3,2,1,0:T(8,128)(2,1)S(1)}, u32[]{:S(2)}, u32[]{:S(2)}) async-start(bf16[32,6,8,128]{3,2,1,0:T(8,128)(2,1)} %pack.1), calls=%async_computation.3 | async-start | bytes 786432 | tf_op jit(solution)/shard_map/all_to_all | solution.py:539
  72.5 0.0 copy-start.4
  72.5 0.0 copy-start.5
  72.5 0.0 copy-start.7
  72.5 0.0 copy-start.8
  72.6 2.5 %slots.1 = (f32[1024,128]{1,0:T(8,128)}, f32[1024,128]{1,0:T(8,128)}, f32[1024,128]{1,0:T(8,128)S(1)}) custom-call(bf16[8,22,8,128]{3,2,1,0:T(8,128)(2,1)S(1)} %all_to_all.20.recv, f32[128,128]{1,0:T(8,128)S(1)} %get-tuple-element.28.hit, f32[1024,128]{1,0:T(8,128)S(1)} %bitcast.12, f32[1024,128]{1,0:T(8,128)S(1)} %bitcast.14, f32[1024,128]{1,0:T(8,128)} %bitcast.18), custom_call_target="tpu_custom_call" | custom-call | flops 262144000 | bytes 3145728 | tf_op jit(solution)/shard_map/slots/pallas_call | solution.py:435
  75.1 7.6 %all-to-all-done.3.recv = bf16[32,6,8,128]{3,2,1,0:T(8,128)(2,1)S(1)} async-done(((bf16[32,6,8,128]{3,2,1,0:T(8,128)(2,1)}), bf16[32,6,8,128]{3,2,1,0:T(8,128)(2,1)S(1)}, u32[]{:S(2)}, u32[]{:S(2)}) %all-to-all-start.3) | async-done | bytes 393248 | tf_op jit(solution)/shard_map/all_to_all | solution.py:539
  82.6 0.0 copy-done.4
  82.7 0.0 copy-done.5
  82.7 0.0 copy-done.7
  82.7 0.0 copy-done.8
  82.7 3.8 %last.1 = (f32[1024,128]{1,0:T(8,128)}, f32[13,512]{1,0:T(8,128)}, f32[512,256]{1,0:T(8,128)}, f32[256,128]{1,0:T(8,128)}, f32[13,512]{1,0:T(8,128)}, /*index=5*...) custom-call(s32[128,1]{1,0:T(8,128)S(1)} %copy.31.slot_table, ...), custom_call_target="tpu_custom_call" | custom-call | tf_op jit(solution)/shard_map/last/pallas_call | solution.py:520
  (1 shorter events, 0.0 us)
Async XLA Ops:
  0.6 11.2 %copy-start.2 = (f32[512,256]{1,0:T(8,128)S(1)}, f32[512,256]{1,0:T(8,128)}, u32[]{:S(2)}) copy-start(f32[512,256]{1,0:T(8,128)} %refs_1_.1) | copy-start | bytes 1572868
  2.7 9.1 %copy-start.3 = (f32[256,128]{1,0:T(8,128)S(1)}, f32[256,128]{1,0:T(8,128)}, u32[]{:S(2)}) copy-start(f32[256,128]{1,0:T(8,128)} %refs_2_.1) | copy-start | bytes 393220
  2.7 9.2 %copy-start.6 = (f32[13,512]{1,0:T(8,128)S(1)}, f32[13,512]{1,0:T(8,128)}, u32[]{:S(2)}) copy-start(f32[13,512]{1,0:T(8,128)} %refs_0_.1) | copy-start | bytes 79876
  2.7 9.2 %copy-start.9 = (bf16[13,4096]{1,0:T(8,128)(2,1)S(1)}, bf16[13,4096]{1,0:T(8,128)(2,1)}, u32[]{:S(2)}) copy-start(bf16[13,4096]{1,0:T(8,128)(2,1)} %x_in.1) | copy-start | bytes 319492
  2.7 20.0 %all-to-all-start = ((bf16[8,17,8,128]{3,2,1,0:T(8,128)(2,1)}), bf16[8,17,8,128]{3,2,1,0:T(8,128)(2,1)S(1)}, u32[]{:S(2)}, u32[]{:S(2)}) async-start(bf16[8,17,8,128]{3,2,1,0:T(8,128)(2,1)} %route.1), calls=%async_computation | async-start | bytes 557056 | tf_op jit(solution)/shard_map/all_to_all | solution.py:539
  23.9 10.3 %copy-start = (f32[128,8,128]{2,1,0:T(8,128)S(1)}, f32[128,8,128]{2,1,0:T(8,128)}, u32[]{:S(2)}) copy-start(f32[128,8,128]{2,1,0:T(8,128)} %param.18) | copy-start | bytes 1572868
  24.0 10.4 %copy-start.1 = (f32[128,8,128]{2,1,0:T(8,128)S(1)}, f32[128,8,128]{2,1,0:T(8,128)}, u32[]{:S(2)}) copy-start(f32[128,8,128]{2,1,0:T(8,128)} %param.19) | copy-start | bytes 1572868
  24.0 25.2 %all-to-all-start.1 = ((bf16[32,14,8,128]{3,2,1,0:T(8,128)(2,1)}), bf16[32,14,8,128]{3,2,1,0:T(8,128)(2,1)S(1)}, u32[]{:S(2)}, u32[]{:S(2)}) async-start(bf16[32,14,8,128]{3,2,1,0:T(8,128)(2,1)} %bucket.1), calls=%async_computation.1 | async-start | bytes 1835008 | tf_op jit(solution)/shard_map/all_to_all | solution.py:539
  33.5 0.7 copy-start.10
  67.0 15.6 %all-to-all-start.3 = ((bf16[32,6,8,128]{3,2,1,0:T(8,128)(2,1)}), bf16[32,6,8,128]{3,2,1,0:T(8,128)(2,1)S(1)}, u32[]{:S(2)}, u32[]{:S(2)}) async-start(bf16[32,6,8,128]{3,2,1,0:T(8,128)(2,1)} %pack.1), calls=%async_computation.3 | async-start | bytes 786432 | tf_op jit(solution)/shard_map/all_to_all | solution.py:539
  72.5 10.1 %copy-start.4 = (f32[256,128]{1,0:T(8,128)S(1)}, f32[256,128]{1,0:T(8,128)}, u32[]{:S(2)}) copy-start(f32[256,128]{1,0:T(8,128)} %refs_5_.1) | copy-start | bytes 393220
  72.5 10.1 %copy-start.5 = (f32[256,128]{1,0:T(8,128)S(1)}, f32[256,128]{1,0:T(8,128)}, u32[]{:S(2)}) copy-start(f32[256,128]{1,0:T(8,128)} %refs_8_.1) | copy-start | bytes 393220
  72.5 10.1 %copy-start.7 = (f32[13,512]{1,0:T(8,128)S(1)}, f32[13,512]{1,0:T(8,128)}, u32[]{:S(2)}) copy-start(f32[13,512]{1,0:T(8,128)} %refs_3_.1) | copy-start | bytes 79876
  72.5 10.1 %copy-start.8 = (f32[13,512]{1,0:T(8,128)S(1)}, f32[13,512]{1,0:T(8,128)}, u32[]{:S(2)}) copy-start(f32[13,512]{1,0:T(8,128)} %refs_6_.1) | copy-start | bytes 79876
